TPU v7x, 512 devices: a whole 4x8x8 slice. The times are simulated.
512 devices in a mesh: gy: 64 (over x, z, core), gx: 8 (over y).
Axes of the slice: x: 4, y: 8, z: 8, core: 2. Of those that a mesh axis runs over, the one named last changes fastest.
Arguments:
- level_set: float32 [4096, 4096], P('gy', 'gx'), may hold values from -6 to 6
- velocity: float32 [2, 4096, 4096], P(None, 'gy', 'gx'), may hold values from -2 to 2
- particles: float32 [32768, 3, 128], P(('gy', 'gx')), may hold values from -0.5 to 0.5
- escaped: int32 [32768, 128], P(('gy', 'gx')), may hold values 0 or 1
- home_cell: int32 [32768], P(('gy', 'gx')), may hold values from 0 to 32767
- land_cell: int32 [32768], P(('gy', 'gx')), may hold values from 0 to 32767
- dest_rank: int32 [32768], P(('gy', 'gx')), may hold values from 0 to 63, as said below
- block_count: int32 [512], P(('gy', 'gx')), may hold values from 48 to 64, as said below
Outputs:
- new_level: float32 [4096, 4096], P('gy', 'gx')
- moved_blocks: float32 [131072, 4, 128], P(('gy', 'gx'))
Inputs may be any that keep to these rules, and one draw needn't show every extreme that they name: `block_count`: live blocks are the first ones of a device; in every draw some device holds 64 live blocks. `dest_rank`: among one device's live blocks at most 4 go to one band; in every draw one band receives exactly 4 live blocks from every device.
All inputs are finite; a program needn't handle non-finite values. No bound on the sum of `escaped` on one device may be relied on, other than what follows from the above.
Results may differ from a plain program's by a relative error of at most 0.0003.
Values sent between devices are 32-bit elements; how exact they have to be, the bound alone decides.
No kernel may reach another device: no remote copies, remote signals or barrier semaphores. Data moves between devices by JAX's collectives and lax.ppermute only.
A program may use at most 64 MiB of HBM per device.

v0:
```python
import jax
import jax.numpy as jnp
from jax import lax
from jax.sharding import PartitionSpec as P

CAP = 4


time_step = 0.3
epsilon_weno = 1e-06


def with_halo(cells, sides, width):
    for axis, dim in sides:
        count = lax.axis_size(axis)
        head = lax.slice_in_dim(cells, 0, width, axis=dim)
        tail = lax.slice_in_dim(cells, cells.shape[dim] - width, cells.shape[dim], axis=dim)
        cells = jnp.concatenate(
            [
                lax.ppermute(tail, axis, [(i, (i + 1) % count) for i in range(count)]),
                cells,
                lax.ppermute(head, axis, [((i + 1) % count, i) for i in range(count)]),
            ],
            axis=dim,
        )
    return cells


def shifted_2(block, axis, distance):
    devices = range(lax.axis_size(axis))
    route = [((i - distance) % len(devices), i) for i in devices]
    return lax.ppermute(block, axis, route)


def blended(a, b, c, d, e):
    smooth_one = 13.0 / 12.0 * (a - 2.0 * b + c) ** 2 + 0.25 * (a - 4.0 * b + 3.0 * c) ** 2
    smooth_two = 13.0 / 12.0 * (b - 2.0 * c + d) ** 2 + 0.25 * (b - d) ** 2
    smooth_three = 13.0 / 12.0 * (c - 2.0 * d + e) ** 2 + 0.25 * (3.0 * c - 4.0 * d + e) ** 2
    weight_one = 0.1 / (smooth_one + epsilon_weno) ** 2
    weight_two = 0.6 / (smooth_two + epsilon_weno) ** 2
    weight_three = 0.3 / (smooth_three + epsilon_weno) ** 2
    weight_sum = weight_one + weight_two + weight_three
    candidate = (
        weight_one * (a / 3.0 - 7.0 * b / 6.0 + 11.0 * c / 6.0)
        + weight_two * (-b / 6.0 + 5.0 * c / 6.0 + d / 3.0)
        + weight_three * (c / 3.0 + 5.0 * d / 6.0 - e / 6.0)
    )
    return candidate / weight_sum


def upwinded(shifted, advecting):
    differences = [shifted(k + 1) - shifted(k) for k in range(-3, 3)]
    left_sided = blended(
        differences[0], differences[1], differences[2], differences[3], differences[4]
    )
    right_sided = blended(
        differences[5], differences[4], differences[3], differences[2], differences[1]
    )
    return advecting * jnp.where(advecting > 0, left_sided, right_sided)


def tendency(padded, along_x, along_y):
    height = along_x.shape[0]
    across = along_x.shape[1]

    def columns(k):
        return padded[3 : 3 + height, 3 + k : 3 + k + across]

    def rows_at(k):
        return padded[3 + k : 3 + k + height, 3 : 3 + across]

    return -(upwinded(columns, along_x) + upwinded(rows_at, along_y))


def advect(offset_x, offset_y, corners):
    fraction_y = offset_y + 0.5
    fraction_x = offset_x + 0.5

    def mixture(component):
        c = corners[:, component]
        return (
            (1.0 - fraction_y) * (1.0 - fraction_x) * c[:, 0:1]
            + fraction_y * (1.0 - fraction_x) * c[:, 1:2]
            + (1.0 - fraction_y) * fraction_x * c[:, 2:3]
            + fraction_y * fraction_x * c[:, 3:4]
        )

    return (offset_x + time_step * mixture(0), offset_y + time_step * mixture(1))


def shards(level_set, velocity, particles, escaped, home_cell, land_cell, dest_rank, block_count):
    height, across = level_set.shape
    band_count = lax.axis_size("gy")
    slot_count = band_count * CAP
    block_total = particles.shape[0]
    per_block = particles.shape[2]
    stacked = jnp.concatenate([level_set[None], velocity], axis=0)
    extended = with_halo(stacked, (("gy", 1), ("gx", 2)), 9)
    surface = extended[0]
    flow_field = extended[1:]
    section_one = surface[3:-3, 3:-3] + time_step * tendency(
        surface, flow_field[0, 3:-3, 3:-3], flow_field[1, 3:-3, 3:-3]
    )
    section_two = 0.75 * surface[6:-6, 6:-6] + 0.25 * (
        section_one[3:-3, 3:-3]
        + time_step * tendency(section_one, flow_field[0, 6:-6, 6:-6], flow_field[1, 6:-6, 6:-6])
    )
    section_three = surface[9:-9, 9:-9] / 3.0 + 2.0 / 3.0 * (
        section_two[3:-3, 3:-3] + time_step * tendency(section_two, velocity[0], velocity[1])
    )
    corner_flow = flow_field[:, 9 : height + 10, 9 : across + 10]
    position = jnp.arange(block_total, dtype=jnp.int32)
    is_live = position < block_count[0]
    earlier_same = (
        (dest_rank[None, :] == dest_rank[:, None])
        & is_live[None, :]
        & (position[None, :] < position[:, None])
    )
    slot_rank = jnp.sum(earlier_same.astype(jnp.int32), axis=1)
    target = jnp.where(is_live, dest_rank * CAP + slot_rank, -1)
    chooser = jnp.arange(slot_count, dtype=jnp.int32)[:, None] == target[None, :]
    selector = chooser.astype(jnp.float32)
    cell_out = jnp.sum(jnp.where(chooser, land_cell[None, :], 0), axis=1).reshape(band_count, CAP)
    home_flat = home_cell // across * (across + 1) + home_cell % across
    flattened = corner_flow.reshape(2, -1)
    corners = jnp.stack(
        [
            flattened[:, home_flat],
            flattened[:, home_flat + across + 1],
            flattened[:, home_flat + 1],
            flattened[:, home_flat + across + 2],
        ],
        axis=-1,
    )
    corners = jnp.transpose(corners, (1, 0, 2))
    radius = particles[:, 2, :]
    weight = escaped.astype(jnp.float32) * radius
    new_x, new_y = advect(particles[:, 0, :], particles[:, 1, :], corners)
    payload = jnp.stack([new_x, new_y, radius, weight], axis=1).reshape(block_total, 4 * per_block)
    packed = jnp.dot(selector, payload, precision=lax.Precision.HIGHEST).reshape(
        band_count, CAP, 4 * per_block
    )
    arrived, cells_in = (
        lax.all_to_all(packed, "gy", split_axis=0, concat_axis=0, tiled=True),
        lax.all_to_all(cell_out, "gy", split_axis=0, concat_axis=0, tiled=True),
    )
    moved_rows = arrived.reshape(slot_count, 4, per_block)
    cells_in = cells_in.reshape(slot_count)
    fraction_y = moved_rows[:, 1, :] + 0.5
    fraction_x = moved_rows[:, 0, :] + 0.5
    carried = moved_rows[:, 3, :]
    low_low = jnp.sum(carried * (1.0 - fraction_y) * (1.0 - fraction_x), axis=1)
    high_low = jnp.sum(carried * fraction_y * (1.0 - fraction_x), axis=1)
    low_high = jnp.sum(carried * (1.0 - fraction_y) * fraction_x, axis=1)
    high_high = jnp.sum(carried * fraction_y * fraction_x, axis=1)
    anchor = cells_in // across * (across + 1) + cells_in % across
    deposit = jnp.zeros(((height + 1) * (across + 1),), jnp.float32)
    deposit = deposit.at[anchor].add(low_low)
    deposit = deposit.at[anchor + across + 1].add(high_low)
    deposit = deposit.at[anchor + 1].add(low_high)
    deposit = deposit.at[anchor + across + 2].add(high_high)
    deposit = deposit.reshape(height + 1, across + 1)
    incoming = shifted_2(deposit[height], "gy", 1)
    deposit = deposit.at[0].add(incoming)
    sideways = shifted_2(deposit[:height, across], "gx", 1)
    correction = deposit[:height, :across].at[:, 0].add(sideways)
    return (section_three + correction, moved_rows)


def solution(mesh):
    in_specs = (
        P("gy", "gx"),
        P(None, "gy", "gx"),
        P(("gy", "gx"), None, None),
        P(("gy", "gx"), None),
        P(("gy", "gx")),
        P(("gy", "gx")),
        P(("gy", "gx")),
        P(("gy", "gx")),
    )
    out_specs = (P("gy", "gx"), P(("gy", "gx"), None, None))
    return jax.shard_map(shards, mesh=mesh, in_specs=in_specs, out_specs=out_specs, check_vma=False)
```

profile of v0, /device:TPU:24, one launch (start us, length us, event | category | flops | bytes accessed | tf_op | source)
XLA Modules:
  0.0 128.7 jit_solution(5592404875393762551)
XLA Ops:
  1.6 1.9 %collective-permute-start = (f32[3,9,512]{2,1,0:T(8,128)S(1)}, f32[3,9,512]{2,1,0:T(8,128)S(1)}, u32[]{:S(2)}, u32[]{:S(2)}) collective-permute-start(f32[3,9,512]{2,1,0:T(8,128)S(1)} %get-tuple-element.41), channel_id=1, source_target_pairs={{0,8},{8,16},{16,24},{24,32},{32,40},{40,48},{48,56},{56,64},{64,7... | collective-permute-start | bytes 165896 | tf_op jit(solution)/shard_map/ppermute | solution.py:20
  3.6 12.6 %collective-permute-start.1 = (f32[3,9,512]{2,1,0:T(8,128)S(1)}, f32[3,9,512]{2,1,0:T(8,128)S(1)}, u32[]{:S(2)}, u32[]{:S(2)}) collective-permute-start(f32[3,9,512]{2,1,0:T(8,128)S(1)} %get-tuple-element.42), channel_id=1, source_target_pairs={{8,0},{16,8},{24,16},{32,24},{40,32},{48,40},{56,48},{64,56},{72,6... | collective-permute-start | bytes 165896 | tf_op jit(solution)/shard_map/ppermute | solution.py:22
  19.9 6.0 %all-to-all-start = ((s32[64,1,4]{2,1,0:T(1,128)}), s32[64,1,4]{2,1,0:T(1,128)S(1)}, u32[]{:S(2)}, u32[]{:S(2)}) async-start(s32[64,1,4]{2,1,0:T(1,128)} %bitcast.9), calls=%async_computation | async-start | bytes 65536 | tf_op jit(solution)/shard_map/all_to_all | solution.py:145
  28.4 2.4 %collective-permute-start.3 = (f32[3,82,9]{2,1,0:T(8,128)S(1)}, f32[3,82,9]{2,1,0:T(8,128)S(1)}, u32[]{:S(2)}, u32[]{:S(2)}) collective-permute-start(f32[3,82,9]{2,1,0:T(8,128)S(1)} %get-tuple-element.37), channel_id=1, source_target_pairs={{1,0},{2,1},{3,2},{4,3},{5,4},{6,5},{7,6},{0,7},{9,8},{10,9},{11,1... | collective-permute-start | bytes 26576 | tf_op jit(solution)/shard_map/ppermute | solution.py:22
  30.8 6.3 %collective-permute-done.3 = f32[3,82,9]{2,1,0:T(8,128)S(1)} collective-permute-done((f32[3,82,9]{2,1,0:T(8,128)S(1)}, f32[3,82,9]{2,1,0:T(8,128)S(1)}, u32[]{:S(2)}, u32[]{:S(2)}) %collective-permute-start.3) | collective-permute-done | bytes 8888 | tf_op jit(solution)/shard_map/ppermute | solution.py:22
  38.5 8.4 %copy.68 = f32[2,33345]{0,1:T(8,128)} copy(f32[2,33345]{1,0:T(2,128)S(1)} %reshape.353) | data formatting | bytes 533520 | tf_op jit(solution)/shard_map/reshape | solution.py:125
  46.9 6.5 %gather_fusion.2 = f32[64,2]{1,0:T(8,128)S(1)} fusion(f32[2,33345]{0,1:T(8,128)} %copy.68, s32[1024]{0:T(1024)S(1)} %get-tuple-element.63), kind=kCustom, calls=%fused_computation.2 | custom fusion | bytes 1280 | tf_op jit(solution)/shard_map/gather | solution.py:130
  53.5 6.5 %gather_fusion.3 = f32[64,2]{1,0:T(8,128)S(1)} fusion(f32[2,33345]{0,1:T(8,128)} %copy.68, s32[1024]{0:T(1024)S(1)} %get-tuple-element.62), kind=kCustom, calls=%fused_computation.3 | custom fusion | bytes 1280 | tf_op jit(solution)/shard_map/gather | solution.py:131
  60.0 6.5 %gather_fusion.1 = f32[64,2]{1,0:T(8,128)S(1)} fusion(f32[2,33345]{0,1:T(8,128)} %copy.68, s32[1024]{0:T(1024)S(1)} %pad_clamp_fusion.2), kind=kCustom, calls=%fused_computation.1 | custom fusion | bytes 1280 | tf_op jit(solution)/shard_map/gather | solution.py:129
  66.5 6.5 %gather_fusion = f32[64,2]{1,0:T(8,128)S(1)} fusion(f32[2,33345]{0,1:T(8,128)} %copy.68, s32[1024]{0:T(1024)S(1)} %pad_clamp_fusion.3), kind=kCustom, calls=%fused_computation | custom fusion | bytes 1280 | tf_op jit(solution)/shard_map/gather | solution.py:128
  75.0 10.4 %all-to-all-start.1 = ((f32[64,4,512]{2,1,0:T(4,128)}), f32[64,4,512]{2,1,0:T(4,128)S(1)}, u32[]{:S(2)}, u32[]{:S(2)}) async-start(f32[64,4,512]{2,1,0:T(4,128)} %copy.77), calls=%async_computation.1 | async-start | bytes 1048576 | tf_op jit(solution)/shard_map/all_to_all | solution.py:144
  87.5 3.5 %collective-permute-start.2 = (f32[3,82,9]{2,1,0:T(8,128)S(1)}, f32[3,82,9]{2,1,0:T(8,128)S(1)}, u32[]{:S(2)}, u32[]{:S(2)}) collective-permute-start(f32[3,82,9]{2,1,0:T(8,128)S(1)} %get-tuple-element.36), channel_id=1, source_target_pairs={{0,1},{1,2},{2,3},{3,4},{4,5},{5,6},{6,7},{7,0},{8,9},{9,10},{10,1... | collective-permute-start | bytes 26576 | tf_op jit(solution)/shard_map/ppermute | solution.py:20
  91.0 3.9 %collective-permute-done.2 = f32[3,82,9]{2,1,0:T(8,128)S(1)} collective-permute-done((f32[3,82,9]{2,1,0:T(8,128)S(1)}, f32[3,82,9]{2,1,0:T(8,128)S(1)}, u32[]{:S(2)}, u32[]{:S(2)}) %collective-permute-start.2) | collective-permute-done | bytes 8888 | tf_op jit(solution)/shard_map/ppermute | solution.py:20
  95.3 7.2 %all-to-all-done.1 = f32[64,4,512]{2,1,0:T(4,128)S(1)} async-done(((f32[64,4,512]{2,1,0:T(4,128)}), f32[64,4,512]{2,1,0:T(4,128)S(1)}, u32[]{:S(2)}, u32[]{:S(2)}) %all-to-all-start.1) | async-done | bytes 524320 | tf_op jit(solution)/shard_map/all_to_all | solution.py:144
  103.4 2.1 %scatter_custom_fusion = f32[33345]{0:T(1024)S(1)} fusion(s32[256]{0:T(256)S(1)} %bitcast.127, f32[256]{0:T(256)S(1)} %get-tuple-element.31, f32[]{:T(128)} %constant.292.clone.1), kind=kCustom, calls=%fused_computation.80 | custom fusion | flops 256 | bytes 133384 | tf_op jit(solution)/shard_map/scatter-add | solution.py:158
  105.4 2.1 %scatter_fusion = f32[33345]{0:T(1024)S(1)} fusion(f32[33345]{0:T(1024)S(1)} %scatter_custom_fusion, s32[256]{0:T(256)S(1)} %bitcast.122, f32[256]{0:T(256)S(1)} %get-tuple-element.29), kind=kCustom, calls=%fused_computation.5 | custom fusion | flops 256 | bytes 4096 | tf_op jit(solution)/shard_map/scatter-add | solution.py:159
  107.5 2.1 %scatter_fusion.1 = f32[33345]{0:T(1024)S(1)} fusion(f32[33345]{0:T(1024)S(1)} %scatter_fusion, s32[256]{0:T(256)S(1)} %bitcast.121, f32[256]{0:T(256)S(1)} %get-tuple-element.30), kind=kCustom, calls=%fused_computation.6 | custom fusion | flops 256 | bytes 4096 | tf_op jit(solution)/shard_map/scatter-add | solution.py:160
  109.6 2.1 %scatter_fusion.2 = f32[33345]{0:T(1024)S(1)} fusion(f32[33345]{0:T(1024)S(1)} %scatter_fusion.1, s32[256]{0:T(256)S(1)} %bitcast.120, f32[256]{0:T(256)S(1)} %get-tuple-element.28), kind=kCustom, calls=%fused_computation.7 | custom fusion | flops 256 | bytes 4096 | tf_op jit(solution)/shard_map/scatter-add | solution.py:161
  111.8 2.3 %collective-permute-start.4 = (f32[513]{0:T(1024)S(1)}, f32[513]{0:T(1024)S(1)}, u32[]{:S(2)}, u32[]{:S(2)}) collective-permute-start(f32[513]{0:T(1024)S(1)} %slice.454), channel_id=1, source_target_pairs={{504,0},{0,8},{8,16},{16,24},{24,32},{32,40},{40,48},{48,56},{56,6... | collective-permute-start | bytes 6164 | tf_op jit(solution)/shard_map/ppermute | solution.py:32
  114.1 2.2 %multiply_add_fusion = f32[76,524]{1,0:T(8,128)S(1)} fusion(f32[82,530]{1,0:T(8,128)S(1)} %slice_bitcast_fusion, f32[3,82,530]{2,1,0:T(8,128)S(1)} %pad_maximum_fusion), kind=kLoop, calls=%fused_computation.20 | loop fusion | flops 10752480 | bytes 2548736 | tf_op jit(solution)/shard_map/add | solution.py:101
  116.5 3.5 %collective-permute-done.4 = f32[513]{0:T(1024)S(1)} collective-permute-done((f32[513]{0:T(1024)S(1)}, f32[513]{0:T(1024)S(1)}, u32[]{:S(2)}, u32[]{:S(2)}) %collective-permute-start.4) | collective-permute-done | bytes 2084 | tf_op jit(solution)/shard_map/ppermute | solution.py:32
  120.2 3.4 %collective-permute-start.5 = (f32[64]{0:T(128)S(1)}, f32[64]{0:T(128)S(1)}, u32[]{:S(2)}, u32[]{:S(2)}) collective-permute-start(f32[64]{0:T(128)S(1)} %slice_reduce_fusion), channel_id=1, source_target_pairs={{7,0},{0,1},{1,2},{2,3},{3,4},{4,5},{5,6},{6,7},{15,8},{8,9},{9,10... | collective-permute-start | bytes 776 | tf_op jit(solution)/shard_map/ppermute | solution.py:32
  123.6 2.0 %fusion.4 = f32[70,518]{1,0:T(8,128)S(1)} fusion(f32[82,530]{1,0:T(8,128)S(1)} %slice_bitcast_fusion, f32[76,524]{1,0:T(8,128)S(1)} %multiply_add_fusion, f32[3,82,530]{2,1,0:T(8,128)S(1)} %pad_maximum_fusion), kind=kLoop, calls=%fused_computation.34 | loop fusion | flops 9898980 | bytes 2465680 | tf_op jit(solution)/shard_map/add | solution.py:104
  126.6 2.1 %fusion.10 = f32[64,512]{1,0:T(8,128)} fusion(f32[64,512]{1,0:T(8,128)S(1)} %scatter-add.43, f32[82,530]{1,0:T(8,128)S(1)} %slice_bitcast_fusion, f32[70,518]{1,0:T(8,128)S(1)} %fusion.4, f32[2,64,512]{2,1,0:T(8,128)S(1)} %copy-done), kind=kLoop, calls=%fused_computation.52 | loop fusion | flops 8978432 | bytes 2359296 | tf_op jit(solution)/shard_map/add | solution.py:167
  (64 shorter events, 14.8 us)
Async XLA Ops:
  0.6 94.3 %copy-start.1 = (f32[64,512]{1,0:T(8,128)S(1)}, f32[64,512]{1,0:T(8,128)}, u32[]{:S(2)}) copy-start(f32[64,512]{1,0:T(8,128)} %param.12) | copy-start | bytes 393220
  0.6 94.3 %copy-start = (f32[2,64,512]{2,1,0:T(8,128)S(1)}, f32[2,64,512]{2,1,0:T(8,128)}, u32[]{:S(2)}) copy-start(f32[2,64,512]{2,1,0:T(8,128)} %param.13) | copy-start | bytes 786436
  0.7 72.5 %copy-start.3 = (f32[64,3,128]{2,0,1:T(8,128)S(1)}, f32[64,3,128]{2,0,1:T(8,128)}, u32[]{:S(2)}) copy-start(f32[64,3,128]{2,0,1:T(8,128)} %param.14) | copy-start | bytes 294916
  1.6 25.8 %collective-permute-start = (f32[3,9,512]{2,1,0:T(8,128)S(1)}, f32[3,9,512]{2,1,0:T(8,128)S(1)}, u32[]{:S(2)}, u32[]{:S(2)}) collective-permute-start(f32[3,9,512]{2,1,0:T(8,128)S(1)} %get-tuple-element.41), channel_id=1, source_target_pairs={{0,8},{8,16},{16,24},{24,32},{32,40},{40,48},{48,56},{56,64},{64,7... | collective-permute-start | bytes 165896 | tf_op jit(solution)/shard_map/ppermute | solution.py:20
  3.6 23.9 %collective-permute-start.1 = (f32[3,9,512]{2,1,0:T(8,128)S(1)}, f32[3,9,512]{2,1,0:T(8,128)S(1)}, u32[]{:S(2)}, u32[]{:S(2)}) collective-permute-start(f32[3,9,512]{2,1,0:T(8,128)S(1)} %get-tuple-element.42), channel_id=1, source_target_pairs={{8,0},{16,8},{24,16},{32,24},{40,32},{48,40},{56,48},{64,56},{72,6... | collective-permute-start | bytes 165896 | tf_op jit(solution)/shard_map/ppermute | solution.py:22
  19.9 55.1 %all-to-all-start = ((s32[64,1,4]{2,1,0:T(1,128)}), s32[64,1,4]{2,1,0:T(1,128)S(1)}, u32[]{:S(2)}, u32[]{:S(2)}) async-start(s32[64,1,4]{2,1,0:T(1,128)} %bitcast.9), calls=%async_computation | async-start | bytes 65536 | tf_op jit(solution)/shard_map/all_to_all | solution.py:145
  28.4 8.6 %collective-permute-start.3 = (f32[3,82,9]{2,1,0:T(8,128)S(1)}, f32[3,82,9]{2,1,0:T(8,128)S(1)}, u32[]{:S(2)}, u32[]{:S(2)}) collective-permute-start(f32[3,82,9]{2,1,0:T(8,128)S(1)} %get-tuple-element.37), channel_id=1, source_target_pairs={{1,0},{2,1},{3,2},{4,3},{5,4},{6,5},{7,6},{0,7},{9,8},{10,9},{11,1... | collective-permute-start | bytes 26576 | tf_op jit(solution)/shard_map/ppermute | solution.py:22
  75.0 27.4 %all-to-all-start.1 = ((f32[64,4,512]{2,1,0:T(4,128)}), f32[64,4,512]{2,1,0:T(4,128)S(1)}, u32[]{:S(2)}, u32[]{:S(2)}) async-start(f32[64,4,512]{2,1,0:T(4,128)} %copy.77), calls=%async_computation.1 | async-start | bytes 1048576 | tf_op jit(solution)/shard_map/all_to_all | solution.py:144
  87.5 7.4 %collective-permute-start.2 = (f32[3,82,9]{2,1,0:T(8,128)S(1)}, f32[3,82,9]{2,1,0:T(8,128)S(1)}, u32[]{:S(2)}, u32[]{:S(2)}) collective-permute-start(f32[3,82,9]{2,1,0:T(8,128)S(1)} %get-tuple-element.36), channel_id=1, source_target_pairs={{0,1},{1,2},{2,3},{3,4},{4,5},{5,6},{6,7},{7,0},{8,9},{9,10},{10,1... | collective-permute-start | bytes 26576 | tf_op jit(solution)/shard_map/ppermute | solution.py:20
  102.8 25.9 %copy-start.2 = (f32[256,4,128]{2,1,0:T(4,128)}, f32[256,4,128]{2,1,0:T(4,128)S(1)}, u32[]{:S(2)}) copy-start(f32[256,4,128]{2,1,0:T(4,128)S(1)} %reshape.355) | copy-start | bytes 1572868
  111.8 8.2 %collective-permute-start.4 = (f32[513]{0:T(1024)S(1)}, f32[513]{0:T(1024)S(1)}, u32[]{:S(2)}, u32[]{:S(2)}) collective-permute-start(f32[513]{0:T(1024)S(1)} %slice.454), channel_id=1, source_target_pairs={{504,0},{0,8},{8,16},{16,24},{24,32},{32,40},{40,48},{48,56},{56,6... | collective-permute-start | bytes 6164 | tf_op jit(solution)/shard_map/ppermute | solution.py:32
  120.2 5.5 %collective-permute-start.5 = (f32[64]{0:T(128)S(1)}, f32[64]{0:T(128)S(1)}, u32[]{:S(2)}, u32[]{:S(2)}) collective-permute-start(f32[64]{0:T(128)S(1)} %slice_reduce_fusion), channel_id=1, source_target_pairs={{7,0},{0,1},{1,2},{2,3},{3,4},{4,5},{5,6},{6,7},{15,8},{8,9},{9,10... | collective-permute-start | bytes 776 | tf_op jit(solution)/shard_map/ppermute | solution.py:32
where the time goes:
time: 130 us; the launch traced here: 129 us
  starting transfers between devices  42.5 us (33%)
  local copies, waits for them, and re-layouts  38.7 us (30%)
  other arithmetic  24.6 us (19%)
  waiting for transfers between devices  20.9 us (16%)
  between operations  1.67 us (1%)
    ppermute x2, starting transfers between devices, with_halo(): lax.ppermute(head, axis, [((i + 1) % count, i) for i in range(count)])  14.9 us
    all_to_all x1, starting transfers between devices, shards(): lax.all_to_all(packed, 'gy', split_axis=0, concat_axis=0, tiled=True)  10.4 us
    reshape x2, local copies, waits for them, and re-layouts, shards(): flattened = corner_flow.reshape(2, -1)  8.87 us
    all_to_all x1, waiting for transfers between devices, shards(): lax.all_to_all(packed, 'gy', split_axis=0, concat_axis=0, tiled=True)  7.17 us
    gather x2, local copies, waits for them, and re-layouts, shards(): flattened[:, home_flat + across + 1]  6.53 us
    gather x2, local copies, waits for them, and re-layouts, shards(): flattened[:, home_flat]  6.53 us
    gather x2, local copies, waits for them, and re-layouts, shards(): flattened[:, home_flat + across + 2]  6.53 us
    gather x2, local copies, waits for them, and re-layouts, shards(): flattened[:, home_flat + 1]  6.52 us
  transfers between devices with their start and end apart: 8, of which 4 were waited for; matrix products, arithmetic and copies ran while one was open for 38% of the time, Pallas kernels for 0%

commit v1 on v0

v1 whole, which is shorter than its diff:
```python
import functools
import jax
import jax.numpy as jnp
from jax import lax
from jax.experimental import pallas as pl
from jax.experimental.pallas import tpu as pltpu
from jax.sharding import PartitionSpec as P

CAP = 4
DT = 0.3
INTERPRET = False
F32 = jnp.float32
BF16 = jnp.bfloat16


def iota(shape, dim):
    return lax.broadcasted_iota(jnp.int32, shape, dim).astype(F32)


def split3(x):
    hi = x.astype(BF16)
    rest = x - hi.astype(F32)
    mid = rest.astype(BF16)
    lo = (rest - mid.astype(F32)).astype(BF16)
    return hi, mid, lo


def mm(a, b):
    return lax.dot_general(a, b, (((1,), (0,)), ((), ())), preferred_element_type=F32)


def exact_pick(one_hot, x):
    hi, mid, lo = split3(x)
    return (mm(one_hot, hi) + mm(one_hot, mid)) + mm(one_hot, lo)


def eye(n):
    return iota((n, n), 0) == iota((n, n), 1)


def to_column(row, n):
    return jnp.sum(jnp.where(eye(n), jnp.broadcast_to(row, (n, n)), 0.0), axis=1, keepdims=True)


def to_row(col, n):
    return jnp.sum(jnp.where(eye(n), jnp.broadcast_to(col, (n, n)), 0.0), axis=0, keepdims=True)


def one_hot(mask):
    return jnp.where(mask, 1.0, 0.0).astype(BF16)


def floor_div(x, k):
    return jnp.floor((x + 0.5) * (1.0 / k))


def call(body, outs, *args, scratch=()):
    vm = pl.BlockSpec(memory_space=pltpu.VMEM)
    return pl.pallas_call(
        body,
        out_shape=tuple(outs),
        in_specs=[vm] * len(args),
        out_specs=tuple(vm for _ in outs),
        scratch_shapes=list(scratch),
        interpret=INTERPRET,
    )(*args)


def prepare_body(u_ref, v_ref, rad_ref, esc_ref, ints_ref, count_ref, meta_ref, w_ref, sel_ref):
    n = rad_ref.shape[0]
    height, across = u_ref.shape
    ints = ints_ref[...].astype(F32)
    home = to_column(ints[0:1], n)
    land = to_column(ints[1:2], n)
    dest_row = ints[2:3]
    dest = to_column(dest_row, n)
    count = count_ref[...].astype(F32)
    row = floor_div(home, across)
    col = home - row * across
    land_row = floor_div(land, across)
    land_col = land - land_row * across
    other = iota((n, n), 0)
    mine = iota((n, n), 1)
    same = (dest == dest_row) & (other < mine) & (other < count)
    rank_row = jnp.sum(jnp.where(same, 1.0, 0.0), axis=0, keepdims=True)
    live_row = iota((1, n), 1) < count
    slot_row = jnp.where(live_row, dest_row * CAP + rank_row, -1.0)
    slot = to_column(slot_row, n)
    lane = iota((n, height), 1)
    pick = jnp.concatenate([one_hot(lane == row), one_hot(lane == row + 1.0)], axis=0)
    lanes = iota((n, across), 1)
    at0 = lanes == col
    at1 = lanes == col + 1.0
    parts = []
    for ref in (u_ref, v_ref):
        both = exact_pick(pick, ref[...])
        low = both[0:n]
        high = both[n:]
        for where_at in (at0, at1):
            for rows in (low, high):
                parts.append(jnp.sum(jnp.where(where_at, rows, 0.0), axis=1, keepdims=True))
    columns = parts + [row, col, land_row, land_col, slot]
    lane = iota((n, 128), 1)
    meta = jnp.zeros((n, 128), F32)
    for i, value in enumerate(columns):
        meta = jnp.where(lane == float(i), value, meta)
    meta_ref[...] = meta
    w_ref[...] = esc_ref[...].astype(F32) * rad_ref[...]
    total = sel_ref.shape[0]
    step = 4 * CAP + 1
    r = iota((total, 1), 0)
    d = floor_div(r, step)
    q = r - d * step
    code = jnp.where(q < 4.0 * CAP, d * (4.0 * CAP) + q, -1000.0)
    slots = jnp.concatenate([slot_row * 4.0 + float(j) for j in range(4)], axis=1)
    slots = jnp.where(jnp.concatenate([slot_row] * 4, axis=1) < 0.0, -1.0, slots)
    sel_ref[...] = one_hot(code == slots)


def edges_body(f_ref, u_ref, v_ref, below_ref, meta_ref, x_ref, y_ref, w_ref, left_ref, right_ref, meta2_ref):
    n = x_ref.shape[0]
    height, across = f_ref.shape
    meta = meta_ref[...]
    lane = iota((n, 128), 1)
    row = meta[:, 8:9]
    col = meta[:, 9:10]
    last = row == float(height - 1)
    lanes = iota((n, across), 1)
    at0 = (lanes == col) & last
    at1 = (lanes == col + 1.0) & last
    for base, r in ((0, 9), (4, 15)):
        line = jnp.broadcast_to(below_ref[r : r + 1, :], (n, across))
        c10 = jnp.sum(jnp.where(at0, line, 0.0), axis=1, keepdims=True)
        c11 = jnp.sum(jnp.where(at1, line, 0.0), axis=1, keepdims=True)
        meta = meta + jnp.where(lane == float(base + 1), c10, 0.0) + jnp.where(lane == float(base + 3), c11, 0.0)
    meta2_ref[...] = meta
    far = across - 128

    def pack_left(f, u, v):
        lane = iota(f.shape, 1)
        return jnp.where(lane < 16.0, f, jnp.where(lane < 32.0, pltpu.roll(u, 16, 1), pltpu.roll(v, 32, 1)))

    def pack_right(f, u, v, m):
        lane = iota(f.shape, 1)
        out = jnp.where(
            lane >= 112.0, f, jnp.where(lane >= 96.0, pltpu.roll(u, 112, 1), pltpu.roll(v, 96, 1))
        )
        return jnp.where(lane < 16.0, m, out)

    left_ref[0:height] = pack_left(f_ref[:, 0:128], u_ref[:, 0:128], v_ref[:, 0:128])
    right_ref[0:height] = pack_right(f_ref[:, far:], u_ref[:, far:], v_ref[:, far:], meta)
    zero = jnp.zeros((8, 128), F32)
    left_ref[height : height + 8] = pack_left(below_ref[0:8, 0:128], below_ref[9:17, 0:128], below_ref[15:23, 0:128])
    left_ref[height + 8 : height + 16] = pack_left(below_ref[8:16, 0:128], zero, zero)
    right_ref[height : height + 8] = pack_right(below_ref[0:8, far:], below_ref[9:17, far:], below_ref[15:23, far:], zero)
    right_ref[height + 8 : height + 16] = pack_right(below_ref[8:16, far:], zero, zero, zero)
    top = height + 16
    right_ref[top : top + n] = x_ref[...]
    right_ref[top + n : top + 2 * n] = y_ref[...]
    right_ref[top + 2 * n : top + 3 * n] = w_ref[...]


def halo_tiles(from_right, from_left):
    lane = iota(from_right.shape, 1)
    right_side = lane < 64.0
    f = jnp.where(right_side, from_right, from_left)
    u = jnp.where(right_side, pltpu.roll(from_right, 112, 1), pltpu.roll(from_left, 16, 1))
    v = jnp.where(right_side, pltpu.roll(from_right, 96, 1), pltpu.roll(from_left, 32, 1))
    return f, u, v


def moved_particles(meta, x, y, column, across):
    n = x.shape[0]
    row = meta[:, 8:9]
    last = meta[:, 9:10] == float(across - 1)
    lane = iota((n, column.shape[0]), 1)
    pick = jnp.concatenate([one_hot((lane == row) & last), one_hot((lane == row + 1.0) & last)], axis=0)
    both = exact_pick(pick, column)
    low = both[0:n]
    high = both[n:]
    u = [meta[:, 0:1], meta[:, 1:2], meta[:, 2:3] + low[:, 16:17], meta[:, 3:4] + high[:, 16:17]]
    v = [meta[:, 4:5], meta[:, 5:6], meta[:, 6:7] + low[:, 32:33], meta[:, 7:8] + high[:, 32:33]]
    fy = y + 0.5
    fx = x + 0.5
    w00 = (1.0 - fy) * (1.0 - fx)
    w10 = fy * (1.0 - fx)
    w01 = (1.0 - fy) * fx
    w11 = fy * fx
    new_x = x + DT * (w00 * u[0] + w10 * u[1] + w01 * u[2] + w11 * u[3])
    new_y = y + DT * (w00 * v[0] + w10 * v[1] + w01 * v[2] + w11 * v[3])
    return new_x, new_y


def lane_sum(x):
    return jnp.sum(x, axis=1, keepdims=True)


def pack_body(
    f_ref, u_ref, v_ref, x_ref, y_ref, rad_ref, w_ref, meta_ref, mine_ref, left_ref, right_ref, sel_ref, out_ref, tail_ref
):
    n = x_ref.shape[0]
    height, across = f_ref.shape
    bands = out_ref.shape[0] // (4 * CAP + 1)
    meta = meta_ref[...]
    top = height + 16
    w = w_ref[...]
    new_x, new_y = moved_particles(meta, x_ref[...], y_ref[...], right_ref[...], across)
    left_meta = left_ref[0:n]
    left_w = left_ref[top + 2 * n : top + 3 * n]
    left_x, left_y = moved_particles(
        left_meta, left_ref[top : top + n], left_ref[top + n : top + 2 * n], mine_ref[...], across
    )
    body = jnp.concatenate([new_x, new_y, rad_ref[...], w], axis=0)
    out_ref[...] = exact_pick(sel_ref[...], body)
    gy = new_y + 0.5
    gx = new_x + 0.5
    sums = [
        meta[:, 10:11],
        meta[:, 11:12],
        lane_sum(w * (1.0 - gy) * (1.0 - gx)),
        lane_sum(w * gy * (1.0 - gx)),
        lane_sum(w * (1.0 - gy) * gx),
        lane_sum(w * gy * gx),
    ]
    lane = iota((n, 128), 1)
    lane16 = lane - 16.0 * jnp.floor(lane * 0.0625)
    mine = jnp.zeros((n, 128), F32)
    for i, value in enumerate(sums):
        mine = jnp.where(lane16 == float(i), value, mine)
    gy = left_y + 0.5
    gx = left_x + 0.5
    over = left_meta[:, 11:12] == float(across - 1)
    sums = [
        left_meta[:, 10:11],
        jnp.where(over, lane_sum(left_w * (1.0 - gy) * gx), 0.0),
        jnp.where(over, lane_sum(left_w * gy * gx), 0.0),
    ]
    theirs = jnp.zeros((n, 128), F32)
    for i, value in enumerate(sums):
        theirs = jnp.where(lane16 == float(8 + i), value, theirs)
    values = jnp.concatenate([mine, theirs], axis=0)
    slot = jnp.concatenate([to_row(meta[:, 12:13], n), to_row(left_meta[:, 12:13], n)], axis=1)
    d4 = iota((bands, 2 * n), 0) * float(CAP)
    choose = jnp.concatenate([one_hot(d4 + float(k) == slot) for k in range(CAP)], axis=0)
    chosen = exact_pick(choose, values)
    lane = iota((bands, 128), 1)
    group = jnp.floor(lane * 0.0625)
    table = jnp.zeros((bands, 128), F32)
    for k in range(CAP):
        table = jnp.where(group == float(k), chosen[k * bands : (k + 1) * bands], table)
    table = table + pltpu.roll(pltpu.roll(table, 1, 0), 64, 1)
    step = 4 * CAP + 1
    out_ref[pl.ds(4 * CAP, bands, stride=step), :] = table
    f4, u4, v4 = halo_tiles(right_ref[height - 16 : height], left_ref[height - 16 : height])
    tail_ref[0:9, 0:across] = f_ref[height - 9 : height]
    tail_ref[9:15, 0:across] = u_ref[height - 6 : height]
    tail_ref[15:21, 0:across] = v_ref[height - 6 : height]
    tail_ref[0:9, across:] = f4[7:16]
    tail_ref[9:15, across:] = u4[10:16]
    tail_ref[15:21, across:] = v4[10:16]
    tail_ref[21:24, :] = jnp.zeros((3, across + 128), F32)


def side_term(speed, e0, e1, e2, e3, e4, d2, d3):
    ahead = speed > 0.0
    p = jnp.where(ahead, e0, e4)
    q = jnp.where(ahead, e1, e3)
    s = jnp.where(ahead, e3, e1)
    c = jnp.where(ahead, d2, d3)
    r = e2
    rr = r * r
    t1 = p * (4.0 * p - 11.0 * q) + (10.0 * (q * q) + 3e-6)
    t2 = q * (4.0 * q - 5.0 * r) + (4.0 * rr + 3e-6)
    t3 = s * (4.0 * s - 11.0 * r) + (10.0 * rr + 3e-6)
    a1 = t2 * t3
    a2 = t1 * t3
    a3 = t1 * t2
    w1 = a1 * a1
    w2 = 6.0 * (a2 * a2)
    w3 = 3.0 * (a3 * a3)
    top = w1 * (2.0 * p - 5.0 * q) - w2 * (q + 2.0 * r) + w3 * (s - 4.0 * r)
    return speed * c + jnp.abs(speed) * (top / (6.0 * (w1 + w2 + w3)))


def stencil_body(f_ref, u_ref, v_ref, below_ref, right_ref, left_ref, above_ref, out_ref, f0, us, vs, f1, f2):
    height, across = f_ref.shape
    width = across + 128
    tiles = width // 128
    off = 16
    span = height + 32
    f4, u4, v4 = halo_tiles(right_ref[...], left_ref[0 : height + 16])
    for buf, own, halo, start, count in ((f0, f_ref, f4, 0, 9), (us, u_ref, u4, 9, 6), (vs, v_ref, v4, 15, 6)):
        for j in range(tiles):
            sl = slice(128 * j, 128 * j + 128)
            top = span * j + off
            if j < tiles - 1:
                buf[top : top + height, :] = own[:, sl]
                buf[top + height : top + height + count, :] = below_ref[start : start + count, sl]
            else:
                buf[top : top + height + 16, :] = halo
            buf[top - count : top, :] = above_ref[start : start + count, sl]

    lane = lax.broadcasted_iota(jnp.int32, (8, 128), 1)

    def stage(src, dst_tiles, base, write):
        rolled = {}

        def shifted(tag, tiles_in, k):
            key = (tag, k)
            if key not in rolled:
                turned = [pltpu.roll(t, (-k) % 128, 1) for t in tiles_in]
                out = []
                for j in range(tiles):
                    if k > 0:
                        out.append(jnp.where(lane < 128 - k, turned[j], turned[(j + 1) % tiles]))
                    else:
                        out.append(jnp.where(lane >= -k, turned[j], turned[(j - 1) % tiles]))
                rolled[key] = out
            return rolled[key]

        f = [src[pl.ds(span * j + base, 8), :] for j in range(tiles)]
        nxt = shifted("f", f, 1)
        d3 = [nxt[j] - f[j] for j in range(tiles)]
        d2 = shifted("d", d3, -1)
        e2 = [d2[j] - d3[j] for j in range(tiles)]
        e0 = shifted("e", e2, -2)
        e1 = shifted("e", e2, -1)
        e3 = shifted("e", e2, 1)
        e4 = shifted("e", e2, 2)
        for j in range(dst_tiles):
            at = span * j + base
            u = us[pl.ds(at, 8), :]
            v = vs[pl.ds(at, 8), :]
            x_term = side_term(u, e0[j], e1[j], e2[j], e3[j], e4[j], d2[j], d3[j])
            rows = [f[j] if k == 0 else src[pl.ds(at + k, 8), :] for k in range(-3, 4)]
            d = [rows[k + 1] - rows[k] for k in range(6)]
            e = [d[k] - d[k + 1] for k in range(5)]
            y_term = side_term(v, e[0], e[1], e[2], e[3], e[4], d[2], d[3])
            write(j, f[j] - DT * (x_term + y_term))

    def first(i, carry):
        base = pl.multiple_of(i * 8 + 8, 8)

        def write(j, value):
            f1[pl.ds(span * j + base, 8), :] = value

        stage(f0, tiles, base, write)
        return carry

    def second(i, carry):
        base = pl.multiple_of(i * 8 + 8, 8)

        def write(j, value):
            at = pl.ds(span * j + base, 8)
            f2[at, :] = 0.75 * f0[at, :] + 0.25 * value

        stage(f1, tiles, base, write)
        return carry

    def third(i, carry):
        base = pl.multiple_of(i * 8 + 16, 8)
        place = pl.multiple_of(i * 8, 8)

        def write(j, value):
            kept = f0[pl.ds(span * j + base, 8), :]
            out_ref[pl.ds(place, 8), 128 * j : 128 * j + 128] = kept * (1.0 / 3.0) + (2.0 / 3.0) * value

        stage(f2, tiles - 1, base, write)
        return carry

    lax.fori_loop(0, height // 8 + 2, first, 0)
    lax.fori_loop(0, height // 8 + 2, second, 0)
    lax.fori_loop(0, height // 8, third, 0)


def deposit_body(recv_ref, base_ref, out_ref, moved_ref):
    height, across = base_ref.shape
    step = 4 * CAP + 1
    bands = recv_ref.shape[0] // step
    block = 4 * CAP
    for g in range(bands):
        moved_ref[block * g : block * g + block] = recv_ref[step * g : step * g + block]
    table = recv_ref[pl.ds(block, bands, stride=step), :]
    lanes = iota((bands, across), 1)
    lane = iota((bands, 128), 1)
    rows = iota((height, bands), 0)
    total = jnp.zeros((height, 2 * across), F32)
    side = jnp.zeros((height, 128), F32)
    first_row = jnp.zeros((bands, across), F32)
    corner = jnp.zeros((bands, 1), F32)

    def two(x):
        hi = x.astype(BF16)
        return hi, (x - hi.astype(F32)).astype(BF16)

    for k in range(CAP):
        o = 16 * k
        part = [table[:, o + i : o + i + 1] for i in range(11)]
        row, col, ll, hl, lh, hh = part[0:6]
        at0 = lanes == col
        at1 = lanes == col + 1.0
        spread = jnp.concatenate(
            [
                jnp.where(at0, ll, 0.0) + jnp.where(at1, lh, 0.0),
                jnp.where(at0, hl, 0.0) + jnp.where(at1, hh, 0.0),
            ],
            axis=1,
        )
        pick = one_hot(rows == to_row(row, bands))
        hi, lo = two(spread)
        total = total + (mm(pick, hi) + mm(pick, lo))
        pick = one_hot(rows == to_row(part[8], bands))
        values = jnp.where(lane == 0.0, part[9], jnp.where(lane == 1.0, part[10], 0.0))
        hi, lo = two(values)
        side = side + (mm(pick, hi) + mm(pick, lo))
        o = 64 + 16 * k
        part = [table[:, o + i : o + i + 1] for i in range(11)]
        row, col, ll, hl, lh, hh = part[0:6]
        edge = row == float(height - 1)
        first_row = (
            first_row
            + jnp.where((lanes == col) & edge, hl, 0.0)
            + jnp.where((lanes == col + 1.0) & edge, hh, 0.0)
        )
        corner = corner + jnp.where(part[8] == float(height - 1), part[10], 0.0)
    same = total[:, 0:across]
    down = pltpu.roll(total[:, across:], 1, 0)
    side_down = pltpu.roll(side, 1, 0)
    r = iota((height, across), 0)
    c = iota((height, across), 1)
    incoming = jnp.sum(first_row, axis=0, keepdims=True)
    incoming = incoming + jnp.where(iota((1, across), 1) == 0.0, jnp.sum(corner), 0.0)
    down = jnp.where(r == 0.0, incoming, down)
    column = side[:, 0:1] + jnp.where(iota((height, 1), 0) == 0.0, 0.0, side_down[:, 1:2])
    out_ref[...] = base_ref[...] + (same + down + jnp.where(c == 0.0, column, 0.0))


def ring(axis, distance):
    n = lax.axis_size(axis)
    return [(i, (i + distance) % n) for i in range(n)]


def shards(level_set, velocity, particles, escaped, home_cell, land_cell, dest_rank, block_count):
    height, across = level_set.shape
    n = particles.shape[0]
    bands = lax.axis_size("gy")
    step = 4 * CAP + 1
    sds = jax.ShapeDtypeStruct
    u, v = velocity[0], velocity[1]
    head = jnp.concatenate([level_set[0:9], u[0:6], v[0:6], jnp.zeros((3, across), F32)], axis=0)
    below = lax.ppermute(head, "gy", ring("gy", -1))
    x, y, radius = particles[:, 0, :], particles[:, 1, :], particles[:, 2, :]
    ints = jnp.stack([home_cell, land_cell, dest_rank], axis=0)
    meta, weight, select = call(
        prepare_body,
        (sds((n, 128), F32), sds((n, 128), F32), sds((bands * step, 4 * n), BF16)),
        u, v, radius, escaped, ints, block_count.reshape(1, 1),
    )
    to_left, to_right, meta = call(
        edges_body,
        (sds((height + 16, 128), F32), sds((height + 16 + 3 * n, 128), F32), sds((n, 128), F32)),
        level_set, u, v, below, meta, x, y, weight,
    )
    from_right = lax.ppermute(to_left, "gx", ring("gx", -1))
    from_left = lax.ppermute(to_right, "gx", ring("gx", 1))
    packed, tail = call(
        pack_body,
        (sds((bands * step, 128), F32), sds((24, across + 128), F32)),
        level_set, u, v, x, y, radius, weight, meta, to_left, from_left, from_right, select,
    )
    arrived = lax.all_to_all(
        packed.reshape(bands * step, 1, 128), "gy", split_axis=0, concat_axis=0, tiled=True
    ).reshape(bands * step, 128)
    above = lax.ppermute(tail, "gy", ring("gy", 1))
    wide = pltpu.VMEM(((across // 128 + 1) * (height + 32), 128), F32)
    (section,) = call(
        stencil_body,
        (sds((height, across), F32),),
        level_set, u, v, below, from_right, from_left, above,
        scratch=[wide] * 5,
    )
    level, moved = call(
        deposit_body,
        (sds((height, across), F32), sds((bands * CAP * 4, 128), F32)),
        arrived, section,
    )
    return level, moved.reshape(bands * CAP, 4, 128)


def solution(mesh):
    in_specs = (
        P("gy", "gx"),
        P(None, "gy", "gx"),
        P(("gy", "gx"), None, None),
        P(("gy", "gx"), None),
        P(("gy", "gx")),
        P(("gy", "gx")),
        P(("gy", "gx")),
        P(("gy", "gx")),
    )
    out_specs = (P("gy", "gx"), P(("gy", "gx"), None, None))
    return jax.shard_map(shards, mesh=mesh, in_specs=in_specs, out_specs=out_specs, check_vma=False)
```

time: 130 us -> 77.4 us (0.60)
  local copies, waits for them, and re-layouts: 38.7 us -> 6.54 us
  other arithmetic: 24.6 us -> 0.66 us
  Pallas kernels: 0 us -> 20.7 us
  starting transfers between devices: 42.5 us -> 26 us
    gather x8 -> x0, local copies, waits for them, and re-layouts: 26.1 us -> none  [the longest x2 6.53 us: shards(): flattened[:, home_flat + across + 1]]
    pallas_call x0 -> x5, Pallas kernels: none -> 20.7 us  [call(): pl.pallas_call(body, out_shape=tuple(outs), in_specs=[vm] * len(args), ou...]
    all_to_all x2 -> x1, starting transfers between devices: 16.4 us -> 4.77 us  [shards(): lax.all_to_all(packed.reshape(bands * step, 1, 128), 'gy', split_axis=0,...]
    reshape x6 -> x0, local copies, waits for them, and re-layouts: 9.53 us -> none  [the longest x2 8.87 us: shards(): flattened = corner_flow.reshape(2, -1)]
    scatter-add x4 -> x0, other arithmetic: 8.29 us -> none  [the longest x1 2.08 us: shards(): deposit = deposit.at[anchor].add(low_low)]
    ppermute x6 -> x4, waiting for transfers between devices: 13.7 us -> 21.5 us  [the longest x1 16.1 us: shards(): above = lax.ppermute(tail, 'gy', ring('gy', 1))]
    all_to_all x2 -> x1, waiting for transfers between devices: 7.17 us -> 0.01 us  [shards(): lax.all_to_all(packed.reshape(bands * step, 1, 128), 'gy', split_axis=0,...]
    add x5 -> x0, other arithmetic: 6.46 us -> none  [the longest x1 2.2 us: shards(): surface[3:-3, 3:-3]]
  transfers between devices with their start and end apart: 8 -> 5, of which waited for: 4 -> 2; matrix products, arithmetic and copies ran while one was open for 38% -> 4% of each run, Pallas kernels for 0% -> 16%
where the time goes in v1:
time: 77.4 us; the launch traced here: 76.8 us
  starting transfers between devices  26 us (34%)
  waiting for transfers between devices  21.5 us (28%)
  Pallas kernels  20.7 us (27%)
  local copies, waits for them, and re-layouts  6.54 us (8%)
  between operations  1.35 us (2%)
    pallas_call x5, Pallas kernels, call(): pl.pallas_call(body, out_shape=tuple(outs), in_specs=[vm] * len(args), ou...  20.7 us
    ppermute x1, waiting for transfers between devices, shards(): above = lax.ppermute(tail, 'gy', ring('gy', 1))  16.1 us
    ppermute x1, starting transfers between devices, shards(): below = lax.ppermute(head, 'gy', ring('gy', -1))  12.7 us
    ppermute x1, waiting for transfers between devices, shards(): from_right = lax.ppermute(to_left, 'gx', ring('gx', -1))  5.39 us
    all_to_all x1, starting transfers between devices, shards(): lax.all_to_all(packed.reshape(bands * step, 1, 128), 'gy', split_axis=0,...  4.77 us
    ppermute x1, starting transfers between devices, shards(): from_left = lax.ppermute(to_right, 'gx', ring('gx', 1))  4.68 us
    unnamed x20, local copies, waits for them, and re-layouts  3.4 us
    ppermute x1, starting transfers between devices, shards(): above = lax.ppermute(tail, 'gy', ring('gy', 1))  1.92 us
  transfers between devices with their start and end apart: 5, of which 2 were waited for; matrix products, arithmetic and copies ran while one was open for 4% of the time, Pallas kernels for 16%

profile of v1, /device:TPU:24, one launch (start us, length us, event | category | flops | bytes accessed | tf_op | source)
XLA Modules:
  0.0 76.8 jit_solution(10923769071907048945)
XLA Ops:
  0.6 0.7 slice_bitcast_fusion.6
  1.4 0.1 pad.3.clone
  1.5 0.1 maximum_maximum_fusion
  1.5 12.7 %collective-permute-start = (f32[24,512]{1,0:T(8,128)S(1)}, f32[24,512]{1,0:T(8,128)S(1)}, u32[]{:S(2)}, u32[]{:S(2)}) collective-permute-start(f32[24,512]{1,0:T(8,128)S(1)} %maximum_maximum_fusion), channel_id=1, source_target_pairs={{0,504},{8,0},{16,8},{24,16},{32,24},{40,32},{48,40},{56,48},{64,5... | collective-permute-start | bytes 147464 | tf_op jit(solution)/shard_map/ppermute | solution.py:451
  14.3 1.7 %slice_bitcast_fusion = (f32[64,512]{1,0:T(8,128)}, f32[64,512]{1,0:T(8,128)}) fusion(f32[2,64,512]{2,1,0:T(8,128)} %param.9), kind=kLoop, calls=%fused_computation | loop fusion | bytes 524288 | tf_op jit(solution)/shard_map/squeeze | solution.py:449
  15.9 0.6 slice_bitcast_fusion.2
  16.6 0.6 copy-done.6
  17.3 0.6 pad_add_fusion.ints_ref
  18.5 2.8 %shard_map.95 = (f32[64,128]{1,0:T(8,128)}, f32[64,128]{1,0:T(8,128)}, bf16[1088,256]{1,0:T(8,128)(2,1)}) custom-call(f32[64,512]{1,0:T(8,128)} %get-tuple-element.25.u_ref, f32[64,512]{1,0:T(8,128)} %get-tuple-element.24.v_ref, f32[64,128]{1,0:T(8,128)} %get-tuple-element.26.rad_ref, s32[64,128]{1,0:T(8,128)} %esc_ref.1, s32[3,64]{1,0:T(4,128)} %pad_add_fusion.ints_ref, ...), custom_call_target="tpu_custom_call" | custom-call | tf_op jit(solution)/shard_map/pallas_call | solution.py:59
  21.3 0.6 copy-done.2
  22.0 2.0 %shard_map.96 = (f32[80,128]{1,0:T(8,128)}, f32[272,128]{1,0:T(8,128)}, f32[64,128]{1,0:T(8,128)}) custom-call(f32[64,512]{1,0:T(8,128)} %f_ref.5, f32[64,512]{1,0:T(8,128)} %get-tuple-element.25.u_ref, f32[64,512]{1,0:T(8,128)} %get-tuple-element.24.v_ref, f32[24,512]{1,0:T(8,128)} %copy-done.2, f32[64,128]{1,0:T(8,128)} %get-tuple-element.13.meta_ref, ...), custom_call_target="tpu_custom_call" | custom-call | tf_op jit(solution)/shard_map/pallas_call | solution.py:59
  23.9 4.7 %collective-permute-start.1 = (f32[272,128]{1,0:T(8,128)}, f32[272,128]{1,0:T(8,128)S(1)}, u32[]{:S(2)}, u32[]{:S(2)}) collective-permute-start(f32[272,128]{1,0:T(8,128)} %get-tuple-element.16), channel_id=1, source_target_pairs={{0,1},{1,2},{2,3},{3,4},{4,5},{5,6},{6,7},{7,0},{8,9},{9,10},{10,1... | collective-permute-start | bytes 417800 | tf_op jit(solution)/shard_map/ppermute | solution.py:465
  28.6 1.9 %collective-permute-start.2 = (f32[80,128]{1,0:T(8,128)}, f32[80,128]{1,0:T(8,128)S(1)}, u32[]{:S(2)}, u32[]{:S(2)}) collective-permute-start(f32[80,128]{1,0:T(8,128)} %get-tuple-element.15.mine_ref), channel_id=1, source_target_pairs={{0,7},{1,0},{2,1},{3,2},{4,3},{5,4},{6,5},{7,6},{8,15},{9,8},{10,9... | collective-permute-start | bytes 122888 | tf_op jit(solution)/shard_map/ppermute | solution.py:464
  30.6 5.4 %collective-permute-done.2.right_ref = f32[80,128]{1,0:T(8,128)S(1)} collective-permute-done((f32[80,128]{1,0:T(8,128)}, f32[80,128]{1,0:T(8,128)S(1)}, u32[]{:S(2)}, u32[]{:S(2)}) %collective-permute-start.2) | collective-permute-done | bytes 40992 | tf_op jit(solution)/shard_map/ppermute | solution.py:464
  36.0 0.6 copy-done.3
  36.6 0.1 copy-done.1
  36.6 3.5 %shard_map.97 = (f32[1088,128]{1,0:T(8,128)}, f32[24,640]{1,0:T(8,128)}) custom-call(f32[64,512]{1,0:T(8,128)} %f_ref.5, f32[64,512]{1,0:T(8,128)} %get-tuple-element.25.u_ref, f32[64,512]{1,0:T(8,128)} %get-tuple-element.24.v_ref, f32[64,128]{1,0:T(8,128)} %get-tuple-element.27.x_ref, f32[64,128]{1,0:T(8,128)} %get-tuple-element.28.y_ref, ...), custom_call_target="tpu_custom_call" | custom-call | tf_op jit(solution)/shard_map/pallas_call | solution.py:59
  40.1 4.8 %all-to-all-start = ((f32[1088,1,128]{2,1,0:T(1,128)}), f32[1088,1,128]{2,1,0:T(1,128)S(1)}, u32[]{:S(2)}, u32[]{:S(2)}) async-start(f32[1088,1,128]{2,1,0:T(1,128)} %bitcast.25), calls=%async_computation | async-start | bytes 1114112 | tf_op jit(solution)/shard_map/all_to_all | solution.py:471
  44.9 1.9 %collective-permute-start.3 = (f32[24,640]{1,0:T(8,128)S(1)}, f32[24,640]{1,0:T(8,128)S(1)}, u32[]{:S(2)}, u32[]{:S(2)}) collective-permute-start(f32[24,640]{1,0:T(8,128)S(1)} %copy-done.9), channel_id=1, source_target_pairs={{0,8},{8,16},{16,24},{24,32},{32,40},{40,48},{48,56},{56,64},{64,7... | collective-permute-start | bytes 184328 | tf_op jit(solution)/shard_map/ppermute | solution.py:474
  46.8 16.1 %collective-permute-done.3.above_ref = f32[24,640]{1,0:T(8,128)S(1)} collective-permute-done((f32[24,640]{1,0:T(8,128)S(1)}, f32[24,640]{1,0:T(8,128)S(1)}, u32[]{:S(2)}, u32[]{:S(2)}) %collective-permute-start.3) | collective-permute-done | bytes 61472 | tf_op jit(solution)/shard_map/ppermute | solution.py:474
  62.9 0.6 copy-done.5
  63.5 9.5 %shard_map.98.base_ref = f32[64,512]{1,0:T(8,128)} custom-call(f32[64,512]{1,0:T(8,128)} %f_ref.5, f32[64,512]{1,0:T(8,128)} %get-tuple-element.25.u_ref, f32[64,512]{1,0:T(8,128)} %get-tuple-element.24.v_ref, f32[24,512]{1,0:T(8,128)} %copy-done.2, f32[80,128]{1,0:T(8,128)} %copy-done.3, f32[272,128]{1,0:T(8,128)} %copy-done.1, f32[24,640]{1,0:T(8,128)} %copy-done.5), custom_call_target="tpu_custom_call" | custom-call | tf_op jit(solution)/shard_map/pallas_call | solution.py:59
  73.0 0.8 %copy-done = f32[1088,1,128]{2,1,0:T(1,128)} copy-done((f32[1088,1,128]{2,1,0:T(1,128)}, f32[1088,1,128]{2,1,0:T(1,128)S(1)}, u32[]{:S(2)}) %copy-start) | copy-done | bytes 557080
  73.8 3.0 %shard_map.99 = (f32[64,512]{1,0:T(8,128)}, f32[1024,128]{1,0:T(8,128)}) custom-call(f32[1088,128]{1,0:T(8,128)} %bitcast.24, f32[64,512]{1,0:T(8,128)} %shard_map.98.base_ref), custom_call_target="tpu_custom_call" | custom-call | tf_op jit(solution)/shard_map/pallas_call | solution.py:59
  (20 shorter events, 0.1 us)
Async XLA Ops:
  0.6 0.8 %slice-start = ((f32[64,512]{1,0:T(8,128)}), f32[9,512]{1,0:T(8,128)S(1)}, s32[]{:S(2)}) async-start(f32[64,512]{1,0:T(8,128)} %f_ref.5), calls=%async_computation.1 | async-start | bytes 65536 | tf_op jit(solution)/shard_map/slice | solution.py:450
  1.5 14.4 %copy-start.4 = (f32[64,3,128]{2,0,1:T(8,128)S(1)}, f32[64,3,128]{2,0,1:T(8,128)}, u32[]{:S(2)}) copy-start(f32[64,3,128]{2,0,1:T(8,128)} %param.10) | copy-start | bytes 294916
  1.5 19.8 %collective-permute-start = (f32[24,512]{1,0:T(8,128)S(1)}, f32[24,512]{1,0:T(8,128)S(1)}, u32[]{:S(2)}, u32[]{:S(2)}) collective-permute-start(f32[24,512]{1,0:T(8,128)S(1)} %maximum_maximum_fusion), channel_id=1, source_target_pairs={{0,504},{8,0},{16,8},{24,16},{32,24},{40,32},{48,40},{56,48},{64,5... | collective-permute-start | bytes 147464 | tf_op jit(solution)/shard_map/ppermute | solution.py:451
  16.6 0.7 copy-start.6
  16.6 0.7 copy-start.7
  16.6 0.7 copy-start.8
  21.3 0.6 copy-start.2
  23.9 12.0 %collective-permute-start.1 = (f32[272,128]{1,0:T(8,128)}, f32[272,128]{1,0:T(8,128)S(1)}, u32[]{:S(2)}, u32[]{:S(2)}) collective-permute-start(f32[272,128]{1,0:T(8,128)} %get-tuple-element.16), channel_id=1, source_target_pairs={{0,1},{1,2},{2,3},{3,4},{4,5},{5,6},{6,7},{7,0},{8,9},{9,10},{10,1... | collective-permute-start | bytes 417800 | tf_op jit(solution)/shard_map/ppermute | solution.py:465
  28.6 7.3 %collective-permute-start.2 = (f32[80,128]{1,0:T(8,128)}, f32[80,128]{1,0:T(8,128)S(1)}, u32[]{:S(2)}, u32[]{:S(2)}) collective-permute-start(f32[80,128]{1,0:T(8,128)} %get-tuple-element.15.mine_ref), channel_id=1, source_target_pairs={{0,7},{1,0},{2,1},{3,2},{4,3},{5,4},{6,5},{7,6},{8,15},{9,8},{10,9... | collective-permute-start | bytes 122888 | tf_op jit(solution)/shard_map/ppermute | solution.py:464
  36.0 0.6 copy-start.3
  36.0 0.7 copy-start.1
  40.1 4.8 %copy-start.9 = (f32[24,640]{1,0:T(8,128)S(1)}, f32[24,640]{1,0:T(8,128)}, u32[]{:S(2)}) copy-start(f32[24,640]{1,0:T(8,128)} %get-tuple-element.19) | copy-start | bytes 184324
  40.1 32.9 %all-to-all-start = ((f32[1088,1,128]{2,1,0:T(1,128)}), f32[1088,1,128]{2,1,0:T(1,128)S(1)}, u32[]{:S(2)}, u32[]{:S(2)}) async-start(f32[1088,1,128]{2,1,0:T(1,128)} %bitcast.25), calls=%async_computation | async-start | bytes 1114112 | tf_op jit(solution)/shard_map/all_to_all | solution.py:471
  44.9 18.1 %collective-permute-start.3 = (f32[24,640]{1,0:T(8,128)S(1)}, f32[24,640]{1,0:T(8,128)S(1)}, u32[]{:S(2)}, u32[]{:S(2)}) collective-permute-start(f32[24,640]{1,0:T(8,128)S(1)} %copy-done.9), channel_id=1, source_target_pairs={{0,8},{8,16},{16,24},{24,32},{32,40},{40,48},{48,56},{56,64},{64,7... | collective-permute-start | bytes 184328 | tf_op jit(solution)/shard_map/ppermute | solution.py:474
  62.9 0.6 copy-start.5
  73.0 0.8 %copy-start = (f32[1088,1,128]{2,1,0:T(1,128)}, f32[1088,1,128]{2,1,0:T(1,128)S(1)}, u32[]{:S(2)}) copy-start(f32[1088,1,128]{2,1,0:T(1,128)S(1)} %all-to-all-done) | copy-start | bytes 1671172

commit v2 on v1

--- a/solution.py
+++ b/solution.py
@@ -54,27 +54,28 @@
     return jnp.floor((x + 0.5) * (1.0 / k))
 
 
-def call(body, outs, *args, scratch=()):
+def call(body, outs, *args, scratch=(), scalars=()):
     vm = pl.BlockSpec(memory_space=pltpu.VMEM)
+    sm = pl.BlockSpec(memory_space=pltpu.SMEM)
     return pl.pallas_call(
         body,
         out_shape=tuple(outs),
-        in_specs=[vm] * len(args),
+        in_specs=[sm] * len(scalars) + [vm] * len(args),
         out_specs=tuple(vm for _ in outs),
         scratch_shapes=list(scratch),
+        compiler_params=pltpu.CompilerParams(vmem_limit_bytes=16 * 1024 * 1024),
         interpret=INTERPRET,
-    )(*args)
-
-
-def prepare_body(u_ref, v_ref, rad_ref, esc_ref, ints_ref, count_ref, meta_ref, w_ref, sel_ref):
-    n = rad_ref.shape[0]
-    height, across = u_ref.shape
-    ints = ints_ref[...].astype(F32)
-    home = to_column(ints[0:1], n)
-    land = to_column(ints[1:2], n)
-    dest_row = ints[2:3]
+    )(*scalars, *args)
+
+
+def prepare_body(count_ref, flow_ref, part_ref, esc_ref, home_ref, land_ref, dest_ref, meta_ref, w_ref, sel_ref):
+    n = esc_ref.shape[0]
+    height, across = flow_ref.shape[1:]
+    home = to_column(home_ref[...].astype(F32), n)
+    land = to_column(land_ref[...].astype(F32), n)
+    dest_row = dest_ref[...].astype(F32)
     dest = to_column(dest_row, n)
-    count = count_ref[...].astype(F32)
+    count = count_ref[0].astype(F32)
     row = floor_div(home, across)
     col = home - row * across
     land_row = floor_div(land, across)
@@ -92,8 +93,8 @@
     at0 = lanes == col
     at1 = lanes == col + 1.0
     parts = []
-    for ref in (u_ref, v_ref):
-        both = exact_pick(pick, ref[...])
+    for component in range(2):
+        both = exact_pick(pick, flow_ref[component])
         low = both[0:n]
         high = both[n:]
         for where_at in (at0, at1):
@@ -105,7 +106,7 @@
     for i, value in enumerate(columns):
         meta = jnp.where(lane == float(i), value, meta)
     meta_ref[...] = meta
-    w_ref[...] = esc_ref[...].astype(F32) * rad_ref[...]
+    w_ref[...] = esc_ref[...].astype(F32) * part_ref[2]
     total = sel_ref.shape[0]
     step = 4 * CAP + 1
     r = iota((total, 1), 0)
@@ -117,8 +118,8 @@
     sel_ref[...] = one_hot(code == slots)
 
 
-def edges_body(f_ref, u_ref, v_ref, below_ref, meta_ref, x_ref, y_ref, w_ref, left_ref, right_ref, meta2_ref):
-    n = x_ref.shape[0]
+def edges_body(f_ref, flow_ref, below_ref, above_ref, meta_ref, part_ref, w_ref, left_ref, right_ref, meta2_ref):
+    n = w_ref.shape[0]
     height, across = f_ref.shape
     meta = meta_ref[...]
     lane = iota((n, 128), 1)
@@ -147,16 +148,21 @@
         )
         return jnp.where(lane < 16.0, m, out)
 
-    left_ref[0:height] = pack_left(f_ref[:, 0:128], u_ref[:, 0:128], v_ref[:, 0:128])
-    right_ref[0:height] = pack_right(f_ref[:, far:], u_ref[:, far:], v_ref[:, far:], meta)
     zero = jnp.zeros((8, 128), F32)
-    left_ref[height : height + 8] = pack_left(below_ref[0:8, 0:128], below_ref[9:17, 0:128], below_ref[15:23, 0:128])
-    left_ref[height + 8 : height + 16] = pack_left(below_ref[8:16, 0:128], zero, zero)
-    right_ref[height : height + 8] = pack_right(below_ref[0:8, far:], below_ref[9:17, far:], below_ref[15:23, far:], zero)
-    right_ref[height + 8 : height + 16] = pack_right(below_ref[8:16, far:], zero, zero, zero)
-    top = height + 16
-    right_ref[top : top + n] = x_ref[...]
-    right_ref[top + n : top + 2 * n] = y_ref[...]
+
+    def pieces(sl):
+        yield 0, height, f_ref[:, sl], flow_ref[0, :, sl], flow_ref[1, :, sl], meta
+        for top, ref in ((height, below_ref), (height + 16, above_ref)):
+            yield top, 8, ref[0:8, sl], ref[9:17, sl], ref[15:23, sl], zero
+            yield top + 8, 8, ref[8:16, sl], zero, zero, zero
+
+    for top, rows, f, u, v, _ in pieces(slice(0, 128)):
+        left_ref[top : top + rows] = pack_left(f, u, v)
+    for top, rows, f, u, v, m in pieces(slice(far, across)):
+        right_ref[top : top + rows] = pack_right(f, u, v, m)
+    top = height + 32
+    right_ref[top : top + n] = part_ref[0]
+    right_ref[top + n : top + 2 * n] = part_ref[1]
     right_ref[top + 2 * n : top + 3 * n] = w_ref[...]
 
 
@@ -195,22 +201,19 @@
     return jnp.sum(x, axis=1, keepdims=True)
 
 
-def pack_body(
-    f_ref, u_ref, v_ref, x_ref, y_ref, rad_ref, w_ref, meta_ref, mine_ref, left_ref, right_ref, sel_ref, out_ref, tail_ref
-):
-    n = x_ref.shape[0]
-    height, across = f_ref.shape
+def pack_body(part_ref, w_ref, meta_ref, mine_ref, left_ref, right_ref, sel_ref, out_ref, height, across):
+    n = w_ref.shape[0]
     bands = out_ref.shape[0] // (4 * CAP + 1)
     meta = meta_ref[...]
-    top = height + 16
+    top = height + 32
     w = w_ref[...]
-    new_x, new_y = moved_particles(meta, x_ref[...], y_ref[...], right_ref[...], across)
+    new_x, new_y = moved_particles(meta, part_ref[0], part_ref[1], right_ref[0 : height + 16], across)
     left_meta = left_ref[0:n]
     left_w = left_ref[top + 2 * n : top + 3 * n]
     left_x, left_y = moved_particles(
-        left_meta, left_ref[top : top + n], left_ref[top + n : top + 2 * n], mine_ref[...], across
-    )
-    body = jnp.concatenate([new_x, new_y, rad_ref[...], w], axis=0)
+        left_meta, left_ref[top : top + n], left_ref[top + n : top + 2 * n], mine_ref[0 : height + 16], across
+    )
+    body = jnp.concatenate([new_x, new_y, part_ref[2], w], axis=0)
     out_ref[...] = exact_pick(sel_ref[...], body)
     gy = new_y + 0.5
     gx = new_x + 0.5
@@ -251,15 +254,6 @@
     table = table + pltpu.roll(pltpu.roll(table, 1, 0), 64, 1)
     step = 4 * CAP + 1
     out_ref[pl.ds(4 * CAP, bands, stride=step), :] = table
-    f4, u4, v4 = halo_tiles(right_ref[height - 16 : height], left_ref[height - 16 : height])
-    tail_ref[0:9, 0:across] = f_ref[height - 9 : height]
-    tail_ref[9:15, 0:across] = u_ref[height - 6 : height]
-    tail_ref[15:21, 0:across] = v_ref[height - 6 : height]
-    tail_ref[0:9, across:] = f4[7:16]
-    tail_ref[9:15, across:] = u4[10:16]
-    tail_ref[15:21, across:] = v4[10:16]
-    tail_ref[21:24, :] = jnp.zeros((3, across + 128), F32)
-
 
 def side_term(speed, e0, e1, e2, e3, e4, d2, d3):
     ahead = speed > 0.0
@@ -282,23 +276,25 @@
     return speed * c + jnp.abs(speed) * (top / (6.0 * (w1 + w2 + w3)))
 
 
-def stencil_body(f_ref, u_ref, v_ref, below_ref, right_ref, left_ref, above_ref, out_ref, f0, us, vs, f1, f2):
+def stencil_body(f_ref, flow_ref, below_ref, above_ref, right_ref, left_ref, out_ref, f0, us, vs, f1, f2):
     height, across = f_ref.shape
     width = across + 128
     tiles = width // 128
     off = 16
     span = height + 32
-    f4, u4, v4 = halo_tiles(right_ref[...], left_ref[0 : height + 16])
-    for buf, own, halo, start, count in ((f0, f_ref, f4, 0, 9), (us, u_ref, u4, 9, 6), (vs, v_ref, v4, 15, 6)):
+    f4, u4, v4 = halo_tiles(right_ref[...], left_ref[0 : height + 32])
+    fields = ((f0, f_ref, f4, 0, 9), (us, flow_ref.at[0], u4, 9, 6), (vs, flow_ref.at[1], v4, 15, 6))
+    for buf, own, halo, start, count in fields:
         for j in range(tiles):
             sl = slice(128 * j, 128 * j + 128)
             top = span * j + off
             if j < tiles - 1:
                 buf[top : top + height, :] = own[:, sl]
                 buf[top + height : top + height + count, :] = below_ref[start : start + count, sl]
+                buf[top - count : top, :] = above_ref[start : start + count, sl]
             else:
-                buf[top : top + height + 16, :] = halo
-            buf[top - count : top, :] = above_ref[start : start + count, sl]
+                buf[top : top + height + count, :] = halo[0 : height + count]
+                buf[top - count : top, :] = halo[height + 16 : height + 16 + count]
 
     lane = lax.broadcasted_iota(jnp.int32, (8, 128), 1)
 
@@ -447,36 +443,38 @@
     step = 4 * CAP + 1
     sds = jax.ShapeDtypeStruct
     u, v = velocity[0], velocity[1]
-    head = jnp.concatenate([level_set[0:9], u[0:6], v[0:6], jnp.zeros((3, across), F32)], axis=0)
+    pad = jnp.zeros((3, across), F32)
+    head = jnp.concatenate([level_set[:9], u[:6], v[:6], pad], axis=0)
+    tail = jnp.concatenate([level_set[-9:], u[-6:], v[-6:], pad], axis=0)
     below = lax.ppermute(head, "gy", ring("gy", -1))
-    x, y, radius = particles[:, 0, :], particles[:, 1, :], particles[:, 2, :]
-    ints = jnp.stack([home_cell, land_cell, dest_rank], axis=0)
+    above = lax.ppermute(tail, "gy", ring("gy", 1))
+    parts = jnp.transpose(particles, (1, 0, 2))
     meta, weight, select = call(
         prepare_body,
         (sds((n, 128), F32), sds((n, 128), F32), sds((bands * step, 4 * n), BF16)),
-        u, v, radius, escaped, ints, block_count.reshape(1, 1),
+        velocity, parts, escaped, home_cell.reshape(1, n), land_cell.reshape(1, n), dest_rank.reshape(1, n),
+        scalars=(block_count,),
     )
     to_left, to_right, meta = call(
         edges_body,
-        (sds((height + 16, 128), F32), sds((height + 16 + 3 * n, 128), F32), sds((n, 128), F32)),
-        level_set, u, v, below, meta, x, y, weight,
+        (sds((height + 32, 128), F32), sds((height + 32 + 3 * n, 128), F32), sds((n, 128), F32)),
+        level_set, velocity, below, above, meta, parts, weight,
     )
     from_right = lax.ppermute(to_left, "gx", ring("gx", -1))
     from_left = lax.ppermute(to_right, "gx", ring("gx", 1))
-    packed, tail = call(
-        pack_body,
-        (sds((bands * step, 128), F32), sds((24, across + 128), F32)),
-        level_set, u, v, x, y, radius, weight, meta, to_left, from_left, from_right, select,
+    (packed,) = call(
+        functools.partial(pack_body, height=height, across=across),
+        (sds((bands * step, 128), F32),),
+        parts, weight, meta, to_left, from_left, from_right, select,
     )
     arrived = lax.all_to_all(
         packed.reshape(bands * step, 1, 128), "gy", split_axis=0, concat_axis=0, tiled=True
     ).reshape(bands * step, 128)
-    above = lax.ppermute(tail, "gy", ring("gy", 1))
     wide = pltpu.VMEM(((across // 128 + 1) * (height + 32), 128), F32)
     (section,) = call(
         stencil_body,
         (sds((height, across), F32),),
-        level_set, u, v, below, from_right, from_left, above,
+        level_set, velocity, below, above, from_right, from_left,
         scratch=[wide] * 5,
     )
     level, moved = call(

time: 77.4 us -> 60.3 us (0.78)
  the two profiles are of different devices: /device:TPU:24 before, /device:TPU:31 now
where the time goes in v2:
time: 60.3 us; the launch traced here: 59.8 us
  starting transfers between devices  27.7 us (46%)
  waiting for transfers between devices  15.5 us (26%)
  Pallas kernels  12.9 us (21%)
  local copies, waits for them, and re-layouts  2.32 us (4%)
  between operations  1.41 us (2%)
    all_to_all x1, starting transfers between devices, shards(): lax.all_to_all(packed.reshape(bands * step, 1, 128), 'gy', split_axis=0,...  14.9 us
    pallas_call x5, Pallas kernels, call(): pl.pallas_call(body, out_shape=tuple(outs), in_specs=[sm] * len(scalars)...  12.9 us
    all_to_all x1, waiting for transfers between devices, shards(): lax.all_to_all(packed.reshape(bands * step, 1, 128), 'gy', split_axis=0,...  10.2 us
    ppermute x1, starting transfers between devices, shards(): above = lax.ppermute(tail, 'gy', ring('gy', 1))  4.55 us
    ppermute x1, starting transfers between devices, shards(): from_left = lax.ppermute(to_right, 'gx', ring('gx', 1))  4.42 us
    ppermute x1, waiting for transfers between devices, shards(): from_right = lax.ppermute(to_left, 'gx', ring('gx', -1))  4.12 us
    ppermute x1, starting transfers between devices, shards(): from_right = lax.ppermute(to_left, 'gx', ring('gx', -1))  1.92 us
    ppermute x1, starting transfers between devices, shards(): below = lax.ppermute(head, 'gy', ring('gy', -1))  1.92 us
  transfers between devices with their start and end apart: 5, of which 3 were waited for; matrix products, arithmetic and copies ran while one was open for 0% of the time, Pallas kernels for 14%

profile of v2, /device:TPU:31, one launch (start us, length us, event | category | flops | bytes accessed | tf_op | source)
XLA Modules:
  0.0 59.8 jit_solution(17966835724055438184)
XLA Ops:
  0.6 0.8 %slice_bitcast_fusion.1 = (f32[6,512]{1,0:T(8,128)S(1)}, f32[6,512]{1,0:T(8,128)S(1)}, f32[6,512]{1,0:T(8,128)S(1)}, f32[6,512]{1,0:T(8,128)S(1)}) fusion(f32[2,64,512]{2,1,0:T(8,128)} %flow_ref.5), kind=kLoop, calls=%fused_computation.3 | loop fusion | bytes 98304 | tf_op jit(solution)/shard_map/slice | solution.py:448
  1.5 0.8 %fusion = (f32[9,512]{1,0:T(8,128)S(1)}, f32[9,512]{1,0:T(8,128)S(1)}) fusion(f32[64,512]{1,0:T(8,128)} %f_ref.3), kind=kLoop, calls=%fused_computation.6 | loop fusion | bytes 73728 | tf_op jit(solution)/shard_map/slice | solution.py:448
  2.2 0.1 pad.7.clone
  2.3 0.1 maximum_maximum_fusion.1
  2.4 4.5 %collective-permute-start.1 = (f32[24,512]{1,0:T(8,128)S(1)}, f32[24,512]{1,0:T(8,128)S(1)}, u32[]{:S(2)}, u32[]{:S(2)}) collective-permute-start(f32[24,512]{1,0:T(8,128)S(1)} %get-tuple-element.24), channel_id=1, source_target_pairs={{0,8},{8,16},{16,24},{24,32},{32,40},{40,48},{48,56},{56,64},{64,7... | collective-permute-start | bytes 147464 | tf_op jit(solution)/shard_map/ppermute | solution.py:450
  7.0 1.9 %collective-permute-start = (f32[24,512]{1,0:T(8,128)S(1)}, f32[24,512]{1,0:T(8,128)S(1)}, u32[]{:S(2)}, u32[]{:S(2)}) collective-permute-start(f32[24,512]{1,0:T(8,128)S(1)} %get-tuple-element.25), channel_id=1, source_target_pairs={{0,504},{8,0},{16,8},{24,16},{32,24},{40,32},{48,40},{56,48},{64,5... | collective-permute-start | bytes 147464 | tf_op jit(solution)/shard_map/ppermute | solution.py:449
  9.5 0.0 copy-start.4
  9.5 0.0 copy-start.5
  9.6 0.0 copy-start.6
  9.6 0.6 copy-done.4
  10.2 0.0 copy-done.5
  10.2 0.0 copy-done.6
  10.2 1.0 %shard_map.95 = (f32[64,128]{1,0:T(8,128)S(1)}, f32[64,128]{1,0:T(8,128)S(1)}, bf16[1088,256]{1,0:T(8,128)(2,1)S(1)}) custom-call(s32[1]{0:T(128)S(6)} %copy.11.count_ref, f32[2,64,512]{2,1,0:T(8,128)S(1)} %copy-done, f32[3,64,128]{2,1,0:T(8,128)S(1)} %bitcast.18, s32[64,128]{1,0:T(8,128)S(1)} %copy-done.3, s32[1,64]{1,0:T(1,128)S(1)} %bitcast.21, ...), custom_call_target="tpu_custom_call" | custom-call | tf_op jit(solution)/shard_map/pallas_call | solution.py:60
  11.2 0.0 collective-permute-done.1.above_ref
  11.2 1.1 %collective-permute-done.below_ref = f32[24,512]{1,0:T(8,128)S(1)} collective-permute-done((f32[24,512]{1,0:T(8,128)S(1)}, f32[24,512]{1,0:T(8,128)S(1)}, u32[]{:S(2)}, u32[]{:S(2)}) %collective-permute-start) | collective-permute-done | bytes 49184 | tf_op jit(solution)/shard_map/ppermute | solution.py:449
  12.4 0.3 shard_map.96
  12.6 4.4 %collective-permute-start.2 = (f32[288,128]{1,0:T(8,128)S(1)}, f32[288,128]{1,0:T(8,128)S(1)}, u32[]{:S(2)}, u32[]{:S(2)}) collective-permute-start(f32[288,128]{1,0:T(8,128)S(1)} %get-tuple-element.14), channel_id=1, source_target_pairs={{0,1},{1,2},{2,3},{3,4},{4,5},{5,6},{6,7},{7,0},{8,9},{9,10},{10,1... | collective-permute-start | bytes 442376 | tf_op jit(solution)/shard_map/ppermute | solution.py:464
  17.1 1.9 %collective-permute-start.3 = (f32[96,128]{1,0:T(8,128)S(1)}, f32[96,128]{1,0:T(8,128)S(1)}, u32[]{:S(2)}, u32[]{:S(2)}) collective-permute-start(f32[96,128]{1,0:T(8,128)S(1)} %get-tuple-element.13.mine_ref), channel_id=1, source_target_pairs={{0,7},{1,0},{2,1},{3,2},{4,3},{5,4},{6,5},{7,6},{8,15},{9,8},{10,9... | collective-permute-start | bytes 147464 | tf_op jit(solution)/shard_map/ppermute | solution.py:463
  19.0 4.1 %collective-permute-done.3.right_ref = f32[96,128]{1,0:T(8,128)S(1)} collective-permute-done((f32[96,128]{1,0:T(8,128)S(1)}, f32[96,128]{1,0:T(8,128)S(1)}, u32[]{:S(2)}, u32[]{:S(2)}) %collective-permute-start.3) | collective-permute-done | bytes 49184 | tf_op jit(solution)/shard_map/ppermute | solution.py:463
  23.1 2.1 %shard_map.97 = f32[1088,128]{1,0:T(8,128)} custom-call(f32[3,64,128]{2,1,0:T(8,128)S(1)} %bitcast.20, f32[64,128]{1,0:T(8,128)S(1)} %get-tuple-element.10.w_ref, f32[64,128]{1,0:T(8,128)S(1)} %get-tuple-element.12.meta_ref, f32[96,128]{1,0:T(8,128)S(1)} %get-tuple-element.13.mine_ref, f32[288,128]{1,0:T(8,128)S(1)} %collective-permute-done.2.left_ref, ...), custom_call_target="tpu_custom_call" | custom-call | tf_op jit(solution)/shard_map/pallas_call | solution.py:60
  25.2 14.9 %all-to-all-start = ((f32[1088,1,128]{2,1,0:T(1,128)}), f32[1088,1,128]{2,1,0:T(1,128)S(1)}, u32[]{:S(2)}, u32[]{:S(2)}) async-start(f32[1088,1,128]{2,1,0:T(1,128)} %bitcast.9), calls=%async_computation | async-start | bytes 1114112 | tf_op jit(solution)/shard_map/all_to_all | solution.py:470
  40.0 7.7 %shard_map.98.base_ref = f32[64,512]{1,0:T(8,128)S(1)} custom-call(f32[64,512]{1,0:T(8,128)S(1)} %copy-done.2, f32[2,64,512]{2,1,0:T(8,128)S(1)} %copy-done, f32[24,512]{1,0:T(8,128)S(1)} %collective-permute-done.below_ref, f32[24,512]{1,0:T(8,128)S(1)} %collective-permute-done.1.above_ref, f32[96,128]{1,0:T(8,128)S(1)} %collective-permute-done.3.right_ref, ...), custom_call_target="tpu_custom_call" | custom-call | tf_op jit(solution)/shard_map/pallas_call | solution.py:60
  47.7 10.2 %all-to-all-done = f32[1088,1,128]{2,1,0:T(1,128)S(1)} async-done(((f32[1088,1,128]{2,1,0:T(1,128)}), f32[1088,1,128]{2,1,0:T(1,128)S(1)}, u32[]{:S(2)}, u32[]{:S(2)}) %all-to-all-start) | async-done | bytes 557088 | tf_op jit(solution)/shard_map/all_to_all | solution.py:470
  57.9 1.9 %shard_map.99 = (f32[64,512]{1,0:T(8,128)}, f32[1024,128]{1,0:T(8,128)}) custom-call(f32[1088,128]{1,0:T(8,128)S(1)} %bitcast.17, f32[64,512]{1,0:T(8,128)S(1)} %shard_map.98.base_ref), custom_call_target="tpu_custom_call" | custom-call | tf_op jit(solution)/shard_map/pallas_call | solution.py:60
  (10 shorter events, 0.0 us)
Async XLA Ops:
  0.6 8.9 %copy-start = (f32[2,64,512]{2,1,0:T(8,128)S(1)}, f32[2,64,512]{2,1,0:T(8,128)}, u32[]{:S(2)}) copy-start(f32[2,64,512]{2,1,0:T(8,128)} %flow_ref.5) | copy-start | bytes 786436
  2.3 7.3 %copy-start.1 = (f32[64,3,128]{2,0,1:T(8,128)S(1)}, f32[64,3,128]{2,0,1:T(8,128)}, u32[]{:S(2)}) copy-start(f32[64,3,128]{2,0,1:T(8,128)} %param.10) | copy-start | bytes 294916
  2.3 7.3 %copy-start.3 = (s32[64,128]{1,0:T(8,128)S(1)}, s32[64,128]{1,0:T(8,128)}, u32[]{:S(2)}) copy-start(s32[64,128]{1,0:T(8,128)} %esc_ref.1) | copy-start | bytes 98308
  2.4 8.8 %collective-permute-start.1 = (f32[24,512]{1,0:T(8,128)S(1)}, f32[24,512]{1,0:T(8,128)S(1)}, u32[]{:S(2)}, u32[]{:S(2)}) collective-permute-start(f32[24,512]{1,0:T(8,128)S(1)} %get-tuple-element.24), channel_id=1, source_target_pairs={{0,8},{8,16},{16,24},{24,32},{32,40},{40,48},{48,56},{56,64},{64,7... | collective-permute-start | bytes 147464 | tf_op jit(solution)/shard_map/ppermute | solution.py:450
  7.0 5.4 %collective-permute-start = (f32[24,512]{1,0:T(8,128)S(1)}, f32[24,512]{1,0:T(8,128)S(1)}, u32[]{:S(2)}, u32[]{:S(2)}) collective-permute-start(f32[24,512]{1,0:T(8,128)S(1)} %get-tuple-element.25), channel_id=1, source_target_pairs={{0,504},{8,0},{16,8},{24,16},{32,24},{40,32},{48,40},{56,48},{64,5... | collective-permute-start | bytes 147464 | tf_op jit(solution)/shard_map/ppermute | solution.py:449
  9.5 0.7 %copy-start.4 = (s32[64]{0:T(128)S(1)}, s32[64]{0:T(128)}, u32[]{:S(2)}) copy-start(s32[64]{0:T(128)} %param.12) | copy-start | bytes 772
  9.5 0.7 %copy-start.5 = (s32[64]{0:T(128)S(1)}, s32[64]{0:T(128)}, u32[]{:S(2)}) copy-start(s32[64]{0:T(128)} %param.13) | copy-start | bytes 772
  9.6 0.7 %copy-start.6 = (s32[64]{0:T(128)S(1)}, s32[64]{0:T(128)}, u32[]{:S(2)}) copy-start(s32[64]{0:T(128)} %param.14) | copy-start | bytes 772
  10.2 2.1 %copy-start.2 = (f32[64,512]{1,0:T(8,128)S(1)}, f32[64,512]{1,0:T(8,128)}, u32[]{:S(2)}) copy-start(f32[64,512]{1,0:T(8,128)} %f_ref.3) | copy-start | bytes 393220
  12.6 10.5 %collective-permute-start.2 = (f32[288,128]{1,0:T(8,128)S(1)}, f32[288,128]{1,0:T(8,128)S(1)}, u32[]{:S(2)}, u32[]{:S(2)}) collective-permute-start(f32[288,128]{1,0:T(8,128)S(1)} %get-tuple-element.14), channel_id=1, source_target_pairs={{0,1},{1,2},{2,3},{3,4},{4,5},{5,6},{6,7},{7,0},{8,9},{9,10},{10,1... | collective-permute-start | bytes 442376 | tf_op jit(solution)/shard_map/ppermute | solution.py:464
  17.1 6.0 %collective-permute-start.3 = (f32[96,128]{1,0:T(8,128)S(1)}, f32[96,128]{1,0:T(8,128)S(1)}, u32[]{:S(2)}, u32[]{:S(2)}) collective-permute-start(f32[96,128]{1,0:T(8,128)S(1)} %get-tuple-element.13.mine_ref), channel_id=1, source_target_pairs={{0,7},{1,0},{2,1},{3,2},{4,3},{5,4},{6,5},{7,6},{8,15},{9,8},{10,9... | collective-permute-start | bytes 147464 | tf_op jit(solution)/shard_map/ppermute | solution.py:463
  25.2 32.8 %all-to-all-start = ((f32[1088,1,128]{2,1,0:T(1,128)}), f32[1088,1,128]{2,1,0:T(1,128)S(1)}, u32[]{:S(2)}, u32[]{:S(2)}) async-start(f32[1088,1,128]{2,1,0:T(1,128)} %bitcast.9), calls=%async_computation | async-start | bytes 1114112 | tf_op jit(solution)/shard_map/all_to_all | solution.py:470

commit v3 on v2

--- a/solution.py
+++ b/solution.py
@@ -68,7 +68,16 @@
     )(*scalars, *args)
 
 
-def prepare_body(count_ref, flow_ref, part_ref, esc_ref, home_ref, land_ref, dest_ref, meta_ref, w_ref, sel_ref):
+def heads_body(f_ref, flow_ref, head_ref, tail_ref):
+    height = f_ref.shape[0]
+    for ref, f0, v0 in ((head_ref, 0, 0), (tail_ref, height - 9, height - 6)):
+        ref[0:9] = f_ref[f0 : f0 + 9]
+        ref[9:15] = flow_ref[0, v0 : v0 + 6]
+        ref[15:21] = flow_ref[1, v0 : v0 + 6]
+        ref[21:24] = jnp.zeros((3, f_ref.shape[1]), F32)
+
+
+def prepare_body(count_ref, flow_ref, part_ref, esc_ref, home_ref, land_ref, dest_ref, meta_ref, w_ref, sel_ref, rw_ref):
     n = esc_ref.shape[0]
     height, across = flow_ref.shape[1:]
     home = to_column(home_ref[...].astype(F32), n)
@@ -106,19 +115,39 @@
     for i, value in enumerate(columns):
         meta = jnp.where(lane == float(i), value, meta)
     meta_ref[...] = meta
-    w_ref[...] = esc_ref[...].astype(F32) * part_ref[2]
-    total = sel_ref.shape[0]
-    step = 4 * CAP + 1
-    r = iota((total, 1), 0)
-    d = floor_div(r, step)
-    q = r - d * step
-    code = jnp.where(q < 4.0 * CAP, d * (4.0 * CAP) + q, -1000.0)
-    slots = jnp.concatenate([slot_row * 4.0 + float(j) for j in range(4)], axis=1)
-    slots = jnp.where(jnp.concatenate([slot_row] * 4, axis=1) < 0.0, -1.0, slots)
-    sel_ref[...] = one_hot(code == slots)
-
-
-def edges_body(f_ref, flow_ref, below_ref, above_ref, meta_ref, part_ref, w_ref, left_ref, right_ref, meta2_ref):
+    w = esc_ref[...].astype(F32) * part_ref[2]
+    w_ref[...] = w
+    slots = sel_ref.shape[0]
+    bands = slots // CAP
+    r = iota((slots, 1), 0)
+    k = floor_div(r, bands)
+    choose = one_hot((r - k * bands) * CAP + k == slot_row)
+    sel_ref[...] = choose
+    rw_ref[...] = exact_pick(choose, jnp.concatenate([part_ref[2], w], axis=1))
+
+
+def pack_left(f, u, v):
+    lane = iota(f.shape, 1)
+    return jnp.where(lane < 16.0, f, jnp.where(lane < 32.0, pltpu.roll(u, 16, 1), pltpu.roll(v, 32, 1)))
+
+
+def pack_right(f, u, v, m):
+    lane = iota(f.shape, 1)
+    out = jnp.where(lane >= 112.0, f, jnp.where(lane >= 96.0, pltpu.roll(u, 112, 1), pltpu.roll(v, 96, 1)))
+    return jnp.where(lane < 16.0, m, out)
+
+
+def corners_body(above_ref, left_ref, right_ref):
+    across = above_ref.shape[1]
+    zero = jnp.zeros((8, 128), F32)
+    near, far = slice(0, 128), slice(across - 128, across)
+    left_ref[0:8] = pack_left(above_ref[0:8, near], above_ref[9:17, near], above_ref[15:23, near])
+    left_ref[8:16] = pack_left(above_ref[8:16, near], zero, zero)
+    right_ref[0:8] = pack_right(above_ref[0:8, far], above_ref[9:17, far], above_ref[15:23, far], zero)
+    right_ref[8:16] = pack_right(above_ref[8:16, far], zero, zero, zero)
+
+
+def edges_body(f_ref, flow_ref, below_ref, meta_ref, part_ref, w_ref, left_ref, right_ref, meta2_ref):
     n = w_ref.shape[0]
     height, across = f_ref.shape
     meta = meta_ref[...]
@@ -137,30 +166,18 @@
     meta2_ref[...] = meta
     far = across - 128
 
-    def pack_left(f, u, v):
-        lane = iota(f.shape, 1)
-        return jnp.where(lane < 16.0, f, jnp.where(lane < 32.0, pltpu.roll(u, 16, 1), pltpu.roll(v, 32, 1)))
-
-    def pack_right(f, u, v, m):
-        lane = iota(f.shape, 1)
-        out = jnp.where(
-            lane >= 112.0, f, jnp.where(lane >= 96.0, pltpu.roll(u, 112, 1), pltpu.roll(v, 96, 1))
-        )
-        return jnp.where(lane < 16.0, m, out)
-
     zero = jnp.zeros((8, 128), F32)
 
     def pieces(sl):
         yield 0, height, f_ref[:, sl], flow_ref[0, :, sl], flow_ref[1, :, sl], meta
-        for top, ref in ((height, below_ref), (height + 16, above_ref)):
-            yield top, 8, ref[0:8, sl], ref[9:17, sl], ref[15:23, sl], zero
-            yield top + 8, 8, ref[8:16, sl], zero, zero, zero
+        yield height, 8, below_ref[0:8, sl], below_ref[9:17, sl], below_ref[15:23, sl], zero
+        yield height + 8, 8, below_ref[8:16, sl], zero, zero, zero
 
     for top, rows, f, u, v, _ in pieces(slice(0, 128)):
         left_ref[top : top + rows] = pack_left(f, u, v)
     for top, rows, f, u, v, m in pieces(slice(far, across)):
         right_ref[top : top + rows] = pack_right(f, u, v, m)
-    top = height + 32
+    top = height + 16
     right_ref[top : top + n] = part_ref[0]
     right_ref[top + n : top + 2 * n] = part_ref[1]
     right_ref[top + 2 * n : top + 3 * n] = w_ref[...]
@@ -201,11 +218,12 @@
     return jnp.sum(x, axis=1, keepdims=True)
 
 
-def pack_body(part_ref, w_ref, meta_ref, mine_ref, left_ref, right_ref, sel_ref, out_ref, height, across):
+def pack_body(part_ref, w_ref, meta_ref, mine_ref, left_ref, right_ref, sel_ref, rw_ref, out_ref, height, across):
     n = w_ref.shape[0]
     bands = out_ref.shape[0] // (4 * CAP + 1)
     meta = meta_ref[...]
-    top = height + 32
+    top = height + 16
+    step = 4 * CAP + 1
     w = w_ref[...]
     new_x, new_y = moved_particles(meta, part_ref[0], part_ref[1], right_ref[0 : height + 16], across)
     left_meta = left_ref[0:n]
@@ -213,8 +231,12 @@
     left_x, left_y = moved_particles(
         left_meta, left_ref[top : top + n], left_ref[top + n : top + 2 * n], mine_ref[0 : height + 16], across
     )
-    body = jnp.concatenate([new_x, new_y, part_ref[2], w], axis=0)
-    out_ref[...] = exact_pick(sel_ref[...], body)
+    choose = sel_ref[...]
+    xy = exact_pick(choose, jnp.concatenate([new_x, new_y], axis=1))
+    for k in range(CAP):
+        rows = slice(k * bands, (k + 1) * bands)
+        for j, source, sl in ((0, xy, slice(0, 128)), (1, xy, slice(128, 256)), (2, rw_ref, slice(0, 128)), (3, rw_ref, slice(128, 256))):
+            out_ref[pl.ds(4 * k + j, bands, stride=step), :] = source[rows, sl]
     gy = new_y + 0.5
     gx = new_x + 0.5
     sums = [
@@ -242,18 +264,18 @@
     for i, value in enumerate(sums):
         theirs = jnp.where(lane16 == float(8 + i), value, theirs)
     values = jnp.concatenate([mine, theirs], axis=0)
-    slot = jnp.concatenate([to_row(meta[:, 12:13], n), to_row(left_meta[:, 12:13], n)], axis=1)
-    d4 = iota((bands, 2 * n), 0) * float(CAP)
-    choose = jnp.concatenate([one_hot(d4 + float(k) == slot) for k in range(CAP)], axis=0)
-    chosen = exact_pick(choose, values)
+    d4 = iota((bands, n), 0) * float(CAP)
+    slot = to_row(left_meta[:, 12:13], n)
+    theirs_choose = jnp.concatenate([one_hot(d4 + float(k) == slot) for k in range(CAP)], axis=0)
+    chosen = exact_pick(jnp.concatenate([choose, theirs_choose], axis=1), values)
     lane = iota((bands, 128), 1)
     group = jnp.floor(lane * 0.0625)
     table = jnp.zeros((bands, 128), F32)
     for k in range(CAP):
         table = jnp.where(group == float(k), chosen[k * bands : (k + 1) * bands], table)
     table = table + pltpu.roll(pltpu.roll(table, 1, 0), 64, 1)
-    step = 4 * CAP + 1
     out_ref[pl.ds(4 * CAP, bands, stride=step), :] = table
+
 
 def side_term(speed, e0, e1, e2, e3, e4, d2, d3):
     ahead = speed > 0.0
@@ -276,15 +298,16 @@
     return speed * c + jnp.abs(speed) * (top / (6.0 * (w1 + w2 + w3)))
 
 
-def stencil_body(f_ref, flow_ref, below_ref, above_ref, right_ref, left_ref, out_ref, f0, us, vs, f1, f2):
+def stencil_body(f_ref, flow_ref, below_ref, above_ref, right_ref, left_ref, right2_ref, left2_ref, out_ref, f0, us, vs, f1, f2):
     height, across = f_ref.shape
     width = across + 128
     tiles = width // 128
     off = 16
     span = height + 32
-    f4, u4, v4 = halo_tiles(right_ref[...], left_ref[0 : height + 32])
-    fields = ((f0, f_ref, f4, 0, 9), (us, flow_ref.at[0], u4, 9, 6), (vs, flow_ref.at[1], v4, 15, 6))
-    for buf, own, halo, start, count in fields:
+    halos = halo_tiles(right_ref[...], left_ref[0 : height + 16])
+    uppers = halo_tiles(right2_ref[...], left2_ref[...])
+    owns = (f_ref, flow_ref.at[0], flow_ref.at[1])
+    for buf, own, halo, upper, start, count in zip((f0, us, vs), owns, halos, uppers, (0, 9, 15), (9, 6, 6)):
         for j in range(tiles):
             sl = slice(128 * j, 128 * j + 128)
             top = span * j + off
@@ -294,7 +317,7 @@
                 buf[top - count : top, :] = above_ref[start : start + count, sl]
             else:
                 buf[top : top + height + count, :] = halo[0 : height + count]
-                buf[top - count : top, :] = halo[height + 16 : height + 16 + count]
+                buf[top - count : top, :] = upper[0:count]
 
     lane = lax.broadcasted_iota(jnp.int32, (8, 128), 1)
 
@@ -442,39 +465,44 @@
     bands = lax.axis_size("gy")
     step = 4 * CAP + 1
     sds = jax.ShapeDtypeStruct
-    u, v = velocity[0], velocity[1]
-    pad = jnp.zeros((3, across), F32)
-    head = jnp.concatenate([level_set[:9], u[:6], v[:6], pad], axis=0)
-    tail = jnp.concatenate([level_set[-9:], u[-6:], v[-6:], pad], axis=0)
+    head, tail = call(heads_body, (sds((24, across), F32), sds((24, across), F32)), level_set, velocity)
     below = lax.ppermute(head, "gy", ring("gy", -1))
     above = lax.ppermute(tail, "gy", ring("gy", 1))
     parts = jnp.transpose(particles, (1, 0, 2))
-    meta, weight, select = call(
+    meta, weight, select, fixed = call(
         prepare_body,
-        (sds((n, 128), F32), sds((n, 128), F32), sds((bands * step, 4 * n), BF16)),
+        (
+            sds((n, 128), F32),
+            sds((n, 128), F32),
+            sds((bands * CAP, n), BF16),
+            sds((bands * CAP, 256), F32),
+        ),
         velocity, parts, escaped, home_cell.reshape(1, n), land_cell.reshape(1, n), dest_rank.reshape(1, n),
         scalars=(block_count,),
     )
     to_left, to_right, meta = call(
         edges_body,
-        (sds((height + 32, 128), F32), sds((height + 32 + 3 * n, 128), F32), sds((n, 128), F32)),
-        level_set, velocity, below, above, meta, parts, weight,
-    )
+        (sds((height + 16, 128), F32), sds((height + 16 + 3 * n, 128), F32), sds((n, 128), F32)),
+        level_set, velocity, below, meta, parts, weight,
+    )
+    from_left = lax.ppermute(to_right, "gx", ring("gx", 1))
     from_right = lax.ppermute(to_left, "gx", ring("gx", -1))
-    from_left = lax.ppermute(to_right, "gx", ring("gx", 1))
     (packed,) = call(
         functools.partial(pack_body, height=height, across=across),
         (sds((bands * step, 128), F32),),
-        parts, weight, meta, to_left, from_left, from_right, select,
+        parts, weight, meta, to_left, from_left, from_right, select, fixed,
     )
     arrived = lax.all_to_all(
         packed.reshape(bands * step, 1, 128), "gy", split_axis=0, concat_axis=0, tiled=True
     ).reshape(bands * step, 128)
+    to_left2, to_right2 = call(corners_body, (sds((16, 128), F32), sds((16, 128), F32)), above)
+    from_left2 = lax.ppermute(to_right2, "gx", ring("gx", 1))
+    from_right2 = lax.ppermute(to_left2, "gx", ring("gx", -1))
     wide = pltpu.VMEM(((across // 128 + 1) * (height + 32), 128), F32)
     (section,) = call(
         stencil_body,
         (sds((height, across), F32),),
-        level_set, velocity, below, above, from_right, from_left,
+        level_set, velocity, below, above, from_right, from_left, from_right2, from_left2,
         scratch=[wide] * 5,
     )
     level, moved = call(

time: 60.3 us -> 74 us (1.23)
  the two profiles are of different devices: /device:TPU:31 before, /device:TPU:32 now
where the time goes in v3:
time: 74 us; the launch traced here: 73.6 us
  starting transfers between devices  34.7 us (47%)
  waiting for transfers between devices  22.3 us (30%)
  Pallas kernels  12.4 us (17%)
  local copies, waits for them, and re-layouts  2.83 us (4%)
  between operations  1.44 us (2%)
    ppermute x1, waiting for transfers between devices, shards(): above = lax.ppermute(tail, 'gy', ring('gy', 1))  15.8 us
    ppermute x1, starting transfers between devices, shards(): below = lax.ppermute(head, 'gy', ring('gy', -1))  12.7 us
    pallas_call x7, Pallas kernels, call(): pl.pallas_call(body, out_shape=tuple(outs), in_specs=[sm] * len(scalars)...  12.4 us
    all_to_all x1, starting transfers between devices, shards(): lax.all_to_all(packed.reshape(bands * step, 1, 128), 'gy', split_axis=0,...  5.86 us
    ppermute x1, starting transfers between devices, shards(): from_right2 = lax.ppermute(to_left2, 'gx', ring('gx', -1))  5.14 us
    ppermute x1, waiting for transfers between devices, shards(): from_left2 = lax.ppermute(to_right2, 'gx', ring('gx', 1))  4.82 us
    ppermute x1, starting transfers between devices, shards(): from_right = lax.ppermute(to_left, 'gx', ring('gx', -1))  4.47 us
    unnamed x18, local copies, waits for them, and re-layouts  2.83 us
  transfers between devices with their start and end apart: 7, of which 3 were waited for; matrix products, arithmetic and copies ran while one was open for 0% of the time, Pallas kernels for 11%

profile of v3, /device:TPU:32, one launch (start us, length us, event | category | flops | bytes accessed | tf_op | source)
XLA Modules:
  0.0 73.6 jit_solution(15906939441939225819)
XLA Ops:
  0.6 0.9 %copy-done = f32[2,64,512]{2,1,0:T(8,128)S(1)} copy-done((f32[2,64,512]{2,1,0:T(8,128)S(1)}, f32[2,64,512]{2,1,0:T(8,128)}, u32[]{:S(2)}) %copy-start) | copy-done | bytes 262168
  1.6 0.9 %copy-done.2 = f32[64,512]{1,0:T(8,128)S(1)} copy-done((f32[64,512]{1,0:T(8,128)S(1)}, f32[64,512]{1,0:T(8,128)}, u32[]{:S(2)}) %copy-start.2) | copy-done | bytes 131096
  2.5 12.7 %collective-permute-start = (f32[24,512]{1,0:T(8,128)S(1)}, f32[24,512]{1,0:T(8,128)S(1)}, u32[]{:S(2)}, u32[]{:S(2)}) collective-permute-start(f32[24,512]{1,0:T(8,128)S(1)} %get-tuple-element.16), channel_id=1, source_target_pairs={{0,504},{8,0},{16,8},{24,16},{32,24},{40,32},{48,40},{56,48},{64,5... | collective-permute-start | bytes 147464 | tf_op jit(solution)/shard_map/ppermute | solution.py:469
  15.9 0.0 copy-start.6
  15.9 0.0 copy-start.7
  15.9 0.6 copy-done.6
  16.5 0.0 copy-done.7
  16.6 0.0 copy-done.8
  16.6 0.6 shard_map.95
  17.1 0.3 copy-done.3
  17.5 0.3 shard_map.97
  17.7 2.6 %collective-permute-start.1 = (f32[272,128]{1,0:T(8,128)S(1)}, f32[272,128]{1,0:T(8,128)S(1)}, u32[]{:S(2)}, u32[]{:S(2)}) collective-permute-start(f32[272,128]{1,0:T(8,128)S(1)} %get-tuple-element.20), channel_id=1, source_target_pairs={{0,1},{1,2},{2,3},{3,4},{4,5},{5,6},{6,7},{7,0},{8,9},{9,10},{10,1... | collective-permute-start | bytes 417800 | tf_op jit(solution)/shard_map/ppermute | solution.py:488
  20.3 4.5 %collective-permute-start.2 = (f32[80,128]{1,0:T(8,128)S(1)}, f32[80,128]{1,0:T(8,128)S(1)}, u32[]{:S(2)}, u32[]{:S(2)}) collective-permute-start(f32[80,128]{1,0:T(8,128)S(1)} %get-tuple-element.19.mine_ref), channel_id=1, source_target_pairs={{0,7},{1,0},{2,1},{3,2},{4,3},{5,4},{6,5},{7,6},{8,15},{9,8},{10,9... | collective-permute-start | bytes 122888 | tf_op jit(solution)/shard_map/ppermute | solution.py:489
  24.8 1.7 %collective-permute-done.2.right_ref = f32[80,128]{1,0:T(8,128)S(1)} collective-permute-done((f32[80,128]{1,0:T(8,128)S(1)}, f32[80,128]{1,0:T(8,128)S(1)}, u32[]{:S(2)}, u32[]{:S(2)}) %collective-permute-start.2) | collective-permute-done | bytes 40992 | tf_op jit(solution)/shard_map/ppermute | solution.py:489
  26.5 1.9 %shard_map.98 = f32[1088,128]{1,0:T(8,128)} custom-call(f32[3,64,128]{2,1,0:T(8,128)S(1)} %bitcast.12, f32[64,128]{1,0:T(8,128)S(1)} %get-tuple-element.15.w_ref, f32[64,128]{1,0:T(8,128)S(1)} %get-tuple-element.18.meta_ref, f32[80,128]{1,0:T(8,128)S(1)} %get-tuple-element.19.mine_ref, f32[272,128]{1,0:T(8,128)S(1)} %collective-permute-done.1.left_ref, ...), custom_call_target="tpu_custom_call" | custom-call | tf_op jit(solution)/shard_map/pallas_call | solution.py:60
  28.4 5.9 %all-to-all-start = ((f32[1088,1,128]{2,1,0:T(1,128)}), f32[1088,1,128]{2,1,0:T(1,128)S(1)}, u32[]{:S(2)}, u32[]{:S(2)}) async-start(f32[1088,1,128]{2,1,0:T(1,128)} %bitcast.5), calls=%async_computation | async-start | bytes 1114112 | tf_op jit(solution)/shard_map/all_to_all | solution.py:495
  34.2 2.0 %collective-permute-start.3 = (f32[24,512]{1,0:T(8,128)S(1)}, f32[24,512]{1,0:T(8,128)S(1)}, u32[]{:S(2)}, u32[]{:S(2)}) collective-permute-start(f32[24,512]{1,0:T(8,128)S(1)} %get-tuple-element.23), channel_id=1, source_target_pairs={{0,8},{8,16},{16,24},{24,32},{32,40},{40,48},{48,56},{56,64},{64,7... | collective-permute-start | bytes 147464 | tf_op jit(solution)/shard_map/ppermute | solution.py:470
  36.2 15.8 %collective-permute-done.3.above_ref = f32[24,512]{1,0:T(8,128)S(1)} collective-permute-done((f32[24,512]{1,0:T(8,128)S(1)}, f32[24,512]{1,0:T(8,128)S(1)}, u32[]{:S(2)}, u32[]{:S(2)}) %collective-permute-start.3) | collective-permute-done | bytes 49184 | tf_op jit(solution)/shard_map/ppermute | solution.py:470
  52.0 0.1 shard_map.99
  52.1 5.1 %collective-permute-start.4 = (f32[16,128]{1,0:T(8,128)S(1)}, f32[16,128]{1,0:T(8,128)S(1)}, u32[]{:S(2)}, u32[]{:S(2)}) collective-permute-start(f32[16,128]{1,0:T(8,128)S(1)} %get-tuple-element.24), channel_id=1, source_target_pairs={{0,7},{1,0},{2,1},{3,2},{4,3},{5,4},{6,5},{7,6},{8,15},{9,8},{10,9... | collective-permute-start | bytes 24584 | tf_op jit(solution)/shard_map/ppermute | solution.py:500
  57.2 1.9 %collective-permute-start.5 = (f32[16,128]{1,0:T(8,128)S(1)}, f32[16,128]{1,0:T(8,128)S(1)}, u32[]{:S(2)}, u32[]{:S(2)}) collective-permute-start(f32[16,128]{1,0:T(8,128)S(1)} %get-tuple-element.25), channel_id=1, source_target_pairs={{0,1},{1,2},{2,3},{3,4},{4,5},{5,6},{6,7},{7,0},{8,9},{9,10},{10,1... | collective-permute-start | bytes 24584 | tf_op jit(solution)/shard_map/ppermute | solution.py:499
  59.2 4.8 %collective-permute-done.5.left2_ref = f32[16,128]{1,0:T(8,128)S(1)} collective-permute-done((f32[16,128]{1,0:T(8,128)S(1)}, f32[16,128]{1,0:T(8,128)S(1)}, u32[]{:S(2)}, u32[]{:S(2)}) %collective-permute-start.5) | collective-permute-done | bytes 8224 | tf_op jit(solution)/shard_map/ppermute | solution.py:499
  64.0 7.7 %shard_map.100.base_ref = f32[64,512]{1,0:T(8,128)S(1)} custom-call(f32[64,512]{1,0:T(8,128)S(1)} %copy-done.3, f32[2,64,512]{2,1,0:T(8,128)S(1)} %copy-done.1, f32[24,512]{1,0:T(8,128)S(1)} %collective-permute-done.below_ref, f32[24,512]{1,0:T(8,128)S(1)} %collective-permute-done.3.above_ref, f32[80,128]{1,0:T(8,128)S(1)} %collective-permute-done.2.right_ref, ...), custom_call_target="tpu_custom_call" | custom-call | tf_op jit(solution)/shard_map/pallas_call | solution.py:60
  71.7 1.9 %shard_map.101 = (f32[64,512]{1,0:T(8,128)}, f32[1024,128]{1,0:T(8,128)}) custom-call(f32[1088,128]{1,0:T(8,128)S(1)} %bitcast.9, f32[64,512]{1,0:T(8,128)S(1)} %shard_map.100.base_ref), custom_call_target="tpu_custom_call" | custom-call | tf_op jit(solution)/shard_map/pallas_call | solution.py:60
  (15 shorter events, 0.0 us)
Async XLA Ops:
  0.6 1.0 %copy-start = (f32[2,64,512]{2,1,0:T(8,128)S(1)}, f32[2,64,512]{2,1,0:T(8,128)}, u32[]{:S(2)}) copy-start(f32[2,64,512]{2,1,0:T(8,128)} %flow_ref.7) | copy-start | bytes 786436
  1.6 0.9 %copy-start.2 = (f32[64,512]{1,0:T(8,128)S(1)}, f32[64,512]{1,0:T(8,128)}, u32[]{:S(2)}) copy-start(f32[64,512]{1,0:T(8,128)} %f_ref.5) | copy-start | bytes 393220
  2.5 13.4 %copy-start.4 = (f32[64,3,128]{2,0,1:T(8,128)S(1)}, f32[64,3,128]{2,0,1:T(8,128)}, u32[]{:S(2)}) copy-start(f32[64,3,128]{2,0,1:T(8,128)} %param.10) | copy-start | bytes 294916
  2.5 13.4 %copy-start.5 = (s32[64,128]{1,0:T(8,128)S(1)}, s32[64,128]{1,0:T(8,128)}, u32[]{:S(2)}) copy-start(s32[64,128]{1,0:T(8,128)} %esc_ref.1) | copy-start | bytes 98308
  2.5 14.6 %collective-permute-start = (f32[24,512]{1,0:T(8,128)S(1)}, f32[24,512]{1,0:T(8,128)S(1)}, u32[]{:S(2)}, u32[]{:S(2)}) collective-permute-start(f32[24,512]{1,0:T(8,128)S(1)} %get-tuple-element.16), channel_id=1, source_target_pairs={{0,504},{8,0},{16,8},{24,16},{32,24},{40,32},{48,40},{56,48},{64,5... | collective-permute-start | bytes 147464 | tf_op jit(solution)/shard_map/ppermute | solution.py:469
  15.9 0.7 copy-start.6
  15.9 0.7 copy-start.7
  15.9 0.7 copy-start.8
  16.6 0.9 %copy-start.3 = (f32[64,512]{1,0:T(8,128)S(1)}, f32[64,512]{1,0:T(8,128)}, u32[]{:S(2)}) copy-start(f32[64,512]{1,0:T(8,128)} %f_ref.5) | copy-start | bytes 393220
  17.7 8.7 %collective-permute-start.1 = (f32[272,128]{1,0:T(8,128)S(1)}, f32[272,128]{1,0:T(8,128)S(1)}, u32[]{:S(2)}, u32[]{:S(2)}) collective-permute-start(f32[272,128]{1,0:T(8,128)S(1)} %get-tuple-element.20), channel_id=1, source_target_pairs={{0,1},{1,2},{2,3},{3,4},{4,5},{5,6},{6,7},{7,0},{8,9},{9,10},{10,1... | collective-permute-start | bytes 417800 | tf_op jit(solution)/shard_map/ppermute | solution.py:488
  20.3 6.1 %collective-permute-start.2 = (f32[80,128]{1,0:T(8,128)S(1)}, f32[80,128]{1,0:T(8,128)S(1)}, u32[]{:S(2)}, u32[]{:S(2)}) collective-permute-start(f32[80,128]{1,0:T(8,128)S(1)} %get-tuple-element.19.mine_ref), channel_id=1, source_target_pairs={{0,7},{1,0},{2,1},{3,2},{4,3},{5,4},{6,5},{7,6},{8,15},{9,8},{10,9... | collective-permute-start | bytes 122888 | tf_op jit(solution)/shard_map/ppermute | solution.py:489
  28.4 35.6 %copy-start.1 = (f32[2,64,512]{2,1,0:T(8,128)S(1)}, f32[2,64,512]{2,1,0:T(8,128)}, u32[]{:S(2)}) copy-start(f32[2,64,512]{2,1,0:T(8,128)} %flow_ref.7) | copy-start | bytes 786436
  28.4 43.3 %all-to-all-start = ((f32[1088,1,128]{2,1,0:T(1,128)}), f32[1088,1,128]{2,1,0:T(1,128)S(1)}, u32[]{:S(2)}, u32[]{:S(2)}) async-start(f32[1088,1,128]{2,1,0:T(1,128)} %bitcast.5), calls=%async_computation | async-start | bytes 1114112 | tf_op jit(solution)/shard_map/all_to_all | solution.py:495
  34.2 17.8 %collective-permute-start.3 = (f32[24,512]{1,0:T(8,128)S(1)}, f32[24,512]{1,0:T(8,128)S(1)}, u32[]{:S(2)}, u32[]{:S(2)}) collective-permute-start(f32[24,512]{1,0:T(8,128)S(1)} %get-tuple-element.23), channel_id=1, source_target_pairs={{0,8},{8,16},{16,24},{24,32},{32,40},{40,48},{48,56},{56,64},{64,7... | collective-permute-start | bytes 147464 | tf_op jit(solution)/shard_map/ppermute | solution.py:470
  52.1 7.1 %collective-permute-start.4 = (f32[16,128]{1,0:T(8,128)S(1)}, f32[16,128]{1,0:T(8,128)S(1)}, u32[]{:S(2)}, u32[]{:S(2)}) collective-permute-start(f32[16,128]{1,0:T(8,128)S(1)} %get-tuple-element.24), channel_id=1, source_target_pairs={{0,7},{1,0},{2,1},{3,2},{4,3},{5,4},{6,5},{7,6},{8,15},{9,8},{10,9... | collective-permute-start | bytes 24584 | tf_op jit(solution)/shard_map/ppermute | solution.py:500
  57.2 6.8 %collective-permute-start.5 = (f32[16,128]{1,0:T(8,128)S(1)}, f32[16,128]{1,0:T(8,128)S(1)}, u32[]{:S(2)}, u32[]{:S(2)}) collective-permute-start(f32[16,128]{1,0:T(8,128)S(1)} %get-tuple-element.25), channel_id=1, source_target_pairs={{0,1},{1,2},{2,3},{3,4},{4,5},{5,6},{6,7},{7,0},{8,9},{9,10},{10,1... | collective-permute-start | bytes 24584 | tf_op jit(solution)/shard_map/ppermute | solution.py:499

commit v4 on v3

--- a/solution.py
+++ b/solution.py
@@ -54,26 +54,36 @@
     return jnp.floor((x + 0.5) * (1.0 / k))
 
 
-def call(body, outs, *args, scratch=(), scalars=()):
-    vm = pl.BlockSpec(memory_space=pltpu.VMEM)
-    sm = pl.BlockSpec(memory_space=pltpu.SMEM)
+def call(body, outs, *args, scratch=(), spaces=None, out_spaces=None, scalars=()):
+    vm, sm = pltpu.VMEM, pltpu.SMEM
+    spaces = spaces or [vm] * len(args)
+    out_spaces = out_spaces or [vm] * len(outs)
+    spec = lambda space: pl.BlockSpec(memory_space=space)
     return pl.pallas_call(
         body,
         out_shape=tuple(outs),
-        in_specs=[sm] * len(scalars) + [vm] * len(args),
-        out_specs=tuple(vm for _ in outs),
+        in_specs=[spec(sm)] * len(scalars) + [spec(x) for x in spaces],
+        out_specs=tuple(spec(x) for x in out_spaces),
         scratch_shapes=list(scratch),
         compiler_params=pltpu.CompilerParams(vmem_limit_bytes=16 * 1024 * 1024),
         interpret=INTERPRET,
     )(*scalars, *args)
 
 
-def heads_body(f_ref, flow_ref, head_ref, tail_ref):
+def heads_body(f_ref, flow_ref, head_ref, tail_ref, f_rows, flow_rows, sems):
     height = f_ref.shape[0]
-    for ref, f0, v0 in ((head_ref, 0, 0), (tail_ref, height - 9, height - 6)):
-        ref[0:9] = f_ref[f0 : f0 + 9]
-        ref[9:15] = flow_ref[0, v0 : v0 + 6]
-        ref[15:21] = flow_ref[1, v0 : v0 + 6]
+    copies = []
+    for i, (f_top, flow_top) in enumerate(((0, 0), (height - 16, height - 8))):
+        copies.append(pltpu.make_async_copy(f_ref.at[pl.ds(f_top, 16)], f_rows.at[i], sems.at[2 * i]))
+        copies.append(pltpu.make_async_copy(flow_ref.at[:, pl.ds(flow_top, 8)], flow_rows.at[i], sems.at[2 * i + 1]))
+    for copy in copies:
+        copy.start()
+    for copy in copies:
+        copy.wait()
+    for i, (ref, f0, v0) in enumerate(((head_ref, 0, 0), (tail_ref, 7, 2))):
+        ref[0:9] = f_rows[i, f0 : f0 + 9]
+        ref[9:15] = flow_rows[i, 0, v0 : v0 + 6]
+        ref[15:21] = flow_rows[i, 1, v0 : v0 + 6]
         ref[21:24] = jnp.zeros((3, f_ref.shape[1]), F32)
 
 
@@ -322,35 +332,22 @@
     lane = lax.broadcasted_iota(jnp.int32, (8, 128), 1)
 
     def stage(src, dst_tiles, base, write):
-        rolled = {}
-
-        def shifted(tag, tiles_in, k):
-            key = (tag, k)
-            if key not in rolled:
-                turned = [pltpu.roll(t, (-k) % 128, 1) for t in tiles_in]
-                out = []
-                for j in range(tiles):
-                    if k > 0:
-                        out.append(jnp.where(lane < 128 - k, turned[j], turned[(j + 1) % tiles]))
-                    else:
-                        out.append(jnp.where(lane >= -k, turned[j], turned[(j - 1) % tiles]))
-                rolled[key] = out
-            return rolled[key]
-
         f = [src[pl.ds(span * j + base, 8), :] for j in range(tiles)]
-        nxt = shifted("f", f, 1)
-        d3 = [nxt[j] - f[j] for j in range(tiles)]
-        d2 = shifted("d", d3, -1)
-        e2 = [d2[j] - d3[j] for j in range(tiles)]
-        e0 = shifted("e", e2, -2)
-        e1 = shifted("e", e2, -1)
-        e3 = shifted("e", e2, 1)
-        e4 = shifted("e", e2, 2)
+
+        def shifted(k):
+            turned = [pltpu.roll(t, (-k) % 128, 1) for t in f]
+            if k > 0:
+                return [jnp.where(lane < 128 - k, turned[j], turned[(j + 1) % tiles]) for j in range(dst_tiles)]
+            return [jnp.where(lane >= -k, turned[j], turned[(j - 1) % tiles]) for j in range(dst_tiles)]
+
+        near = {k: f if k == 0 else shifted(k) for k in range(-3, 4)}
         for j in range(dst_tiles):
             at = span * j + base
             u = us[pl.ds(at, 8), :]
             v = vs[pl.ds(at, 8), :]
-            x_term = side_term(u, e0[j], e1[j], e2[j], e3[j], e4[j], d2[j], d3[j])
+            d = [near[k + 1][j] - near[k][j] for k in range(-3, 3)]
+            e = [d[k] - d[k + 1] for k in range(5)]
+            x_term = side_term(u, e[0], e[1], e[2], e[3], e[4], d[2], d[3])
             rows = [f[j] if k == 0 else src[pl.ds(at + k, 8), :] for k in range(-3, 4)]
             d = [rows[k + 1] - rows[k] for k in range(6)]
             e = [d[k] - d[k + 1] for k in range(5)]
@@ -387,18 +384,18 @@
         stage(f2, tiles - 1, base, write)
         return carry
 
-    lax.fori_loop(0, height // 8 + 2, first, 0)
-    lax.fori_loop(0, height // 8 + 2, second, 0)
-    lax.fori_loop(0, height // 8, third, 0)
-
-
-def deposit_body(recv_ref, base_ref, out_ref, moved_ref):
+    lax.fori_loop(0, height // 8 + 2, first, 0, unroll=2)
+    lax.fori_loop(0, height // 8 + 2, second, 0, unroll=2)
+    lax.fori_loop(0, height // 8, third, 0, unroll=2)
+
+
+def deposit_body(rows_ref, recv_ref, base_ref, out_ref, moved_ref, sem):
     height, across = base_ref.shape
     step = 4 * CAP + 1
     bands = recv_ref.shape[0] // step
     block = 4 * CAP
-    for g in range(bands):
-        moved_ref[block * g : block * g + block] = recv_ref[step * g : step * g + block]
+    copy = pltpu.make_async_copy(rows_ref.at[:, pl.ds(0, block)], moved_ref, sem)
+    copy.start()
     table = recv_ref[pl.ds(block, bands, stride=step), :]
     lanes = iota((bands, across), 1)
     lane = iota((bands, 128), 1)
@@ -452,6 +449,7 @@
     down = jnp.where(r == 0.0, incoming, down)
     column = side[:, 0:1] + jnp.where(iota((height, 1), 0) == 0.0, 0.0, side_down[:, 1:2])
     out_ref[...] = base_ref[...] + (same + down + jnp.where(c == 0.0, column, 0.0))
+    copy.wait()
 
 
 def ring(axis, distance):
@@ -465,7 +463,14 @@
     bands = lax.axis_size("gy")
     step = 4 * CAP + 1
     sds = jax.ShapeDtypeStruct
-    head, tail = call(heads_body, (sds((24, across), F32), sds((24, across), F32)), level_set, velocity)
+    head, tail = call(
+        heads_body,
+        (sds((24, across), F32), sds((24, across), F32)),
+        pltpu.with_memory_space_constraint(level_set, pltpu.HBM),
+        pltpu.with_memory_space_constraint(velocity, pltpu.HBM),
+        spaces=[pltpu.HBM, pltpu.HBM],
+        scratch=[pltpu.VMEM((2, 16, across), F32), pltpu.VMEM((2, 2, 8, across), F32), pltpu.SemaphoreType.DMA((4,))],
+    )
     below = lax.ppermute(head, "gy", ring("gy", -1))
     above = lax.ppermute(tail, "gy", ring("gy", 1))
     parts = jnp.transpose(particles, (1, 0, 2))
@@ -494,7 +499,7 @@
     )
     arrived = lax.all_to_all(
         packed.reshape(bands * step, 1, 128), "gy", split_axis=0, concat_axis=0, tiled=True
-    ).reshape(bands * step, 128)
+    )
     to_left2, to_right2 = call(corners_body, (sds((16, 128), F32), sds((16, 128), F32)), above)
     from_left2 = lax.ppermute(to_right2, "gx", ring("gx", 1))
     from_right2 = lax.ppermute(to_left2, "gx", ring("gx", -1))
@@ -507,8 +512,10 @@
     )
     level, moved = call(
         deposit_body,
-        (sds((height, across), F32), sds((bands * CAP * 4, 128), F32)),
-        arrived, section,
+        (sds((height, across), F32), sds((bands, 4 * CAP, 1, 128), F32)),
+        arrived.reshape(bands, step, 1, 128), arrived.reshape(bands * step, 128), section,
+        out_spaces=[pltpu.VMEM, pltpu.HBM],
+        scratch=[pltpu.SemaphoreType.DMA],
     )
     return level, moved.reshape(bands * CAP, 4, 128)
 

time: 74 us -> 68.4 us (0.924)
  Pallas kernels: 12.4 us -> 8.92 us
  local copies, waits for them, and re-layouts: 2.83 us -> 0.98 us
    pallas_call x7, Pallas kernels: 12.4 us -> 8.92 us  [call(): pl.pallas_call(body, out_shape=tuple(outs), in_specs=[spec(sm)] * len(sca...]
    unnamed x18 -> x14, local copies, waits for them, and re-layouts: 2.83 us -> 0.98 us
  transfers between devices with their start and end apart: 7 -> 7, of which waited for: 3 -> 3; matrix products, arithmetic and copies ran while one was open for 0% -> 0% of each run, Pallas kernels for 11% -> 6%
where the time goes in v4:
time: 68.4 us; the launch traced here: 68 us
  starting transfers between devices  34.4 us (50%)
  waiting for transfers between devices  22.3 us (33%)
  Pallas kernels  8.92 us (13%)
  between operations  1.46 us (2%)
  local copies, waits for them, and re-layouts  0.98 us (1%)
    ppermute x1, waiting for transfers between devices, shards(): above = lax.ppermute(tail, 'gy', ring('gy', 1))  15.8 us
    ppermute x1, starting transfers between devices, shards(): below = lax.ppermute(head, 'gy', ring('gy', -1))  12.6 us
    pallas_call x7, Pallas kernels, call(): pl.pallas_call(body, out_shape=tuple(outs), in_specs=[spec(sm)] * len(sca...  8.92 us
    all_to_all x1, starting transfers between devices, shards(): lax.all_to_all(packed.reshape(bands * step, 1, 128), 'gy', split_axis=0,...  5.73 us
    ppermute x1, starting transfers between devices, shards(): from_right2 = lax.ppermute(to_left2, 'gx', ring('gx', -1))  5.15 us
    ppermute x1, waiting for transfers between devices, shards(): from_left2 = lax.ppermute(to_right2, 'gx', ring('gx', 1))  4.82 us
    ppermute x1, starting transfers between devices, shards(): from_right = lax.ppermute(to_left, 'gx', ring('gx', -1))  4.47 us
    ppermute x1, starting transfers between devices, shards(): from_left = lax.ppermute(to_right, 'gx', ring('gx', 1))  2.59 us
  transfers between devices with their start and end apart: 7, of which 3 were waited for; matrix products, arithmetic and copies ran while one was open for 0% of the time, Pallas kernels for 6%

profile of v4, /device:TPU:32, one launch (start us, length us, event | category | flops | bytes accessed | tf_op | source)
XLA Modules:
  0.0 68.0 jit_solution(41174358256311920)
XLA Ops:
  0.7 0.9 %shard_map.96 = (f32[24,512]{1,0:T(8,128)S(1)}, f32[24,512]{1,0:T(8,128)S(1)}) custom-call(f32[64,512]{1,0:T(8,128)} %f_ref.5, f32[2,64,512]{2,1,0:T(8,128)} %flow_ref.7), custom_call_target="tpu_custom_call" | custom-call | tf_op jit(solution)/shard_map/pallas_call | solution.py:62
  1.6 12.6 %collective-permute-start = (f32[24,512]{1,0:T(8,128)S(1)}, f32[24,512]{1,0:T(8,128)S(1)}, u32[]{:S(2)}, u32[]{:S(2)}) collective-permute-start(f32[24,512]{1,0:T(8,128)S(1)} %get-tuple-element.16), channel_id=1, source_target_pairs={{0,504},{8,0},{16,8},{24,16},{32,24},{40,32},{48,40},{56,48},{64,5... | collective-permute-start | bytes 147464 | tf_op jit(solution)/shard_map/ppermute | solution.py:474
  14.8 0.0 copy-start.4
  14.8 0.0 copy-start.5
  14.8 0.0 copy-start.6
  14.9 0.6 copy-done.4
  15.5 0.0 copy-done.5
  15.5 0.0 copy-done.6
  15.5 0.6 shard_map.95
  16.1 0.3 copy-done.1
  16.4 0.3 shard_map.97
  16.7 2.6 %collective-permute-start.1 = (f32[272,128]{1,0:T(8,128)S(1)}, f32[272,128]{1,0:T(8,128)S(1)}, u32[]{:S(2)}, u32[]{:S(2)}) collective-permute-start(f32[272,128]{1,0:T(8,128)S(1)} %get-tuple-element.20), channel_id=1, source_target_pairs={{0,1},{1,2},{2,3},{3,4},{4,5},{5,6},{6,7},{7,0},{8,9},{9,10},{10,1... | collective-permute-start | bytes 417800 | tf_op jit(solution)/shard_map/ppermute | solution.py:493
  19.3 4.5 %collective-permute-start.2 = (f32[80,128]{1,0:T(8,128)S(1)}, f32[80,128]{1,0:T(8,128)S(1)}, u32[]{:S(2)}, u32[]{:S(2)}) collective-permute-start(f32[80,128]{1,0:T(8,128)S(1)} %get-tuple-element.19.mine_ref), channel_id=1, source_target_pairs={{0,7},{1,0},{2,1},{3,2},{4,3},{5,4},{6,5},{7,6},{8,15},{9,8},{10,9... | collective-permute-start | bytes 122888 | tf_op jit(solution)/shard_map/ppermute | solution.py:494
  23.7 1.7 %collective-permute-done.2.right_ref = f32[80,128]{1,0:T(8,128)S(1)} collective-permute-done((f32[80,128]{1,0:T(8,128)S(1)}, f32[80,128]{1,0:T(8,128)S(1)}, u32[]{:S(2)}, u32[]{:S(2)}) %collective-permute-start.2) | collective-permute-done | bytes 40992 | tf_op jit(solution)/shard_map/ppermute | solution.py:494
  25.4 1.9 %shard_map.98 = f32[1088,128]{1,0:T(8,128)} custom-call(f32[3,64,128]{2,1,0:T(8,128)S(1)} %bitcast.14, f32[64,128]{1,0:T(8,128)S(1)} %get-tuple-element.15.w_ref, f32[64,128]{1,0:T(8,128)S(1)} %get-tuple-element.18.meta_ref, f32[80,128]{1,0:T(8,128)S(1)} %get-tuple-element.19.mine_ref, f32[272,128]{1,0:T(8,128)S(1)} %collective-permute-done.1.left_ref, ...), custom_call_target="tpu_custom_call" | custom-call | tf_op jit(solution)/shard_map/pallas_call | solution.py:62
  27.3 5.7 %all-to-all-start = ((f32[1088,1,128]{2,1,0:T(1,128)}), f32[1088,1,128]{2,1,0:T(1,128)S(1)}, u32[]{:S(2)}, u32[]{:S(2)}) async-start(f32[1088,1,128]{2,1,0:T(1,128)} %bitcast.5), calls=%async_computation | async-start | bytes 1114112 | tf_op jit(solution)/shard_map/all_to_all | solution.py:500
  33.0 2.0 %collective-permute-start.3 = (f32[24,512]{1,0:T(8,128)S(1)}, f32[24,512]{1,0:T(8,128)S(1)}, u32[]{:S(2)}, u32[]{:S(2)}) collective-permute-start(f32[24,512]{1,0:T(8,128)S(1)} %get-tuple-element.23), channel_id=1, source_target_pairs={{0,8},{8,16},{16,24},{24,32},{32,40},{40,48},{48,56},{56,64},{64,7... | collective-permute-start | bytes 147464 | tf_op jit(solution)/shard_map/ppermute | solution.py:475
  35.0 15.8 %collective-permute-done.3.above_ref = f32[24,512]{1,0:T(8,128)S(1)} collective-permute-done((f32[24,512]{1,0:T(8,128)S(1)}, f32[24,512]{1,0:T(8,128)S(1)}, u32[]{:S(2)}, u32[]{:S(2)}) %collective-permute-start.3) | collective-permute-done | bytes 49184 | tf_op jit(solution)/shard_map/ppermute | solution.py:475
  50.8 0.1 shard_map.99
  50.9 5.1 %collective-permute-start.4 = (f32[16,128]{1,0:T(8,128)S(1)}, f32[16,128]{1,0:T(8,128)S(1)}, u32[]{:S(2)}, u32[]{:S(2)}) collective-permute-start(f32[16,128]{1,0:T(8,128)S(1)} %get-tuple-element.24), channel_id=1, source_target_pairs={{0,7},{1,0},{2,1},{3,2},{4,3},{5,4},{6,5},{7,6},{8,15},{9,8},{10,9... | collective-permute-start | bytes 24584 | tf_op jit(solution)/shard_map/ppermute | solution.py:505
  56.0 1.9 %collective-permute-start.5 = (f32[16,128]{1,0:T(8,128)S(1)}, f32[16,128]{1,0:T(8,128)S(1)}, u32[]{:S(2)}, u32[]{:S(2)}) collective-permute-start(f32[16,128]{1,0:T(8,128)S(1)} %get-tuple-element.25), channel_id=1, source_target_pairs={{0,1},{1,2},{2,3},{3,4},{4,5},{5,6},{6,7},{7,0},{8,9},{9,10},{10,1... | collective-permute-start | bytes 24584 | tf_op jit(solution)/shard_map/ppermute | solution.py:504
  58.0 4.8 %collective-permute-done.5.left2_ref = f32[16,128]{1,0:T(8,128)S(1)} collective-permute-done((f32[16,128]{1,0:T(8,128)S(1)}, f32[16,128]{1,0:T(8,128)S(1)}, u32[]{:S(2)}, u32[]{:S(2)}) %collective-permute-start.5) | collective-permute-done | bytes 8224 | tf_op jit(solution)/shard_map/ppermute | solution.py:504
  62.8 3.4 %shard_map.100.base_ref = f32[64,512]{1,0:T(8,128)S(1)} custom-call(f32[64,512]{1,0:T(8,128)S(1)} %copy-done.1, f32[2,64,512]{2,1,0:T(8,128)S(1)} %copy-done, f32[24,512]{1,0:T(8,128)S(1)} %collective-permute-done.below_ref, f32[24,512]{1,0:T(8,128)S(1)} %collective-permute-done.3.above_ref, f32[80,128]{1,0:T(8,128)S(1)} %collective-permute-done.2.right_ref, ...), custom_call_target="tpu_custom_call" | custom-call | tf_op jit(solution)/shard_map/pallas_call | solution.py:62
  66.2 1.8 %shard_map.101 = (f32[64,512]{1,0:T(8,128)}, f32[64,16,1,128]{3,2,1,0:T(1,128)}) custom-call(f32[64,17,1,128]{3,2,1,0:T(1,128)S(1)} %bitcast.10, f32[1088,128]{1,0:T(8,128)S(1)} %bitcast.11, f32[64,512]{1,0:T(8,128)S(1)} %shard_map.100.base_ref), custom_call_target="tpu_custom_call" | custom-call | tf_op jit(solution)/shard_map/pallas_call | solution.py:62
  (11 shorter events, 0.0 us)
Async XLA Ops:
  0.6 14.2 %copy-start = (f32[2,64,512]{2,1,0:T(8,128)S(1)}, f32[2,64,512]{2,1,0:T(8,128)}, u32[]{:S(2)}) copy-start(f32[2,64,512]{2,1,0:T(8,128)} %flow_ref.7) | copy-start | bytes 786436
  0.6 14.2 %copy-start.2 = (f32[64,3,128]{2,0,1:T(8,128)S(1)}, f32[64,3,128]{2,0,1:T(8,128)}, u32[]{:S(2)}) copy-start(f32[64,3,128]{2,0,1:T(8,128)} %param.10) | copy-start | bytes 294916
  0.7 14.2 %copy-start.3 = (s32[64,128]{1,0:T(8,128)S(1)}, s32[64,128]{1,0:T(8,128)}, u32[]{:S(2)}) copy-start(s32[64,128]{1,0:T(8,128)} %esc_ref.1) | copy-start | bytes 98308
  1.6 14.5 %collective-permute-start = (f32[24,512]{1,0:T(8,128)S(1)}, f32[24,512]{1,0:T(8,128)S(1)}, u32[]{:S(2)}, u32[]{:S(2)}) collective-permute-start(f32[24,512]{1,0:T(8,128)S(1)} %get-tuple-element.16), channel_id=1, source_target_pairs={{0,504},{8,0},{16,8},{24,16},{32,24},{40,32},{48,40},{56,48},{64,5... | collective-permute-start | bytes 147464 | tf_op jit(solution)/shard_map/ppermute | solution.py:474
  14.8 0.7 copy-start.4
  14.8 0.7 copy-start.5
  14.8 0.7 copy-start.6
  15.5 0.9 %copy-start.1 = (f32[64,512]{1,0:T(8,128)S(1)}, f32[64,512]{1,0:T(8,128)}, u32[]{:S(2)}) copy-start(f32[64,512]{1,0:T(8,128)} %f_ref.5) | copy-start | bytes 393220
  16.7 8.7 %collective-permute-start.1 = (f32[272,128]{1,0:T(8,128)S(1)}, f32[272,128]{1,0:T(8,128)S(1)}, u32[]{:S(2)}, u32[]{:S(2)}) collective-permute-start(f32[272,128]{1,0:T(8,128)S(1)} %get-tuple-element.20), channel_id=1, source_target_pairs={{0,1},{1,2},{2,3},{3,4},{4,5},{5,6},{6,7},{7,0},{8,9},{9,10},{10,1... | collective-permute-start | bytes 417800 | tf_op jit(solution)/shard_map/ppermute | solution.py:493
  19.3 6.1 %collective-permute-start.2 = (f32[80,128]{1,0:T(8,128)S(1)}, f32[80,128]{1,0:T(8,128)S(1)}, u32[]{:S(2)}, u32[]{:S(2)}) collective-permute-start(f32[80,128]{1,0:T(8,128)S(1)} %get-tuple-element.19.mine_ref), channel_id=1, source_target_pairs={{0,7},{1,0},{2,1},{3,2},{4,3},{5,4},{6,5},{7,6},{8,15},{9,8},{10,9... | collective-permute-start | bytes 122888 | tf_op jit(solution)/shard_map/ppermute | solution.py:494
  27.3 38.9 %all-to-all-start = ((f32[1088,1,128]{2,1,0:T(1,128)}), f32[1088,1,128]{2,1,0:T(1,128)S(1)}, u32[]{:S(2)}, u32[]{:S(2)}) async-start(f32[1088,1,128]{2,1,0:T(1,128)} %bitcast.5), calls=%async_computation | async-start | bytes 1114112 | tf_op jit(solution)/shard_map/all_to_all | solution.py:500
  33.0 17.8 %collective-permute-start.3 = (f32[24,512]{1,0:T(8,128)S(1)}, f32[24,512]{1,0:T(8,128)S(1)}, u32[]{:S(2)}, u32[]{:S(2)}) collective-permute-start(f32[24,512]{1,0:T(8,128)S(1)} %get-tuple-element.23), channel_id=1, source_target_pairs={{0,8},{8,16},{16,24},{24,32},{32,40},{40,48},{48,56},{56,64},{64,7... | collective-permute-start | bytes 147464 | tf_op jit(solution)/shard_map/ppermute | solution.py:475
  50.9 7.1 %collective-permute-start.4 = (f32[16,128]{1,0:T(8,128)S(1)}, f32[16,128]{1,0:T(8,128)S(1)}, u32[]{:S(2)}, u32[]{:S(2)}) collective-permute-start(f32[16,128]{1,0:T(8,128)S(1)} %get-tuple-element.24), channel_id=1, source_target_pairs={{0,7},{1,0},{2,1},{3,2},{4,3},{5,4},{6,5},{7,6},{8,15},{9,8},{10,9... | collective-permute-start | bytes 24584 | tf_op jit(solution)/shard_map/ppermute | solution.py:505
  56.0 6.8 %collective-permute-start.5 = (f32[16,128]{1,0:T(8,128)S(1)}, f32[16,128]{1,0:T(8,128)S(1)}, u32[]{:S(2)}, u32[]{:S(2)}) collective-permute-start(f32[16,128]{1,0:T(8,128)S(1)} %get-tuple-element.25), channel_id=1, source_target_pairs={{0,1},{1,2},{2,3},{3,4},{4,5},{5,6},{6,7},{7,0},{8,9},{9,10},{10,1... | collective-permute-start | bytes 24584 | tf_op jit(solution)/shard_map/ppermute | solution.py:504

commit v5 on v4

--- a/solution.py
+++ b/solution.py
@@ -29,9 +29,13 @@
     return lax.dot_general(a, b, (((1,), (0,)), ((), ())), preferred_element_type=F32)
 
 
-def exact_pick(one_hot, x):
-    hi, mid, lo = split3(x)
-    return (mm(one_hot, hi) + mm(one_hot, mid)) + mm(one_hot, lo)
+def stack3(x):
+    return jnp.concatenate(split3(x), axis=0)
+
+
+def phase(shape, period):
+    lane = iota(shape, 1)
+    return lane - period * floor_div(lane, period)
 
 
 def eye(n):
@@ -106,14 +110,14 @@
     live_row = iota((1, n), 1) < count
     slot_row = jnp.where(live_row, dest_row * CAP + rank_row, -1.0)
     slot = to_column(slot_row, n)
-    lane = iota((n, height), 1)
+    lane = phase((n, 3 * height), height)
     pick = jnp.concatenate([one_hot(lane == row), one_hot(lane == row + 1.0)], axis=0)
     lanes = iota((n, across), 1)
     at0 = lanes == col
     at1 = lanes == col + 1.0
     parts = []
     for component in range(2):
-        both = exact_pick(pick, flow_ref[component])
+        both = mm(pick, stack3(flow_ref[component]))
         low = both[0:n]
         high = both[n:]
         for where_at in (at0, at1):
@@ -131,9 +135,9 @@
     bands = slots // CAP
     r = iota((slots, 1), 0)
     k = floor_div(r, bands)
-    choose = one_hot((r - k * bands) * CAP + k == slot_row)
+    choose = one_hot((r - k * bands) * CAP + k == jnp.concatenate([slot_row] * 3, axis=1))
     sel_ref[...] = choose
-    rw_ref[...] = exact_pick(choose, jnp.concatenate([part_ref[2], w], axis=1))
+    rw_ref[...] = mm(choose, stack3(jnp.concatenate([part_ref[2], w], axis=1)))
 
 
 def pack_left(f, u, v):
@@ -144,7 +148,7 @@
 def pack_right(f, u, v, m):
     lane = iota(f.shape, 1)
     out = jnp.where(lane >= 112.0, f, jnp.where(lane >= 96.0, pltpu.roll(u, 112, 1), pltpu.roll(v, 96, 1)))
-    return jnp.where(lane < 16.0, m, out)
+    return jnp.where(lane < 32.0, m, out)
 
 
 def corners_body(above_ref, left_ref, right_ref):
@@ -174,12 +178,28 @@
         c11 = jnp.sum(jnp.where(at1, line, 0.0), axis=1, keepdims=True)
         meta = meta + jnp.where(lane == float(base + 1), c10, 0.0) + jnp.where(lane == float(base + 3), c11, 0.0)
     meta2_ref[...] = meta
+    x = part_ref[0]
+    y = part_ref[1]
+    w = w_ref[...]
+    fy = y + 0.5
+    fx = x + 0.5
+    near0 = (1.0 - fy) * (1.0 - fx)
+    near1 = fy * (1.0 - fx)
+    gx = fx + DT * (near0 * meta[:, 0:1] + near1 * meta[:, 1:2])
+    gy = fy + DT * (near0 * meta[:, 4:5] + near1 * meta[:, 5:6])
+    e1 = DT * ((1.0 - fy) * fx)
+    e2 = DT * (fy * fx)
+    wgx, wgy, w1, w2 = w * gx, w * gy, w * e1, w * e2
+    moments = [wgx, w1, w2, wgx * gy, wgy * e1, wgy * e2, wgx * e1, wgx * e2, w1 * e1, w1 * e2, w2 * e2]
+    sent = meta
+    for i, value in enumerate(moments):
+        sent = jnp.where(lane == float(16 + i), lane_sum(value), sent)
     far = across - 128
 
     zero = jnp.zeros((8, 128), F32)
 
     def pieces(sl):
-        yield 0, height, f_ref[:, sl], flow_ref[0, :, sl], flow_ref[1, :, sl], meta
+        yield 0, height, f_ref[:, sl], flow_ref[0, :, sl], flow_ref[1, :, sl], sent
         yield height, 8, below_ref[0:8, sl], below_ref[9:17, sl], below_ref[15:23, sl], zero
         yield height + 8, 8, below_ref[8:16, sl], zero, zero, zero
 
@@ -187,10 +207,6 @@
         left_ref[top : top + rows] = pack_left(f, u, v)
     for top, rows, f, u, v, m in pieces(slice(far, across)):
         right_ref[top : top + rows] = pack_right(f, u, v, m)
-    top = height + 16
-    right_ref[top : top + n] = part_ref[0]
-    right_ref[top + n : top + 2 * n] = part_ref[1]
-    right_ref[top + 2 * n : top + 3 * n] = w_ref[...]
 
 
 def halo_tiles(from_right, from_left):
@@ -202,17 +218,7 @@
     return f, u, v
 
 
-def moved_particles(meta, x, y, column, across):
-    n = x.shape[0]
-    row = meta[:, 8:9]
-    last = meta[:, 9:10] == float(across - 1)
-    lane = iota((n, column.shape[0]), 1)
-    pick = jnp.concatenate([one_hot((lane == row) & last), one_hot((lane == row + 1.0) & last)], axis=0)
-    both = exact_pick(pick, column)
-    low = both[0:n]
-    high = both[n:]
-    u = [meta[:, 0:1], meta[:, 1:2], meta[:, 2:3] + low[:, 16:17], meta[:, 3:4] + high[:, 16:17]]
-    v = [meta[:, 4:5], meta[:, 5:6], meta[:, 6:7] + low[:, 32:33], meta[:, 7:8] + high[:, 32:33]]
+def advanced(x, y, u, v):
     fy = y + 0.5
     fx = x + 0.5
     w00 = (1.0 - fy) * (1.0 - fx)
@@ -224,29 +230,40 @@
     return new_x, new_y
 
 
+def home_corners(meta, column, across):
+    n = meta.shape[0]
+    depth = column.shape[0]
+    row = meta[:, 8:9]
+    last = meta[:, 9:10] == float(across - 1)
+    lane = phase((n, 3 * depth), depth)
+    pick = jnp.concatenate([one_hot((lane == row) & last), one_hot((lane == row + 1.0) & last)], axis=0)
+    both = mm(pick, stack3(column))
+    low = both[0:n]
+    high = both[n:]
+    u = [meta[:, 0:1], meta[:, 1:2], meta[:, 2:3] + low[:, 16:17], meta[:, 3:4] + high[:, 16:17]]
+    v = [meta[:, 4:5], meta[:, 5:6], meta[:, 6:7] + low[:, 32:33], meta[:, 7:8] + high[:, 32:33]]
+    return u, v
+
+
 def lane_sum(x):
     return jnp.sum(x, axis=1, keepdims=True)
 
 
-def pack_body(part_ref, w_ref, meta_ref, mine_ref, left_ref, right_ref, sel_ref, rw_ref, out_ref, height, across):
+def pack_body(part_ref, w_ref, meta_ref, mine_ref, left_ref, right_ref, sel_ref, rw_ref, out_ref, across):
     n = w_ref.shape[0]
     bands = out_ref.shape[0] // (4 * CAP + 1)
     meta = meta_ref[...]
-    top = height + 16
     step = 4 * CAP + 1
     w = w_ref[...]
-    new_x, new_y = moved_particles(meta, part_ref[0], part_ref[1], right_ref[0 : height + 16], across)
+    new_x, new_y = advanced(part_ref[0], part_ref[1], *home_corners(meta, right_ref[...], across))
     left_meta = left_ref[0:n]
-    left_w = left_ref[top + 2 * n : top + 3 * n]
-    left_x, left_y = moved_particles(
-        left_meta, left_ref[top : top + n], left_ref[top + n : top + 2 * n], mine_ref[0 : height + 16], across
-    )
+    (_, _, u1, u2), (_, _, v1, v2) = home_corners(left_meta, mine_ref[...], across)
+    m = [left_meta[:, 16 + i : 17 + i] for i in range(11)]
+    left_hh = (m[3] + u1 * m[4] + u2 * m[5] + v1 * m[6] + v2 * m[7]) + (
+        u1 * v1 * m[8] + (u1 * v2 + u2 * v1) * m[9] + u2 * v2 * m[10]
+    )
+    left_lh = (m[0] + u1 * m[1] + u2 * m[2]) - left_hh
     choose = sel_ref[...]
-    xy = exact_pick(choose, jnp.concatenate([new_x, new_y], axis=1))
-    for k in range(CAP):
-        rows = slice(k * bands, (k + 1) * bands)
-        for j, source, sl in ((0, xy, slice(0, 128)), (1, xy, slice(128, 256)), (2, rw_ref, slice(0, 128)), (3, rw_ref, slice(128, 256))):
-            out_ref[pl.ds(4 * k + j, bands, stride=step), :] = source[rows, sl]
     gy = new_y + 0.5
     gx = new_x + 0.5
     sums = [
@@ -262,22 +279,25 @@
     mine = jnp.zeros((n, 128), F32)
     for i, value in enumerate(sums):
         mine = jnp.where(lane16 == float(i), value, mine)
-    gy = left_y + 0.5
-    gx = left_x + 0.5
     over = left_meta[:, 11:12] == float(across - 1)
     sums = [
         left_meta[:, 10:11],
-        jnp.where(over, lane_sum(left_w * (1.0 - gy) * gx), 0.0),
-        jnp.where(over, lane_sum(left_w * gy * gx), 0.0),
+        jnp.where(over, left_lh, 0.0),
+        jnp.where(over, left_hh, 0.0),
     ]
     theirs = jnp.zeros((n, 128), F32)
     for i, value in enumerate(sums):
         theirs = jnp.where(lane16 == float(8 + i), value, theirs)
-    values = jnp.concatenate([mine, theirs], axis=0)
-    d4 = iota((bands, n), 0) * float(CAP)
-    slot = to_row(left_meta[:, 12:13], n)
+    picked = mm(choose, stack3(jnp.concatenate([new_x, new_y, mine], axis=1)))
+    for k in range(CAP):
+        rows = slice(k * bands, (k + 1) * bands)
+        for j, source in ((0, picked), (1, picked), (2, rw_ref), (3, rw_ref)):
+            sl = slice(128 * (j % 2), 128 * (j % 2) + 128)
+            out_ref[pl.ds(4 * k + j, bands, stride=step), :] = source[rows, sl]
+    slot = jnp.concatenate([to_row(left_meta[:, 12:13], n)] * 3, axis=1)
+    d4 = iota((bands, 3 * n), 0) * float(CAP)
     theirs_choose = jnp.concatenate([one_hot(d4 + float(k) == slot) for k in range(CAP)], axis=0)
-    chosen = exact_pick(jnp.concatenate([choose, theirs_choose], axis=1), values)
+    chosen = picked[:, 256:] + mm(theirs_choose, stack3(theirs))
     lane = iota((bands, 128), 1)
     group = jnp.floor(lane * 0.0625)
     table = jnp.zeros((bands, 128), F32)
@@ -314,7 +334,7 @@
     tiles = width // 128
     off = 16
     span = height + 32
-    halos = halo_tiles(right_ref[...], left_ref[0 : height + 16])
+    halos = halo_tiles(right_ref[...], left_ref[...])
     uppers = halo_tiles(right2_ref[...], left2_ref[...])
     owns = (f_ref, flow_ref.at[0], flow_ref.at[1])
     for buf, own, halo, upper, start, count in zip((f0, us, vs), owns, halos, uppers, (0, 9, 15), (9, 6, 6)):
@@ -399,9 +419,8 @@
     table = recv_ref[pl.ds(block, bands, stride=step), :]
     lanes = iota((bands, across), 1)
     lane = iota((bands, 128), 1)
-    rows = iota((height, bands), 0)
-    total = jnp.zeros((height, 2 * across), F32)
-    side = jnp.zeros((height, 128), F32)
+    rows = iota((height, 2 * CAP * bands), 0)
+    spreads, values, spread_rows, value_rows = [], [], [], []
     first_row = jnp.zeros((bands, across), F32)
     corner = jnp.zeros((bands, 1), F32)
 
@@ -422,13 +441,10 @@
             ],
             axis=1,
         )
-        pick = one_hot(rows == to_row(row, bands))
-        hi, lo = two(spread)
-        total = total + (mm(pick, hi) + mm(pick, lo))
-        pick = one_hot(rows == to_row(part[8], bands))
-        values = jnp.where(lane == 0.0, part[9], jnp.where(lane == 1.0, part[10], 0.0))
-        hi, lo = two(values)
-        side = side + (mm(pick, hi) + mm(pick, lo))
+        spreads += two(spread)
+        spread_rows += [to_row(row, bands)] * 2
+        values += two(jnp.where(lane == 0.0, part[9], jnp.where(lane == 1.0, part[10], 0.0)))
+        value_rows += [to_row(part[8], bands)] * 2
         o = 64 + 16 * k
         part = [table[:, o + i : o + i + 1] for i in range(11)]
         row, col, ll, hl, lh, hh = part[0:6]
@@ -439,6 +455,8 @@
             + jnp.where((lanes == col + 1.0) & edge, hh, 0.0)
         )
         corner = corner + jnp.where(part[8] == float(height - 1), part[10], 0.0)
+    total = mm(one_hot(rows == jnp.concatenate(spread_rows, axis=1)), jnp.concatenate(spreads, axis=0))
+    side = mm(one_hot(rows == jnp.concatenate(value_rows, axis=1)), jnp.concatenate(values, axis=0))
     same = total[:, 0:across]
     down = pltpu.roll(total[:, across:], 1, 0)
     side_down = pltpu.roll(side, 1, 0)
@@ -479,7 +497,7 @@
         (
             sds((n, 128), F32),
             sds((n, 128), F32),
-            sds((bands * CAP, n), BF16),
+            sds((bands * CAP, 3 * n), BF16),
             sds((bands * CAP, 256), F32),
         ),
         velocity, parts, escaped, home_cell.reshape(1, n), land_cell.reshape(1, n), dest_rank.reshape(1, n),
@@ -487,13 +505,13 @@
     )
     to_left, to_right, meta = call(
         edges_body,
-        (sds((height + 16, 128), F32), sds((height + 16 + 3 * n, 128), F32), sds((n, 128), F32)),
+        (sds((height + 16, 128), F32), sds((height + 16, 128), F32), sds((n, 128), F32)),
         level_set, velocity, below, meta, parts, weight,
     )
     from_left = lax.ppermute(to_right, "gx", ring("gx", 1))
     from_right = lax.ppermute(to_left, "gx", ring("gx", -1))
     (packed,) = call(
-        functools.partial(pack_body, height=height, across=across),
+        functools.partial(pack_body, across=across),
         (sds((bands * step, 128), F32),),
         parts, weight, meta, to_left, from_left, from_right, select, fixed,
     )

time: 68.4 us -> 68.7 us (level)
  no operation moved by 1% of the time
where the time goes in v5:
time: 68.7 us; the launch traced here: 68.3 us
  starting transfers between devices  34.4 us (50%)
  waiting for transfers between devices  22.3 us (32%)
  Pallas kernels  9.09 us (13%)
  between operations  1.46 us (2%)
  local copies, waits for them, and re-layouts  1.12 us (2%)
    ppermute x1, waiting for transfers between devices, shards(): above = lax.ppermute(tail, 'gy', ring('gy', 1))  15.8 us
    ppermute x1, starting transfers between devices, shards(): below = lax.ppermute(head, 'gy', ring('gy', -1))  12.6 us
    pallas_call x7, Pallas kernels, call(): pl.pallas_call(body, out_shape=tuple(outs), in_specs=[spec(sm)] * len(sca...  9.09 us
    all_to_all x1, starting transfers between devices, shards(): lax.all_to_all(packed.reshape(bands * step, 1, 128), 'gy', split_axis=0,...  5.73 us
    ppermute x1, starting transfers between devices, shards(): from_right2 = lax.ppermute(to_left2, 'gx', ring('gx', -1))  5.14 us
    ppermute x1, waiting for transfers between devices, shards(): from_left2 = lax.ppermute(to_right2, 'gx', ring('gx', 1))  4.82 us
    ppermute x1, starting transfers between devices, shards(): from_right = lax.ppermute(to_left, 'gx', ring('gx', -1))  4.47 us
    ppermute x1, starting transfers between devices, shards(): from_left = lax.ppermute(to_right, 'gx', ring('gx', 1))  2.59 us
  transfers between devices with their start and end apart: 7, of which 3 were waited for; matrix products, arithmetic and copies ran while one was open for 0% of the time, Pallas kernels for 6%

profile of v5, /device:TPU:32, one launch (start us, length us, event | category | flops | bytes accessed | tf_op | source)
XLA Modules:
  0.0 68.3 jit_solution(18018536252346387548)
XLA Ops:
  0.7 0.9 %shard_map.96 = (f32[24,512]{1,0:T(8,128)S(1)}, f32[24,512]{1,0:T(8,128)S(1)}) custom-call(f32[64,512]{1,0:T(8,128)} %f_ref.5, f32[2,64,512]{2,1,0:T(8,128)} %flow_ref.7), custom_call_target="tpu_custom_call" | custom-call | tf_op jit(solution)/shard_map/pallas_call | solution.py:66
  1.6 12.6 %collective-permute-start = (f32[24,512]{1,0:T(8,128)S(1)}, f32[24,512]{1,0:T(8,128)S(1)}, u32[]{:S(2)}, u32[]{:S(2)}) collective-permute-start(f32[24,512]{1,0:T(8,128)S(1)} %get-tuple-element.16), channel_id=1, source_target_pairs={{0,504},{8,0},{16,8},{24,16},{32,24},{40,32},{48,40},{56,48},{64,5... | collective-permute-start | bytes 147464 | tf_op jit(solution)/shard_map/ppermute | solution.py:492
  14.8 0.0 copy-start.5
  14.8 0.0 copy-start.6
  14.9 0.6 copy-done.4
  15.5 0.0 copy-done.5
  15.5 0.0 copy-done.6
  15.5 0.4 shard_map.95
  15.9 0.5 copy-done.1
  16.4 0.5 shard_map.97
  16.9 2.6 %collective-permute-start.1 = (f32[80,128]{1,0:T(8,128)S(1)}, f32[80,128]{1,0:T(8,128)S(1)}, u32[]{:S(2)}, u32[]{:S(2)}) collective-permute-start(f32[80,128]{1,0:T(8,128)S(1)} %get-tuple-element.20), channel_id=1, source_target_pairs={{0,1},{1,2},{2,3},{3,4},{4,5},{5,6},{6,7},{7,0},{8,9},{9,10},{10,1... | collective-permute-start | bytes 122888 | tf_op jit(solution)/shard_map/ppermute | solution.py:511
  19.5 4.5 %collective-permute-start.2 = (f32[80,128]{1,0:T(8,128)S(1)}, f32[80,128]{1,0:T(8,128)S(1)}, u32[]{:S(2)}, u32[]{:S(2)}) collective-permute-start(f32[80,128]{1,0:T(8,128)S(1)} %get-tuple-element.19.mine_ref), channel_id=1, source_target_pairs={{0,7},{1,0},{2,1},{3,2},{4,3},{5,4},{6,5},{7,6},{8,15},{9,8},{10,9... | collective-permute-start | bytes 122888 | tf_op jit(solution)/shard_map/ppermute | solution.py:512
  24.0 0.0 collective-permute-done.1.left_ref
  24.0 1.6 %collective-permute-done.2.right_ref = f32[80,128]{1,0:T(8,128)S(1)} collective-permute-done((f32[80,128]{1,0:T(8,128)S(1)}, f32[80,128]{1,0:T(8,128)S(1)}, u32[]{:S(2)}, u32[]{:S(2)}) %collective-permute-start.2) | collective-permute-done | bytes 40992 | tf_op jit(solution)/shard_map/ppermute | solution.py:512
  25.6 2.0 %shard_map.98 = f32[1088,128]{1,0:T(8,128)} custom-call(f32[3,64,128]{2,1,0:T(8,128)S(1)} %bitcast.14, f32[64,128]{1,0:T(8,128)S(1)} %get-tuple-element.15.w_ref, f32[64,128]{1,0:T(8,128)S(1)} %get-tuple-element.18.meta_ref, f32[80,128]{1,0:T(8,128)S(1)} %get-tuple-element.19.mine_ref, f32[80,128]{1,0:T(8,128)S(1)} %collective-permute-done.1.left_ref, ...), custom_call_target="tpu_custom_call" | custom-call | tf_op jit(solution)/shard_map/pallas_call | solution.py:66
  27.7 5.7 %all-to-all-start = ((f32[1088,1,128]{2,1,0:T(1,128)}), f32[1088,1,128]{2,1,0:T(1,128)S(1)}, u32[]{:S(2)}, u32[]{:S(2)}) async-start(f32[1088,1,128]{2,1,0:T(1,128)} %bitcast.5), calls=%async_computation | async-start | bytes 1114112 | tf_op jit(solution)/shard_map/all_to_all | solution.py:518
  33.4 2.0 %collective-permute-start.3 = (f32[24,512]{1,0:T(8,128)S(1)}, f32[24,512]{1,0:T(8,128)S(1)}, u32[]{:S(2)}, u32[]{:S(2)}) collective-permute-start(f32[24,512]{1,0:T(8,128)S(1)} %get-tuple-element.23), channel_id=1, source_target_pairs={{0,8},{8,16},{16,24},{24,32},{32,40},{40,48},{48,56},{56,64},{64,7... | collective-permute-start | bytes 147464 | tf_op jit(solution)/shard_map/ppermute | solution.py:493
  35.4 15.8 %collective-permute-done.3.above_ref = f32[24,512]{1,0:T(8,128)S(1)} collective-permute-done((f32[24,512]{1,0:T(8,128)S(1)}, f32[24,512]{1,0:T(8,128)S(1)}, u32[]{:S(2)}, u32[]{:S(2)}) %collective-permute-start.3) | collective-permute-done | bytes 49184 | tf_op jit(solution)/shard_map/ppermute | solution.py:493
  51.2 0.1 shard_map.99
  51.2 5.1 %collective-permute-start.4 = (f32[16,128]{1,0:T(8,128)S(1)}, f32[16,128]{1,0:T(8,128)S(1)}, u32[]{:S(2)}, u32[]{:S(2)}) collective-permute-start(f32[16,128]{1,0:T(8,128)S(1)} %get-tuple-element.24), channel_id=1, source_target_pairs={{0,7},{1,0},{2,1},{3,2},{4,3},{5,4},{6,5},{7,6},{8,15},{9,8},{10,9... | collective-permute-start | bytes 24584 | tf_op jit(solution)/shard_map/ppermute | solution.py:523
  56.4 1.9 %collective-permute-start.5 = (f32[16,128]{1,0:T(8,128)S(1)}, f32[16,128]{1,0:T(8,128)S(1)}, u32[]{:S(2)}, u32[]{:S(2)}) collective-permute-start(f32[16,128]{1,0:T(8,128)S(1)} %get-tuple-element.25), channel_id=1, source_target_pairs={{0,1},{1,2},{2,3},{3,4},{4,5},{5,6},{6,7},{7,0},{8,9},{9,10},{10,1... | collective-permute-start | bytes 24584 | tf_op jit(solution)/shard_map/ppermute | solution.py:522
  58.3 4.8 %collective-permute-done.5.left2_ref = f32[16,128]{1,0:T(8,128)S(1)} collective-permute-done((f32[16,128]{1,0:T(8,128)S(1)}, f32[16,128]{1,0:T(8,128)S(1)}, u32[]{:S(2)}, u32[]{:S(2)}) %collective-permute-start.5) | collective-permute-done | bytes 8224 | tf_op jit(solution)/shard_map/ppermute | solution.py:522
  63.1 3.4 %shard_map.100.base_ref = f32[64,512]{1,0:T(8,128)S(1)} custom-call(f32[64,512]{1,0:T(8,128)S(1)} %copy-done.1, f32[2,64,512]{2,1,0:T(8,128)S(1)} %copy-done, f32[24,512]{1,0:T(8,128)S(1)} %collective-permute-done.below_ref, f32[24,512]{1,0:T(8,128)S(1)} %collective-permute-done.3.above_ref, f32[80,128]{1,0:T(8,128)S(1)} %collective-permute-done.2.right_ref, ...), custom_call_target="tpu_custom_call" | custom-call | tf_op jit(solution)/shard_map/pallas_call | solution.py:66
  66.6 1.7 %shard_map.101 = (f32[64,512]{1,0:T(8,128)}, f32[64,16,1,128]{3,2,1,0:T(1,128)}) custom-call(f32[64,17,1,128]{3,2,1,0:T(1,128)S(1)} %bitcast.10, f32[1088,128]{1,0:T(8,128)S(1)} %bitcast.11, f32[64,512]{1,0:T(8,128)S(1)} %shard_map.100.base_ref), custom_call_target="tpu_custom_call" | custom-call | tf_op jit(solution)/shard_map/pallas_call | solution.py:66
  (11 shorter events, 0.0 us)
Async XLA Ops:
  0.6 14.2 %copy-start = (f32[2,64,512]{2,1,0:T(8,128)S(1)}, f32[2,64,512]{2,1,0:T(8,128)}, u32[]{:S(2)}) copy-start(f32[2,64,512]{2,1,0:T(8,128)} %flow_ref.7) | copy-start | bytes 786436
  0.6 14.2 %copy-start.2 = (f32[64,3,128]{2,0,1:T(8,128)S(1)}, f32[64,3,128]{2,0,1:T(8,128)}, u32[]{:S(2)}) copy-start(f32[64,3,128]{2,0,1:T(8,128)} %param.10) | copy-start | bytes 294916
  0.7 14.2 %copy-start.3 = (s32[64,128]{1,0:T(8,128)S(1)}, s32[64,128]{1,0:T(8,128)}, u32[]{:S(2)}) copy-start(s32[64,128]{1,0:T(8,128)} %esc_ref.1) | copy-start | bytes 98308
  1.6 14.3 %collective-permute-start = (f32[24,512]{1,0:T(8,128)S(1)}, f32[24,512]{1,0:T(8,128)S(1)}, u32[]{:S(2)}, u32[]{:S(2)}) collective-permute-start(f32[24,512]{1,0:T(8,128)S(1)} %get-tuple-element.16), channel_id=1, source_target_pairs={{0,504},{8,0},{16,8},{24,16},{32,24},{40,32},{48,40},{56,48},{64,5... | collective-permute-start | bytes 147464 | tf_op jit(solution)/shard_map/ppermute | solution.py:492
  14.8 0.7 copy-start.4
  14.8 0.7 copy-start.5
  14.8 0.7 copy-start.6
  15.5 0.9 %copy-start.1 = (f32[64,512]{1,0:T(8,128)S(1)}, f32[64,512]{1,0:T(8,128)}, u32[]{:S(2)}) copy-start(f32[64,512]{1,0:T(8,128)} %f_ref.5) | copy-start | bytes 393220
  16.9 7.1 %collective-permute-start.1 = (f32[80,128]{1,0:T(8,128)S(1)}, f32[80,128]{1,0:T(8,128)S(1)}, u32[]{:S(2)}, u32[]{:S(2)}) collective-permute-start(f32[80,128]{1,0:T(8,128)S(1)} %get-tuple-element.20), channel_id=1, source_target_pairs={{0,1},{1,2},{2,3},{3,4},{4,5},{5,6},{6,7},{7,0},{8,9},{9,10},{10,1... | collective-permute-start | bytes 122888 | tf_op jit(solution)/shard_map/ppermute | solution.py:511
  19.5 6.1 %collective-permute-start.2 = (f32[80,128]{1,0:T(8,128)S(1)}, f32[80,128]{1,0:T(8,128)S(1)}, u32[]{:S(2)}, u32[]{:S(2)}) collective-permute-start(f32[80,128]{1,0:T(8,128)S(1)} %get-tuple-element.19.mine_ref), channel_id=1, source_target_pairs={{0,7},{1,0},{2,1},{3,2},{4,3},{5,4},{6,5},{7,6},{8,15},{9,8},{10,9... | collective-permute-start | bytes 122888 | tf_op jit(solution)/shard_map/ppermute | solution.py:512
  27.7 38.9 %all-to-all-start = ((f32[1088,1,128]{2,1,0:T(1,128)}), f32[1088,1,128]{2,1,0:T(1,128)S(1)}, u32[]{:S(2)}, u32[]{:S(2)}) async-start(f32[1088,1,128]{2,1,0:T(1,128)} %bitcast.5), calls=%async_computation | async-start | bytes 1114112 | tf_op jit(solution)/shard_map/all_to_all | solution.py:518
  33.4 17.8 %collective-permute-start.3 = (f32[24,512]{1,0:T(8,128)S(1)}, f32[24,512]{1,0:T(8,128)S(1)}, u32[]{:S(2)}, u32[]{:S(2)}) collective-permute-start(f32[24,512]{1,0:T(8,128)S(1)} %get-tuple-element.23), channel_id=1, source_target_pairs={{0,8},{8,16},{16,24},{24,32},{32,40},{40,48},{48,56},{56,64},{64,7... | collective-permute-start | bytes 147464 | tf_op jit(solution)/shard_map/ppermute | solution.py:493
  51.2 7.1 %collective-permute-start.4 = (f32[16,128]{1,0:T(8,128)S(1)}, f32[16,128]{1,0:T(8,128)S(1)}, u32[]{:S(2)}, u32[]{:S(2)}) collective-permute-start(f32[16,128]{1,0:T(8,128)S(1)} %get-tuple-element.24), channel_id=1, source_target_pairs={{0,7},{1,0},{2,1},{3,2},{4,3},{5,4},{6,5},{7,6},{8,15},{9,8},{10,9... | collective-permute-start | bytes 24584 | tf_op jit(solution)/shard_map/ppermute | solution.py:523
  56.4 6.8 %collective-permute-start.5 = (f32[16,128]{1,0:T(8,128)S(1)}, f32[16,128]{1,0:T(8,128)S(1)}, u32[]{:S(2)}, u32[]{:S(2)}) collective-permute-start(f32[16,128]{1,0:T(8,128)S(1)} %get-tuple-element.25), channel_id=1, source_target_pairs={{0,1},{1,2},{2,3},{3,4},{4,5},{5,6},{6,7},{7,0},{8,9},{9,10},{10,1... | collective-permute-start | bytes 24584 | tf_op jit(solution)/shard_map/ppermute | solution.py:522

commit v6 on v5

--- a/solution.py
+++ b/solution.py
@@ -74,21 +74,18 @@
     )(*scalars, *args)
 
 
-def heads_body(f_ref, flow_ref, head_ref, tail_ref, f_rows, flow_rows, sems):
-    height = f_ref.shape[0]
-    copies = []
-    for i, (f_top, flow_top) in enumerate(((0, 0), (height - 16, height - 8))):
-        copies.append(pltpu.make_async_copy(f_ref.at[pl.ds(f_top, 16)], f_rows.at[i], sems.at[2 * i]))
-        copies.append(pltpu.make_async_copy(flow_ref.at[:, pl.ds(flow_top, 8)], flow_rows.at[i], sems.at[2 * i + 1]))
+def heads_body(f_ref, flow_ref, head_ref, f_rows, flow_rows, sems):
+    copies = [
+        pltpu.make_async_copy(f_ref.at[pl.ds(0, 24)], f_rows, sems.at[0]),
+        pltpu.make_async_copy(flow_ref.at[:, pl.ds(0, 16)], flow_rows, sems.at[1]),
+    ]
     for copy in copies:
         copy.start()
     for copy in copies:
         copy.wait()
-    for i, (ref, f0, v0) in enumerate(((head_ref, 0, 0), (tail_ref, 7, 2))):
-        ref[0:9] = f_rows[i, f0 : f0 + 9]
-        ref[9:15] = flow_rows[i, 0, v0 : v0 + 6]
-        ref[15:21] = flow_rows[i, 1, v0 : v0 + 6]
-        ref[21:24] = jnp.zeros((3, f_ref.shape[1]), F32)
+    head_ref[0:18] = f_rows[0:18]
+    head_ref[18:33] = flow_rows[0, 0:15]
+    head_ref[33:48] = flow_rows[1, 0:15]
 
 
 def prepare_body(count_ref, flow_ref, part_ref, esc_ref, home_ref, land_ref, dest_ref, meta_ref, w_ref, sel_ref, rw_ref):
@@ -151,16 +148,6 @@
     return jnp.where(lane < 32.0, m, out)
 
 
-def corners_body(above_ref, left_ref, right_ref):
-    across = above_ref.shape[1]
-    zero = jnp.zeros((8, 128), F32)
-    near, far = slice(0, 128), slice(across - 128, across)
-    left_ref[0:8] = pack_left(above_ref[0:8, near], above_ref[9:17, near], above_ref[15:23, near])
-    left_ref[8:16] = pack_left(above_ref[8:16, near], zero, zero)
-    right_ref[0:8] = pack_right(above_ref[0:8, far], above_ref[9:17, far], above_ref[15:23, far], zero)
-    right_ref[8:16] = pack_right(above_ref[8:16, far], zero, zero, zero)
-
-
 def edges_body(f_ref, flow_ref, below_ref, meta_ref, part_ref, w_ref, left_ref, right_ref, meta2_ref):
     n = w_ref.shape[0]
     height, across = f_ref.shape
@@ -172,7 +159,7 @@
     lanes = iota((n, across), 1)
     at0 = (lanes == col) & last
     at1 = (lanes == col + 1.0) & last
-    for base, r in ((0, 9), (4, 15)):
+    for base, r in ((0, 18), (4, 33)):
         line = jnp.broadcast_to(below_ref[r : r + 1, :], (n, across))
         c10 = jnp.sum(jnp.where(at0, line, 0.0), axis=1, keepdims=True)
         c11 = jnp.sum(jnp.where(at1, line, 0.0), axis=1, keepdims=True)
@@ -200,8 +187,10 @@
 
     def pieces(sl):
         yield 0, height, f_ref[:, sl], flow_ref[0, :, sl], flow_ref[1, :, sl], sent
-        yield height, 8, below_ref[0:8, sl], below_ref[9:17, sl], below_ref[15:23, sl], zero
-        yield height + 8, 8, below_ref[8:16, sl], zero, zero, zero
+        last = pltpu.roll(below_ref[40:48, sl], 7, 0)
+        yield height, 8, below_ref[0:8, sl], below_ref[18:26, sl], below_ref[33:41, sl], zero
+        yield height + 8, 8, below_ref[8:16, sl], below_ref[26:34, sl], last, zero
+        yield height + 16, 8, below_ref[16:24, sl], zero, zero, zero
 
     for top, rows, f, u, v, _ in pieces(slice(0, 128)):
         left_ref[top : top + rows] = pack_left(f, u, v)
@@ -249,15 +238,15 @@
     return jnp.sum(x, axis=1, keepdims=True)
 
 
-def pack_body(part_ref, w_ref, meta_ref, mine_ref, left_ref, right_ref, sel_ref, rw_ref, out_ref, across):
+def pack_body(part_ref, w_ref, meta_ref, mine_ref, left_ref, right_ref, sel_ref, rw_ref, out_ref, height, across):
     n = w_ref.shape[0]
     bands = out_ref.shape[0] // (4 * CAP + 1)
     meta = meta_ref[...]
     step = 4 * CAP + 1
     w = w_ref[...]
-    new_x, new_y = advanced(part_ref[0], part_ref[1], *home_corners(meta, right_ref[...], across))
+    new_x, new_y = advanced(part_ref[0], part_ref[1], *home_corners(meta, right_ref[0 : height + 8], across))
     left_meta = left_ref[0:n]
-    (_, _, u1, u2), (_, _, v1, v2) = home_corners(left_meta, mine_ref[...], across)
+    (_, _, u1, u2), (_, _, v1, v2) = home_corners(left_meta, mine_ref[0 : height + 8], across)
     m = [left_meta[:, 16 + i : 17 + i] for i in range(11)]
     left_hh = (m[3] + u1 * m[4] + u2 * m[5] + v1 * m[6] + v2 * m[7]) + (
         u1 * v1 * m[8] + (u1 * v2 + u2 * v1) * m[9] + u2 * v2 * m[10]
@@ -328,26 +317,18 @@
     return speed * c + jnp.abs(speed) * (top / (6.0 * (w1 + w2 + w3)))
 
 
-def stencil_body(f_ref, flow_ref, below_ref, above_ref, right_ref, left_ref, right2_ref, left2_ref, out_ref, f0, us, vs, f1, f2):
+def stencil_body(f_ref, flow_ref, below_ref, right_ref, left_ref, out_ref, next_ref, f0, us, vs, f1, f2):
     height, across = f_ref.shape
-    width = across + 128
-    tiles = width // 128
-    off = 16
-    span = height + 32
+    tiles = across // 128 + 1
+    span = height + 24
     halos = halo_tiles(right_ref[...], left_ref[...])
-    uppers = halo_tiles(right2_ref[...], left2_ref[...])
     owns = (f_ref, flow_ref.at[0], flow_ref.at[1])
-    for buf, own, halo, upper, start, count in zip((f0, us, vs), owns, halos, uppers, (0, 9, 15), (9, 6, 6)):
-        for j in range(tiles):
+    for buf, own, halo, start, count in zip((f0, us, vs), owns, halos, (0, 18, 33), (18, 15, 15)):
+        for j in range(tiles - 1):
             sl = slice(128 * j, 128 * j + 128)
-            top = span * j + off
-            if j < tiles - 1:
-                buf[top : top + height, :] = own[:, sl]
-                buf[top + height : top + height + count, :] = below_ref[start : start + count, sl]
-                buf[top - count : top, :] = above_ref[start : start + count, sl]
-            else:
-                buf[top : top + height + count, :] = halo[0 : height + count]
-                buf[top - count : top, :] = upper[0:count]
+            buf[span * j : span * j + height, :] = own[:, sl]
+            buf[span * j + height : span * j + height + count, :] = below_ref[start : start + count, sl]
+        buf[span * (tiles - 1) : span * tiles, :] = halo
 
     lane = lax.broadcasted_iota(jnp.int32, (8, 128), 1)
 
@@ -375,7 +356,7 @@
             write(j, f[j] - DT * (x_term + y_term))
 
     def first(i, carry):
-        base = pl.multiple_of(i * 8 + 8, 8)
+        base = i * 8 + 3
 
         def write(j, value):
             f1[pl.ds(span * j + base, 8), :] = value
@@ -384,7 +365,7 @@
         return carry
 
     def second(i, carry):
-        base = pl.multiple_of(i * 8 + 8, 8)
+        base = i * 8 + 6
 
         def write(j, value):
             at = pl.ds(span * j + base, 8)
@@ -394,23 +375,24 @@
         return carry
 
     def third(i, carry):
-        base = pl.multiple_of(i * 8 + 16, 8)
-        place = pl.multiple_of(i * 8, 8)
+        base = i * 8 + 9
 
         def write(j, value):
-            kept = f0[pl.ds(span * j + base, 8), :]
-            out_ref[pl.ds(place, 8), 128 * j : 128 * j + 128] = kept * (1.0 / 3.0) + (2.0 / 3.0) * value
+            at = pl.ds(span * j + base, 8)
+            out_ref[at, :] = f0[at, :] * (1.0 / 3.0) + (2.0 / 3.0) * value
 
         stage(f2, tiles - 1, base, write)
         return carry
 
     lax.fori_loop(0, height // 8 + 2, first, 0, unroll=2)
-    lax.fori_loop(0, height // 8 + 2, second, 0, unroll=2)
+    lax.fori_loop(0, height // 8 + 1, second, 0, unroll=3)
     lax.fori_loop(0, height // 8, third, 0, unroll=2)
-
-
-def deposit_body(rows_ref, recv_ref, base_ref, out_ref, moved_ref, sem):
-    height, across = base_ref.shape
+    for j in range(tiles - 1):
+        next_ref[16 * j : 16 * j + 16] = out_ref[span * j + height : span * j + height + 16]
+
+
+def deposit_body(rows_ref, recv_ref, base_ref, first_ref, out_ref, moved_ref, sem):
+    height, across = out_ref.shape
     step = 4 * CAP + 1
     bands = recv_ref.shape[0] // step
     block = 4 * CAP
@@ -466,7 +448,15 @@
     incoming = incoming + jnp.where(iota((1, across), 1) == 0.0, jnp.sum(corner), 0.0)
     down = jnp.where(r == 0.0, incoming, down)
     column = side[:, 0:1] + jnp.where(iota((height, 1), 0) == 0.0, 0.0, side_down[:, 1:2])
-    out_ref[...] = base_ref[...] + (same + down + jnp.where(c == 0.0, column, 0.0))
+    added = same + down + jnp.where(c == 0.0, column, 0.0)
+    span = height + 24
+    early = iota((16, 128), 0) < 9.0
+    for j in range(across // 128):
+        sl = slice(128 * j, 128 * j + 128)
+        at = span * j
+        level = jnp.where(early, first_ref[16 * j : 16 * j + 16], base_ref[at : at + 16])
+        out_ref[0:16, sl] = level + added[0:16, sl]
+        out_ref[16:, sl] = base_ref[at + 16 : at + height] + added[16:, sl]
     copy.wait()
 
 
@@ -481,16 +471,15 @@
     bands = lax.axis_size("gy")
     step = 4 * CAP + 1
     sds = jax.ShapeDtypeStruct
-    head, tail = call(
+    (head,) = call(
         heads_body,
-        (sds((24, across), F32), sds((24, across), F32)),
+        (sds((48, across), F32),),
         pltpu.with_memory_space_constraint(level_set, pltpu.HBM),
         pltpu.with_memory_space_constraint(velocity, pltpu.HBM),
         spaces=[pltpu.HBM, pltpu.HBM],
-        scratch=[pltpu.VMEM((2, 16, across), F32), pltpu.VMEM((2, 2, 8, across), F32), pltpu.SemaphoreType.DMA((4,))],
+        scratch=[pltpu.VMEM((24, across), F32), pltpu.VMEM((2, 16, across), F32), pltpu.SemaphoreType.DMA((2,))],
     )
     below = lax.ppermute(head, "gy", ring("gy", -1))
-    above = lax.ppermute(tail, "gy", ring("gy", 1))
     parts = jnp.transpose(particles, (1, 0, 2))
     meta, weight, select, fixed = call(
         prepare_body,
@@ -505,33 +494,32 @@
     )
     to_left, to_right, meta = call(
         edges_body,
-        (sds((height + 16, 128), F32), sds((height + 16, 128), F32), sds((n, 128), F32)),
+        (sds((height + 24, 128), F32), sds((height + 24, 128), F32), sds((n, 128), F32)),
         level_set, velocity, below, meta, parts, weight,
     )
     from_left = lax.ppermute(to_right, "gx", ring("gx", 1))
     from_right = lax.ppermute(to_left, "gx", ring("gx", -1))
     (packed,) = call(
-        functools.partial(pack_body, across=across),
+        functools.partial(pack_body, height=height, across=across),
         (sds((bands * step, 128), F32),),
         parts, weight, meta, to_left, from_left, from_right, select, fixed,
     )
     arrived = lax.all_to_all(
         packed.reshape(bands * step, 1, 128), "gy", split_axis=0, concat_axis=0, tiled=True
     )
-    to_left2, to_right2 = call(corners_body, (sds((16, 128), F32), sds((16, 128), F32)), above)
-    from_left2 = lax.ppermute(to_right2, "gx", ring("gx", 1))
-    from_right2 = lax.ppermute(to_left2, "gx", ring("gx", -1))
-    wide = pltpu.VMEM(((across // 128 + 1) * (height + 32), 128), F32)
-    (section,) = call(
+    span = height + 24
+    wide = pltpu.VMEM(((across // 128 + 1) * span, 128), F32)
+    section, ahead = call(
         stencil_body,
-        (sds((height, across), F32),),
-        level_set, velocity, below, above, from_right, from_left, from_right2, from_left2,
+        (sds((across // 128 * span, 128), F32), sds((across // 128 * 16, 128), F32)),
+        level_set, velocity, below, from_right, from_left,
         scratch=[wide] * 5,
     )
+    first_rows = lax.ppermute(ahead, "gy", ring("gy", 1))
     level, moved = call(
         deposit_body,
         (sds((height, across), F32), sds((bands, 4 * CAP, 1, 128), F32)),
-        arrived.reshape(bands, step, 1, 128), arrived.reshape(bands * step, 128), section,
+        arrived.reshape(bands, step, 1, 128), arrived.reshape(bands * step, 128), section, first_rows,
         out_spaces=[pltpu.VMEM, pltpu.HBM],
         scratch=[pltpu.SemaphoreType.DMA],
     )

time: 68.7 us -> 58.1 us (0.85)
  the two profiles are of different devices: /device:TPU:32 before, /device:TPU:24 now
where the time goes in v6:
time: 58.1 us; the launch traced here: 57.7 us
  starting transfers between devices  27.1 us (47%)
  waiting for transfers between devices  19.6 us (34%)
  Pallas kernels  8.87 us (15%)
  between operations  1.43 us (2%)
  local copies, waits for them, and re-layouts  0.7 us (1%)
    ppermute x1, starting transfers between devices, shards(): below = lax.ppermute(head, 'gy', ring('gy', -1))  12.6 us
    ppermute x1, waiting for transfers between devices, shards(): first_rows = lax.ppermute(ahead, 'gy', ring('gy', 1))  11.8 us
    pallas_call x6, Pallas kernels, call(): pl.pallas_call(body, out_shape=tuple(outs), in_specs=[spec(sm)] * len(sca...  8.87 us
    all_to_all x1, starting transfers between devices, shards(): lax.all_to_all(packed.reshape(bands * step, 1, 128), 'gy', split_axis=0,...  5.96 us
    ppermute x1, waiting for transfers between devices, shards(): from_right = lax.ppermute(to_left, 'gx', ring('gx', -1))  5.21 us
    ppermute x1, starting transfers between devices, shards(): from_left = lax.ppermute(to_right, 'gx', ring('gx', 1))  4.7 us
    all_to_all x1, waiting for transfers between devices, shards(): lax.all_to_all(packed.reshape(bands * step, 1, 128), 'gy', split_axis=0,...  2.12 us
    ppermute x1, starting transfers between devices, shards(): first_rows = lax.ppermute(ahead, 'gy', ring('gy', 1))  1.96 us
  transfers between devices with their start and end apart: 5, of which 4 were waited for; matrix products, arithmetic and copies ran while one was open for 0% of the time, Pallas kernels for 6%

profile of v6, /device:TPU:24, one launch (start us, length us, event | category | flops | bytes accessed | tf_op | source)
XLA Modules:
  0.0 57.7 jit_solution(4878973549078256575)
XLA Ops:
  0.7 0.9 %shard_map.96 = f32[48,512]{1,0:T(8,128)S(1)} custom-call(f32[64,512]{1,0:T(8,128)} %f_ref.5, f32[2,64,512]{2,1,0:T(8,128)} %flow_ref.7), custom_call_target="tpu_custom_call" | custom-call | tf_op jit(solution)/shard_map/pallas_call | solution.py:66
  1.6 12.6 %collective-permute-start = (f32[48,512]{1,0:T(8,128)S(1)}, f32[48,512]{1,0:T(8,128)S(1)}, u32[]{:S(2)}, u32[]{:S(2)}) collective-permute-start(f32[48,512]{1,0:T(8,128)S(1)} %shard_map.96), channel_id=1, source_target_pairs={{0,504},{8,0},{16,8},{24,16},{32,24},{40,32},{48,40},{56,48},{64,5... | collective-permute-start | bytes 294920 | tf_op jit(solution)/shard_map/ppermute | solution.py:482
  14.8 0.0 copy-start.4
  14.9 0.0 copy-start.5
  14.9 0.0 copy-start.6
  14.9 0.0 copy-done
  14.9 0.6 %copy-done.4 = s32[64]{0:T(128)S(1)} copy-done((s32[64]{0:T(128)S(1)}, s32[64]{0:T(128)}, u32[]{:S(2)}) %copy-start.4) | copy-done | bytes 280
  15.5 0.0 copy-done.5
  15.5 0.0 copy-done.6
  15.5 0.4 shard_map.95
  15.9 0.4 collective-permute-done.below_ref
  16.4 0.0 copy-done.1
  16.4 0.5 shard_map.97
  16.9 4.7 %collective-permute-start.1 = (f32[88,128]{1,0:T(8,128)S(1)}, f32[88,128]{1,0:T(8,128)S(1)}, u32[]{:S(2)}, u32[]{:S(2)}) collective-permute-start(f32[88,128]{1,0:T(8,128)S(1)} %get-tuple-element.17), channel_id=1, source_target_pairs={{0,1},{1,2},{2,3},{3,4},{4,5},{5,6},{6,7},{7,0},{8,9},{9,10},{10,1... | collective-permute-start | bytes 135176 | tf_op jit(solution)/shard_map/ppermute | solution.py:500
  21.6 1.9 %collective-permute-start.2 = (f32[88,128]{1,0:T(8,128)S(1)}, f32[88,128]{1,0:T(8,128)S(1)}, u32[]{:S(2)}, u32[]{:S(2)}) collective-permute-start(f32[88,128]{1,0:T(8,128)S(1)} %get-tuple-element.16.mine_ref), channel_id=1, source_target_pairs={{0,7},{1,0},{2,1},{3,2},{4,3},{5,4},{6,5},{7,6},{8,15},{9,8},{10,9... | collective-permute-start | bytes 135176 | tf_op jit(solution)/shard_map/ppermute | solution.py:501
  23.6 0.0 collective-permute-done.1.left_ref
  23.6 5.2 %collective-permute-done.2.right_ref = f32[88,128]{1,0:T(8,128)S(1)} collective-permute-done((f32[88,128]{1,0:T(8,128)S(1)}, f32[88,128]{1,0:T(8,128)S(1)}, u32[]{:S(2)}, u32[]{:S(2)}) %collective-permute-start.2) | collective-permute-done | bytes 45088 | tf_op jit(solution)/shard_map/ppermute | solution.py:501
  28.8 2.0 %shard_map.98 = f32[1088,128]{1,0:T(8,128)} custom-call(f32[3,64,128]{2,1,0:T(8,128)S(1)} %bitcast.14, f32[64,128]{1,0:T(8,128)S(1)} %get-tuple-element.13.w_ref, f32[64,128]{1,0:T(8,128)S(1)} %get-tuple-element.15.meta_ref, f32[88,128]{1,0:T(8,128)S(1)} %get-tuple-element.16.mine_ref, f32[88,128]{1,0:T(8,128)S(1)} %collective-permute-done.1.left_ref, ...), custom_call_target="tpu_custom_call" | custom-call | tf_op jit(solution)/shard_map/pallas_call | solution.py:66
  30.8 6.0 %all-to-all-start = ((f32[1088,1,128]{2,1,0:T(1,128)}), f32[1088,1,128]{2,1,0:T(1,128)S(1)}, u32[]{:S(2)}, u32[]{:S(2)}) async-start(f32[1088,1,128]{2,1,0:T(1,128)} %bitcast.5), calls=%async_computation | async-start | bytes 1114112 | tf_op jit(solution)/shard_map/all_to_all | solution.py:507
  36.8 3.3 %shard_map.99 = (f32[352,128]{1,0:T(8,128)S(1)}, f32[64,128]{1,0:T(8,128)S(1)}) custom-call(f32[64,512]{1,0:T(8,128)S(1)} %copy-done.1, f32[2,64,512]{2,1,0:T(8,128)S(1)} %copy-done, f32[48,512]{1,0:T(8,128)S(1)} %collective-permute-done.below_ref, f32[88,128]{1,0:T(8,128)S(1)} %collective-permute-done.2.right_ref, f32[88,128]{1,0:T(8,128)S(1)} %collective-permute-done.1.left_ref), custom_call_target="tpu_custom_call" | custom-call | tf_op jit(solution)/shard_map/pallas_call | solution.py:66
  40.1 2.0 %collective-permute-start.3 = (f32[64,128]{1,0:T(8,128)S(1)}, f32[64,128]{1,0:T(8,128)S(1)}, u32[]{:S(2)}, u32[]{:S(2)}) collective-permute-start(f32[64,128]{1,0:T(8,128)S(1)} %get-tuple-element.21), channel_id=1, source_target_pairs={{0,8},{8,16},{16,24},{24,32},{32,40},{40,48},{48,56},{56,64},{64,7... | collective-permute-start | bytes 98312 | tf_op jit(solution)/shard_map/ppermute | solution.py:518
  42.0 11.8 %collective-permute-done.3.first_ref = f32[64,128]{1,0:T(8,128)S(1)} collective-permute-done((f32[64,128]{1,0:T(8,128)S(1)}, f32[64,128]{1,0:T(8,128)S(1)}, u32[]{:S(2)}, u32[]{:S(2)}) %collective-permute-start.3) | collective-permute-done | bytes 32800 | tf_op jit(solution)/shard_map/ppermute | solution.py:518
  53.9 2.1 %all-to-all-done = f32[1088,1,128]{2,1,0:T(1,128)S(1)} async-done(((f32[1088,1,128]{2,1,0:T(1,128)}), f32[1088,1,128]{2,1,0:T(1,128)S(1)}, u32[]{:S(2)}, u32[]{:S(2)}) %all-to-all-start) | async-done | bytes 557088 | tf_op jit(solution)/shard_map/all_to_all | solution.py:507
  56.0 1.7 %shard_map.100 = (f32[64,512]{1,0:T(8,128)}, f32[64,16,1,128]{3,2,1,0:T(1,128)}) custom-call(f32[64,17,1,128]{3,2,1,0:T(1,128)S(1)} %bitcast.10, f32[1088,128]{1,0:T(8,128)S(1)} %bitcast.11, f32[352,128]{1,0:T(8,128)S(1)} %get-tuple-element.20.base_ref, f32[64,128]{1,0:T(8,128)S(1)} %collective-permute-done.3.first_ref), custom_call_target="tpu_custom_call" | custom-call | tf_op jit(solution)/shard_map/pallas_call | solution.py:66
  (6 shorter events, 0.0 us)
Async XLA Ops:
  0.6 14.2 %copy-start = (f32[2,64,512]{2,1,0:T(8,128)S(1)}, f32[2,64,512]{2,1,0:T(8,128)}, u32[]{:S(2)}) copy-start(f32[2,64,512]{2,1,0:T(8,128)} %flow_ref.7) | copy-start | bytes 786436
  0.6 14.2 %copy-start.3 = (s32[64,128]{1,0:T(8,128)S(1)}, s32[64,128]{1,0:T(8,128)}, u32[]{:S(2)}) copy-start(s32[64,128]{1,0:T(8,128)} %esc_ref.1) | copy-start | bytes 98308
  0.7 14.2 %copy-start.2 = (f32[64,3,128]{2,0,1:T(8,128)S(1)}, f32[64,3,128]{2,0,1:T(8,128)}, u32[]{:S(2)}) copy-start(f32[64,3,128]{2,0,1:T(8,128)} %param.10) | copy-start | bytes 294916
  1.6 14.8 %collective-permute-start = (f32[48,512]{1,0:T(8,128)S(1)}, f32[48,512]{1,0:T(8,128)S(1)}, u32[]{:S(2)}, u32[]{:S(2)}) collective-permute-start(f32[48,512]{1,0:T(8,128)S(1)} %shard_map.96), channel_id=1, source_target_pairs={{0,504},{8,0},{16,8},{24,16},{32,24},{40,32},{48,40},{56,48},{64,5... | collective-permute-start | bytes 294920 | tf_op jit(solution)/shard_map/ppermute | solution.py:482
  14.8 0.7 %copy-start.4 = (s32[64]{0:T(128)S(1)}, s32[64]{0:T(128)}, u32[]{:S(2)}) copy-start(s32[64]{0:T(128)} %param.12) | copy-start | bytes 772
  14.9 0.7 %copy-start.5 = (s32[64]{0:T(128)S(1)}, s32[64]{0:T(128)}, u32[]{:S(2)}) copy-start(s32[64]{0:T(128)} %param.13) | copy-start | bytes 772
  14.9 0.7 %copy-start.6 = (s32[64]{0:T(128)S(1)}, s32[64]{0:T(128)}, u32[]{:S(2)}) copy-start(s32[64]{0:T(128)} %param.14) | copy-start | bytes 772
  15.5 0.9 %copy-start.1 = (f32[64,512]{1,0:T(8,128)S(1)}, f32[64,512]{1,0:T(8,128)}, u32[]{:S(2)}) copy-start(f32[64,512]{1,0:T(8,128)} %f_ref.5) | copy-start | bytes 393220
  16.9 6.6 %collective-permute-start.1 = (f32[88,128]{1,0:T(8,128)S(1)}, f32[88,128]{1,0:T(8,128)S(1)}, u32[]{:S(2)}, u32[]{:S(2)}) collective-permute-start(f32[88,128]{1,0:T(8,128)S(1)} %get-tuple-element.17), channel_id=1, source_target_pairs={{0,1},{1,2},{2,3},{3,4},{4,5},{5,6},{6,7},{7,0},{8,9},{9,10},{10,1... | collective-permute-start | bytes 135176 | tf_op jit(solution)/shard_map/ppermute | solution.py:500
  21.6 7.2 %collective-permute-start.2 = (f32[88,128]{1,0:T(8,128)S(1)}, f32[88,128]{1,0:T(8,128)S(1)}, u32[]{:S(2)}, u32[]{:S(2)}) collective-permute-start(f32[88,128]{1,0:T(8,128)S(1)} %get-tuple-element.16.mine_ref), channel_id=1, source_target_pairs={{0,7},{1,0},{2,1},{3,2},{4,3},{5,4},{6,5},{7,6},{8,15},{9,8},{10,9... | collective-permute-start | bytes 135176 | tf_op jit(solution)/shard_map/ppermute | solution.py:501
  30.8 25.2 %all-to-all-start = ((f32[1088,1,128]{2,1,0:T(1,128)}), f32[1088,1,128]{2,1,0:T(1,128)S(1)}, u32[]{:S(2)}, u32[]{:S(2)}) async-start(f32[1088,1,128]{2,1,0:T(1,128)} %bitcast.5), calls=%async_computation | async-start | bytes 1114112 | tf_op jit(solution)/shard_map/all_to_all | solution.py:507
  40.1 13.8 %collective-permute-start.3 = (f32[64,128]{1,0:T(8,128)S(1)}, f32[64,128]{1,0:T(8,128)S(1)}, u32[]{:S(2)}, u32[]{:S(2)}) collective-permute-start(f32[64,128]{1,0:T(8,128)S(1)} %get-tuple-element.21), channel_id=1, source_target_pairs={{0,8},{8,16},{16,24},{24,32},{32,40},{40,48},{48,56},{56,64},{64,7... | collective-permute-start | bytes 98312 | tf_op jit(solution)/shard_map/ppermute | solution.py:518

commit v7 on v6

--- a/solution.py
+++ b/solution.py
@@ -44,10 +44,6 @@
 
 def to_column(row, n):
     return jnp.sum(jnp.where(eye(n), jnp.broadcast_to(row, (n, n)), 0.0), axis=1, keepdims=True)
-
-
-def to_row(col, n):
-    return jnp.sum(jnp.where(eye(n), jnp.broadcast_to(col, (n, n)), 0.0), axis=0, keepdims=True)
 
 
 def one_hot(mask):
@@ -88,7 +84,19 @@
     head_ref[33:48] = flow_rows[1, 0:15]
 
 
-def prepare_body(count_ref, flow_ref, part_ref, esc_ref, home_ref, land_ref, dest_ref, meta_ref, w_ref, sel_ref, rw_ref):
+def advanced(x, y, u, v):
+    fy = y + 0.5
+    fx = x + 0.5
+    w00 = (1.0 - fy) * (1.0 - fx)
+    w10 = fy * (1.0 - fx)
+    w01 = (1.0 - fy) * fx
+    w11 = fy * fx
+    new_x = x + DT * (w00 * u[0] + w10 * u[1] + w01 * u[2] + w11 * u[3])
+    new_y = y + DT * (w00 * v[0] + w10 * v[1] + w01 * v[2] + w11 * v[3])
+    return new_x, new_y
+
+
+def prepare_body(count_ref, flow_ref, part_ref, esc_ref, home_ref, land_ref, dest_ref, meta_ref, w_ref, x_ref, y_ref, sel_ref, rw_ref):
     n = esc_ref.shape[0]
     height, across = flow_ref.shape[1:]
     home = to_column(home_ref[...].astype(F32), n)
@@ -120,11 +128,11 @@
         for where_at in (at0, at1):
             for rows in (low, high):
                 parts.append(jnp.sum(jnp.where(where_at, rows, 0.0), axis=1, keepdims=True))
-    columns = parts + [row, col, land_row, land_col, slot]
+    x_ref[...], y_ref[...] = advanced(part_ref[0], part_ref[1], parts[0:4], parts[4:8])
     lane = iota((n, 128), 1)
     meta = jnp.zeros((n, 128), F32)
-    for i, value in enumerate(columns):
-        meta = jnp.where(lane == float(i), value, meta)
+    for i, value in enumerate((row, col, land_row, land_col, slot)):
+        meta = jnp.where(lane == float(8 + i), value, meta)
     meta_ref[...] = meta
     w = esc_ref[...].astype(F32) * part_ref[2]
     w_ref[...] = w
@@ -148,7 +156,7 @@
     return jnp.where(lane < 32.0, m, out)
 
 
-def edges_body(f_ref, flow_ref, below_ref, meta_ref, part_ref, w_ref, left_ref, right_ref, meta2_ref):
+def edges_body(f_ref, flow_ref, below_ref, meta_ref, part_ref, w_ref, x_ref, y_ref, left_ref, right_ref, x2_ref, y2_ref):
     n = w_ref.shape[0]
     height, across = f_ref.shape
     meta = meta_ref[...]
@@ -159,23 +167,24 @@
     lanes = iota((n, across), 1)
     at0 = (lanes == col) & last
     at1 = (lanes == col + 1.0) & last
-    for base, r in ((0, 18), (4, 33)):
+    fix = []
+    for r in (18, 33):
         line = jnp.broadcast_to(below_ref[r : r + 1, :], (n, across))
-        c10 = jnp.sum(jnp.where(at0, line, 0.0), axis=1, keepdims=True)
-        c11 = jnp.sum(jnp.where(at1, line, 0.0), axis=1, keepdims=True)
-        meta = meta + jnp.where(lane == float(base + 1), c10, 0.0) + jnp.where(lane == float(base + 3), c11, 0.0)
-    meta2_ref[...] = meta
-    x = part_ref[0]
-    y = part_ref[1]
+        for where_at in (at0, at1):
+            fix.append(jnp.sum(jnp.where(where_at, line, 0.0), axis=1, keepdims=True))
     w = w_ref[...]
-    fy = y + 0.5
-    fx = x + 0.5
-    near0 = (1.0 - fy) * (1.0 - fx)
-    near1 = fy * (1.0 - fx)
-    gx = fx + DT * (near0 * meta[:, 0:1] + near1 * meta[:, 1:2])
-    gy = fy + DT * (near0 * meta[:, 4:5] + near1 * meta[:, 5:6])
+    fy = part_ref[1] + 0.5
+    fx = part_ref[0] + 0.5
+    low1 = fy * (1.0 - fx)
+    high1 = fy * fx
+    new_x = x_ref[...] + DT * (low1 * fix[0] + high1 * fix[1])
+    new_y = y_ref[...] + DT * (low1 * fix[2] + high1 * fix[3])
+    x2_ref[...] = new_x
+    y2_ref[...] = new_y
+    gx = new_x + 0.5
+    gy = new_y + 0.5
     e1 = DT * ((1.0 - fy) * fx)
-    e2 = DT * (fy * fx)
+    e2 = DT * high1
     wgx, wgy, w1, w2 = w * gx, w * gy, w * e1, w * e2
     moments = [wgx, w1, w2, wgx * gy, wgy * e1, wgy * e2, wgx * e1, wgx * e2, w1 * e1, w1 * e2, w2 * e2]
     sent = meta
@@ -207,83 +216,77 @@
     return f, u, v
 
 
-def advanced(x, y, u, v):
-    fy = y + 0.5
-    fx = x + 0.5
-    w00 = (1.0 - fy) * (1.0 - fx)
-    w10 = fy * (1.0 - fx)
-    w01 = (1.0 - fy) * fx
-    w11 = fy * fx
-    new_x = x + DT * (w00 * u[0] + w10 * u[1] + w01 * u[2] + w11 * u[3])
-    new_y = y + DT * (w00 * v[0] + w10 * v[1] + w01 * v[2] + w11 * v[3])
-    return new_x, new_y
-
-
-def home_corners(meta, column, across):
+def right_corners(meta, column, across):
     n = meta.shape[0]
     depth = column.shape[0]
     row = meta[:, 8:9]
     last = meta[:, 9:10] == float(across - 1)
     lane = phase((n, 3 * depth), depth)
     pick = jnp.concatenate([one_hot((lane == row) & last), one_hot((lane == row + 1.0) & last)], axis=0)
-    both = mm(pick, stack3(column))
-    low = both[0:n]
-    high = both[n:]
-    u = [meta[:, 0:1], meta[:, 1:2], meta[:, 2:3] + low[:, 16:17], meta[:, 3:4] + high[:, 16:17]]
-    v = [meta[:, 4:5], meta[:, 5:6], meta[:, 6:7] + low[:, 32:33], meta[:, 7:8] + high[:, 32:33]]
-    return u, v
+    return mm(pick, stack3(column))
 
 
 def lane_sum(x):
     return jnp.sum(x, axis=1, keepdims=True)
 
 
-def pack_body(part_ref, w_ref, meta_ref, mine_ref, left_ref, right_ref, sel_ref, rw_ref, out_ref, height, across):
+def pack_body(part_ref, w_ref, x_ref, y_ref, meta_ref, mine_ref, left_ref, right_ref, sel_ref, rw_ref, out_ref, across):
     n = w_ref.shape[0]
     bands = out_ref.shape[0] // (4 * CAP + 1)
+    depth = right_ref.shape[0] - 16
     meta = meta_ref[...]
     step = 4 * CAP + 1
     w = w_ref[...]
-    new_x, new_y = advanced(part_ref[0], part_ref[1], *home_corners(meta, right_ref[0 : height + 8], across))
     left_meta = left_ref[0:n]
-    (_, _, u1, u2), (_, _, v1, v2) = home_corners(left_meta, mine_ref[0 : height + 8], across)
-    m = [left_meta[:, 16 + i : 17 + i] for i in range(11)]
-    left_hh = (m[3] + u1 * m[4] + u2 * m[5] + v1 * m[6] + v2 * m[7]) + (
-        u1 * v1 * m[8] + (u1 * v2 + u2 * v1) * m[9] + u2 * v2 * m[10]
-    )
-    left_lh = (m[0] + u1 * m[1] + u2 * m[2]) - left_hh
-    choose = sel_ref[...]
+    both = right_corners(meta, right_ref[0:depth], across)
+    left_both = right_corners(left_meta, mine_ref[0:depth], across)
+    fy = part_ref[1] + 0.5
+    fx = part_ref[0] + 0.5
+    e1 = DT * ((1.0 - fy) * fx)
+    e2 = DT * (fy * fx)
+    new_x = x_ref[...] + (e1 * both[0:n, 16:17] + e2 * both[n:, 16:17])
+    new_y = y_ref[...] + (e1 * both[0:n, 32:33] + e2 * both[n:, 32:33])
     gy = new_y + 0.5
     gx = new_x + 0.5
+    wy = w * gy
+    wo = w - wy
     sums = [
         meta[:, 10:11],
         meta[:, 11:12],
-        lane_sum(w * (1.0 - gy) * (1.0 - gx)),
-        lane_sum(w * gy * (1.0 - gx)),
-        lane_sum(w * (1.0 - gy) * gx),
-        lane_sum(w * gy * gx),
+        lane_sum(wo * (1.0 - gx)),
+        lane_sum(wy * (1.0 - gx)),
+        lane_sum(wo * gx),
+        lane_sum(wy * gx),
     ]
     lane = iota((n, 128), 1)
     lane16 = lane - 16.0 * jnp.floor(lane * 0.0625)
     mine = jnp.zeros((n, 128), F32)
     for i, value in enumerate(sums):
         mine = jnp.where(lane16 == float(i), value, mine)
-    over = left_meta[:, 11:12] == float(across - 1)
-    sums = [
-        left_meta[:, 10:11],
-        jnp.where(over, left_lh, 0.0),
-        jnp.where(over, left_hh, 0.0),
-    ]
-    theirs = jnp.zeros((n, 128), F32)
-    for i, value in enumerate(sums):
-        theirs = jnp.where(lane16 == float(8 + i), value, theirs)
+    facts = jnp.transpose(left_meta)
+    flows = jnp.transpose(left_both)
+    u1, u2 = flows[16:17, 0:n], flows[16:17, n:]
+    v1, v2 = flows[32:33, 0:n], flows[32:33, n:]
+    m = [facts[16 + i : 17 + i] for i in range(11)]
+    hh = (m[3] + u1 * m[4] + u2 * m[5] + v1 * m[6] + v2 * m[7]) + (
+        u1 * v1 * m[8] + (u1 * v2 + u2 * v1) * m[9] + u2 * v2 * m[10]
+    )
+    lh = (m[0] + u1 * m[1] + u2 * m[2]) - hh
+    over = facts[11:12] == float(across - 1)
+    line = iota((128, n), 0)
+    line16 = line - 16.0 * jnp.floor(line * 0.0625)
+    theirs = jnp.where(line16 == 8.0, facts[10:11], 0.0)
+    theirs = jnp.where(line16 == 9.0, jnp.where(over, lh, 0.0), theirs)
+    theirs = jnp.where(line16 == 10.0, jnp.where(over, hh, 0.0), theirs)
+    theirs = jnp.transpose(theirs)
+    choose = sel_ref[...]
     picked = mm(choose, stack3(jnp.concatenate([new_x, new_y, mine], axis=1)))
     for k in range(CAP):
         rows = slice(k * bands, (k + 1) * bands)
         for j, source in ((0, picked), (1, picked), (2, rw_ref), (3, rw_ref)):
             sl = slice(128 * (j % 2), 128 * (j % 2) + 128)
             out_ref[pl.ds(4 * k + j, bands, stride=step), :] = source[rows, sl]
-    slot = jnp.concatenate([to_row(left_meta[:, 12:13], n)] * 3, axis=1)
+    slot = jnp.concatenate([facts[12:13]] * 3, axis=1)
     d4 = iota((bands, 3 * n), 0) * float(CAP)
     theirs_choose = jnp.concatenate([one_hot(d4 + float(k) == slot) for k in range(CAP)], axis=0)
     chosen = picked[:, 256:] + mm(theirs_choose, stack3(theirs))
@@ -399,56 +402,38 @@
     copy = pltpu.make_async_copy(rows_ref.at[:, pl.ds(0, block)], moved_ref, sem)
     copy.start()
     table = recv_ref[pl.ds(block, bands, stride=step), :]
-    lanes = iota((bands, across), 1)
-    lane = iota((bands, 128), 1)
-    rows = iota((height, 2 * CAP * bands), 0)
-    spreads, values, spread_rows, value_rows = [], [], [], []
-    first_row = jnp.zeros((bands, across), F32)
-    corner = jnp.zeros((bands, 1), F32)
+    turned = jnp.transpose(table)
+    count = CAP * bands
+
+    def line(first, i):
+        return jnp.concatenate([turned[first + 16 * k + i : first + 16 * k + i + 1] for k in range(CAP)], axis=1)
+
+    r = iota((height, count), 0)
+    row, col, ll, hl, lh, hh = [line(0, i) for i in range(6)]
+    inside = col < float(across - 1)
+    at, under = r == row, r == row + 1.0
+    low = jnp.where(at, ll, jnp.where(under, hl, 0.0))
+    high = jnp.where(inside & at, lh, jnp.where(inside & under, hh, 0.0))
+    row, lh, hh = [line(0, 8 + i) for i in range(3)]
+    side = jnp.where(r == row, lh, jnp.where(r == row + 1.0, hh, 0.0))
+    row, col, _, hl, _, hh = [line(64, i) for i in range(6)]
+    top = (r == 0.0) & (row == float(height - 1))
+    low = jnp.concatenate([low, jnp.where(top, hl, 0.0)], axis=1)
+    high = jnp.concatenate([high, jnp.where(top & (col < float(across - 1)), hh, 0.0)], axis=1)
+    side = side + jnp.where((r == 0.0) & (line(64, 8) == float(height - 1)), line(64, 10), 0.0)
 
     def two(x):
         hi = x.astype(BF16)
-        return hi, (x - hi.astype(F32)).astype(BF16)
-
-    for k in range(CAP):
-        o = 16 * k
-        part = [table[:, o + i : o + i + 1] for i in range(11)]
-        row, col, ll, hl, lh, hh = part[0:6]
-        at0 = lanes == col
-        at1 = lanes == col + 1.0
-        spread = jnp.concatenate(
-            [
-                jnp.where(at0, ll, 0.0) + jnp.where(at1, lh, 0.0),
-                jnp.where(at0, hl, 0.0) + jnp.where(at1, hh, 0.0),
-            ],
-            axis=1,
-        )
-        spreads += two(spread)
-        spread_rows += [to_row(row, bands)] * 2
-        values += two(jnp.where(lane == 0.0, part[9], jnp.where(lane == 1.0, part[10], 0.0)))
-        value_rows += [to_row(part[8], bands)] * 2
-        o = 64 + 16 * k
-        part = [table[:, o + i : o + i + 1] for i in range(11)]
-        row, col, ll, hl, lh, hh = part[0:6]
-        edge = row == float(height - 1)
-        first_row = (
-            first_row
-            + jnp.where((lanes == col) & edge, hl, 0.0)
-            + jnp.where((lanes == col + 1.0) & edge, hh, 0.0)
-        )
-        corner = corner + jnp.where(part[8] == float(height - 1), part[10], 0.0)
-    total = mm(one_hot(rows == jnp.concatenate(spread_rows, axis=1)), jnp.concatenate(spreads, axis=0))
-    side = mm(one_hot(rows == jnp.concatenate(value_rows, axis=1)), jnp.concatenate(values, axis=0))
-    same = total[:, 0:across]
-    down = pltpu.roll(total[:, across:], 1, 0)
-    side_down = pltpu.roll(side, 1, 0)
-    r = iota((height, across), 0)
+        return [hi, (x - hi.astype(F32)).astype(BF16)]
+
+    lanes = iota((bands, across), 1)
+    places = [table[:, o + 16 * k + 1 : o + 16 * k + 2] for o in (0, 64) for k in range(CAP)]
+    spread = jnp.concatenate([one_hot(lanes == place) for place in places], axis=0)
+    total = mm(jnp.concatenate(two(low) + two(high), axis=0), spread)
+    same = total[0:height] + total[height : 2 * height]
+    right = total[2 * height : 3 * height] + total[3 * height :]
     c = iota((height, across), 1)
-    incoming = jnp.sum(first_row, axis=0, keepdims=True)
-    incoming = incoming + jnp.where(iota((1, across), 1) == 0.0, jnp.sum(corner), 0.0)
-    down = jnp.where(r == 0.0, incoming, down)
-    column = side[:, 0:1] + jnp.where(iota((height, 1), 0) == 0.0, 0.0, side_down[:, 1:2])
-    added = same + down + jnp.where(c == 0.0, column, 0.0)
+    added = same + jnp.where(c == 0.0, lane_sum(side), pltpu.roll(right, 1, 1))
     span = height + 24
     early = iota((16, 128), 0) < 9.0
     for j in range(across // 128):
@@ -481,28 +466,27 @@
     )
     below = lax.ppermute(head, "gy", ring("gy", -1))
     parts = jnp.transpose(particles, (1, 0, 2))
-    meta, weight, select, fixed = call(
+    meta, weight, near_x, near_y, select, fixed = call(
         prepare_body,
         (
-            sds((n, 128), F32),
-            sds((n, 128), F32),
+            *[sds((n, 128), F32)] * 4,
             sds((bands * CAP, 3 * n), BF16),
             sds((bands * CAP, 256), F32),
         ),
         velocity, parts, escaped, home_cell.reshape(1, n), land_cell.reshape(1, n), dest_rank.reshape(1, n),
         scalars=(block_count,),
     )
-    to_left, to_right, meta = call(
+    to_left, to_right, near_x, near_y = call(
         edges_body,
-        (sds((height + 24, 128), F32), sds((height + 24, 128), F32), sds((n, 128), F32)),
-        level_set, velocity, below, meta, parts, weight,
+        (*[sds((height + 24, 128), F32)] * 2, *[sds((n, 128), F32)] * 2),
+        level_set, velocity, below, meta, parts, weight, near_x, near_y,
     )
     from_left = lax.ppermute(to_right, "gx", ring("gx", 1))
     from_right = lax.ppermute(to_left, "gx", ring("gx", -1))
     (packed,) = call(
-        functools.partial(pack_body, height=height, across=across),
+        functools.partial(pack_body, across=across),
         (sds((bands * step, 128), F32),),
-        parts, weight, meta, to_left, from_left, from_right, select, fixed,
+        parts, weight, near_x, near_y, meta, to_left, from_left, from_right, select, fixed,
     )
     arrived = lax.all_to_all(
         packed.reshape(bands * step, 1, 128), "gy", split_axis=0, concat_axis=0, tiled=True

time: 58.1 us -> 57.3 us (0.986)
  Pallas kernels: 8.87 us -> 8.13 us
    pallas_call x6, Pallas kernels: 8.87 us -> 8.13 us  [call(): pl.pallas_call(body, out_shape=tuple(outs), in_specs=[spec(sm)] * len(sca...]
where the time goes in v7:
time: 57.3 us; the launch traced here: 57 us
  starting transfers between devices  27.1 us (47%)
  waiting for transfers between devices  19.6 us (34%)
  Pallas kernels  8.13 us (14%)
  between operations  1.43 us (2%)
  local copies, waits for them, and re-layouts  0.7 us (1%)
    ppermute x1, starting transfers between devices, shards(): below = lax.ppermute(head, 'gy', ring('gy', -1))  12.6 us
    ppermute x1, waiting for transfers between devices, shards(): first_rows = lax.ppermute(ahead, 'gy', ring('gy', 1))  11.8 us
    pallas_call x6, Pallas kernels, call(): pl.pallas_call(body, out_shape=tuple(outs), in_specs=[spec(sm)] * len(sca...  8.13 us
    all_to_all x1, starting transfers between devices, shards(): lax.all_to_all(packed.reshape(bands * step, 1, 128), 'gy', split_axis=0,...  5.96 us
    ppermute x1, waiting for transfers between devices, shards(): from_right = lax.ppermute(to_left, 'gx', ring('gx', -1))  5.21 us
    ppermute x1, starting transfers between devices, shards(): from_left = lax.ppermute(to_right, 'gx', ring('gx', 1))  4.7 us
    all_to_all x1, waiting for transfers between devices, shards(): lax.all_to_all(packed.reshape(bands * step, 1, 128), 'gy', split_axis=0,...  2.12 us
    ppermute x1, starting transfers between devices, shards(): first_rows = lax.ppermute(ahead, 'gy', ring('gy', 1))  1.96 us
  transfers between devices with their start and end apart: 5, of which 4 were waited for; matrix products, arithmetic and copies ran while one was open for 0% of the time, Pallas kernels for 6%

profile of v7, /device:TPU:24, one launch (start us, length us, event | category | flops | bytes accessed | tf_op | source)
XLA Modules:
  0.0 57.0 jit_solution(16998458785862532586)
XLA Ops:
  0.7 0.9 %shard_map.96 = f32[48,512]{1,0:T(8,128)S(1)} custom-call(f32[64,512]{1,0:T(8,128)} %f_ref.5, f32[2,64,512]{2,1,0:T(8,128)} %flow_ref.7), custom_call_target="tpu_custom_call" | custom-call | tf_op jit(solution)/shard_map/pallas_call | solution.py:62
  1.6 12.6 %collective-permute-start = (f32[48,512]{1,0:T(8,128)S(1)}, f32[48,512]{1,0:T(8,128)S(1)}, u32[]{:S(2)}, u32[]{:S(2)}) collective-permute-start(f32[48,512]{1,0:T(8,128)S(1)} %shard_map.96), channel_id=1, source_target_pairs={{0,504},{8,0},{16,8},{24,16},{32,24},{40,32},{48,40},{56,48},{64,5... | collective-permute-start | bytes 294920 | tf_op jit(solution)/shard_map/ppermute | solution.py:467
  14.8 0.0 copy-start.4
  14.9 0.0 copy-start.5
  14.9 0.0 copy-start.6
  14.9 0.0 copy-done
  14.9 0.6 %copy-done.4 = s32[64]{0:T(128)S(1)} copy-done((s32[64]{0:T(128)S(1)}, s32[64]{0:T(128)}, u32[]{:S(2)}) %copy-start.4) | copy-done | bytes 280
  15.5 0.0 copy-done.5
  15.5 0.0 copy-done.6
  15.5 0.4 shard_map.95
  16.0 0.4 collective-permute-done.below_ref
  16.4 0.0 copy-done.1
  16.4 0.4 shard_map.97
  16.8 4.7 %collective-permute-start.1 = (f32[88,128]{1,0:T(8,128)S(1)}, f32[88,128]{1,0:T(8,128)S(1)}, u32[]{:S(2)}, u32[]{:S(2)}) collective-permute-start(f32[88,128]{1,0:T(8,128)S(1)} %get-tuple-element.23), channel_id=1, source_target_pairs={{0,1},{1,2},{2,3},{3,4},{4,5},{5,6},{6,7},{7,0},{8,9},{9,10},{10,1... | collective-permute-start | bytes 135176 | tf_op jit(solution)/shard_map/ppermute | solution.py:484
  21.5 1.9 %collective-permute-start.2 = (f32[88,128]{1,0:T(8,128)S(1)}, f32[88,128]{1,0:T(8,128)S(1)}, u32[]{:S(2)}, u32[]{:S(2)}) collective-permute-start(f32[88,128]{1,0:T(8,128)S(1)} %get-tuple-element.22.mine_ref), channel_id=1, source_target_pairs={{0,7},{1,0},{2,1},{3,2},{4,3},{5,4},{6,5},{7,6},{8,15},{9,8},{10,9... | collective-permute-start | bytes 135176 | tf_op jit(solution)/shard_map/ppermute | solution.py:485
  23.5 0.0 collective-permute-done.1.left_ref
  23.5 5.2 %collective-permute-done.2.right_ref = f32[88,128]{1,0:T(8,128)S(1)} collective-permute-done((f32[88,128]{1,0:T(8,128)S(1)}, f32[88,128]{1,0:T(8,128)S(1)}, u32[]{:S(2)}, u32[]{:S(2)}) %collective-permute-start.2) | collective-permute-done | bytes 45088 | tf_op jit(solution)/shard_map/ppermute | solution.py:485
  28.7 1.7 %shard_map.98 = f32[1088,128]{1,0:T(8,128)} custom-call(f32[3,64,128]{2,1,0:T(8,128)S(1)} %bitcast.14, f32[64,128]{1,0:T(8,128)S(1)} %get-tuple-element.16.w_ref, f32[64,128]{1,0:T(8,128)S(1)} %get-tuple-element.20.x_ref, f32[64,128]{1,0:T(8,128)S(1)} %get-tuple-element.21.y_ref, f32[64,128]{1,0:T(8,128)S(1)} %get-tuple-element.17.meta_ref, ...), custom_call_target="tpu_custom_call" | custom-call | tf_op jit(solution)/shard_map/pallas_call | solution.py:62
  30.4 6.0 %all-to-all-start = ((f32[1088,1,128]{2,1,0:T(1,128)}), f32[1088,1,128]{2,1,0:T(1,128)S(1)}, u32[]{:S(2)}, u32[]{:S(2)}) async-start(f32[1088,1,128]{2,1,0:T(1,128)} %bitcast.5), calls=%async_computation | async-start | bytes 1114112 | tf_op jit(solution)/shard_map/all_to_all | solution.py:491
  36.3 3.3 %shard_map.99 = (f32[352,128]{1,0:T(8,128)S(1)}, f32[64,128]{1,0:T(8,128)S(1)}) custom-call(f32[64,512]{1,0:T(8,128)S(1)} %copy-done.1, f32[2,64,512]{2,1,0:T(8,128)S(1)} %copy-done, f32[48,512]{1,0:T(8,128)S(1)} %collective-permute-done.below_ref, f32[88,128]{1,0:T(8,128)S(1)} %collective-permute-done.2.right_ref, f32[88,128]{1,0:T(8,128)S(1)} %collective-permute-done.1.left_ref), custom_call_target="tpu_custom_call" | custom-call | tf_op jit(solution)/shard_map/pallas_call | solution.py:62
  39.6 2.0 %collective-permute-start.3 = (f32[64,128]{1,0:T(8,128)S(1)}, f32[64,128]{1,0:T(8,128)S(1)}, u32[]{:S(2)}, u32[]{:S(2)}) collective-permute-start(f32[64,128]{1,0:T(8,128)S(1)} %get-tuple-element.27), channel_id=1, source_target_pairs={{0,8},{8,16},{16,24},{24,32},{32,40},{40,48},{48,56},{56,64},{64,7... | collective-permute-start | bytes 98312 | tf_op jit(solution)/shard_map/ppermute | solution.py:502
  41.6 11.8 %collective-permute-done.3.first_ref = f32[64,128]{1,0:T(8,128)S(1)} collective-permute-done((f32[64,128]{1,0:T(8,128)S(1)}, f32[64,128]{1,0:T(8,128)S(1)}, u32[]{:S(2)}, u32[]{:S(2)}) %collective-permute-start.3) | collective-permute-done | bytes 32800 | tf_op jit(solution)/shard_map/ppermute | solution.py:502
  53.4 2.1 %all-to-all-done = f32[1088,1,128]{2,1,0:T(1,128)S(1)} async-done(((f32[1088,1,128]{2,1,0:T(1,128)}), f32[1088,1,128]{2,1,0:T(1,128)S(1)}, u32[]{:S(2)}, u32[]{:S(2)}) %all-to-all-start) | async-done | bytes 557088 | tf_op jit(solution)/shard_map/all_to_all | solution.py:491
  55.5 1.5 %shard_map.100 = (f32[64,512]{1,0:T(8,128)}, f32[64,16,1,128]{3,2,1,0:T(1,128)}) custom-call(f32[64,17,1,128]{3,2,1,0:T(1,128)S(1)} %bitcast.10, f32[1088,128]{1,0:T(8,128)S(1)} %bitcast.11, f32[352,128]{1,0:T(8,128)S(1)} %get-tuple-element.26.base_ref, f32[64,128]{1,0:T(8,128)S(1)} %collective-permute-done.3.first_ref), custom_call_target="tpu_custom_call" | custom-call | tf_op jit(solution)/shard_map/pallas_call | solution.py:62
  (6 shorter events, 0.0 us)
Async XLA Ops:
  0.6 14.2 %copy-start = (f32[2,64,512]{2,1,0:T(8,128)S(1)}, f32[2,64,512]{2,1,0:T(8,128)}, u32[]{:S(2)}) copy-start(f32[2,64,512]{2,1,0:T(8,128)} %flow_ref.7) | copy-start | bytes 786436
  0.6 14.2 %copy-start.3 = (s32[64,128]{1,0:T(8,128)S(1)}, s32[64,128]{1,0:T(8,128)}, u32[]{:S(2)}) copy-start(s32[64,128]{1,0:T(8,128)} %esc_ref.1) | copy-start | bytes 98308
  0.7 14.2 %copy-start.2 = (f32[64,3,128]{2,0,1:T(8,128)S(1)}, f32[64,3,128]{2,0,1:T(8,128)}, u32[]{:S(2)}) copy-start(f32[64,3,128]{2,0,1:T(8,128)} %param.10) | copy-start | bytes 294916
  1.6 14.8 %collective-permute-start = (f32[48,512]{1,0:T(8,128)S(1)}, f32[48,512]{1,0:T(8,128)S(1)}, u32[]{:S(2)}, u32[]{:S(2)}) collective-permute-start(f32[48,512]{1,0:T(8,128)S(1)} %shard_map.96), channel_id=1, source_target_pairs={{0,504},{8,0},{16,8},{24,16},{32,24},{40,32},{48,40},{56,48},{64,5... | collective-permute-start | bytes 294920 | tf_op jit(solution)/shard_map/ppermute | solution.py:467
  14.8 0.7 %copy-start.4 = (s32[64]{0:T(128)S(1)}, s32[64]{0:T(128)}, u32[]{:S(2)}) copy-start(s32[64]{0:T(128)} %param.12) | copy-start | bytes 772
  14.9 0.7 %copy-start.5 = (s32[64]{0:T(128)S(1)}, s32[64]{0:T(128)}, u32[]{:S(2)}) copy-start(s32[64]{0:T(128)} %param.13) | copy-start | bytes 772
  14.9 0.7 %copy-start.6 = (s32[64]{0:T(128)S(1)}, s32[64]{0:T(128)}, u32[]{:S(2)}) copy-start(s32[64]{0:T(128)} %param.14) | copy-start | bytes 772
  15.5 0.9 %copy-start.1 = (f32[64,512]{1,0:T(8,128)S(1)}, f32[64,512]{1,0:T(8,128)}, u32[]{:S(2)}) copy-start(f32[64,512]{1,0:T(8,128)} %f_ref.5) | copy-start | bytes 393220
  16.8 6.6 %collective-permute-start.1 = (f32[88,128]{1,0:T(8,128)S(1)}, f32[88,128]{1,0:T(8,128)S(1)}, u32[]{:S(2)}, u32[]{:S(2)}) collective-permute-start(f32[88,128]{1,0:T(8,128)S(1)} %get-tuple-element.23), channel_id=1, source_target_pairs={{0,1},{1,2},{2,3},{3,4},{4,5},{5,6},{6,7},{7,0},{8,9},{9,10},{10,1... | collective-permute-start | bytes 135176 | tf_op jit(solution)/shard_map/ppermute | solution.py:484
  21.5 7.2 %collective-permute-start.2 = (f32[88,128]{1,0:T(8,128)S(1)}, f32[88,128]{1,0:T(8,128)S(1)}, u32[]{:S(2)}, u32[]{:S(2)}) collective-permute-start(f32[88,128]{1,0:T(8,128)S(1)} %get-tuple-element.22.mine_ref), channel_id=1, source_target_pairs={{0,7},{1,0},{2,1},{3,2},{4,3},{5,4},{6,5},{7,6},{8,15},{9,8},{10,9... | collective-permute-start | bytes 135176 | tf_op jit(solution)/shard_map/ppermute | solution.py:485
  30.4 25.2 %all-to-all-start = ((f32[1088,1,128]{2,1,0:T(1,128)}), f32[1088,1,128]{2,1,0:T(1,128)S(1)}, u32[]{:S(2)}, u32[]{:S(2)}) async-start(f32[1088,1,128]{2,1,0:T(1,128)} %bitcast.5), calls=%async_computation | async-start | bytes 1114112 | tf_op jit(solution)/shard_map/all_to_all | solution.py:491
  39.6 13.8 %collective-permute-start.3 = (f32[64,128]{1,0:T(8,128)S(1)}, f32[64,128]{1,0:T(8,128)S(1)}, u32[]{:S(2)}, u32[]{:S(2)}) collective-permute-start(f32[64,128]{1,0:T(8,128)S(1)} %get-tuple-element.27), channel_id=1, source_target_pairs={{0,8},{8,16},{16,24},{24,32},{32,40},{40,48},{48,56},{56,64},{64,7... | collective-permute-start | bytes 98312 | tf_op jit(solution)/shard_map/ppermute | solution.py:502

commit v8 on v7

--- a/solution.py
+++ b/solution.py
@@ -94,6 +94,13 @@
     new_x = x + DT * (w00 * u[0] + w10 * u[1] + w01 * u[2] + w11 * u[3])
     new_y = y + DT * (w00 * v[0] + w10 * v[1] + w01 * v[2] + w11 * v[3])
     return new_x, new_y
+
+
+def put_rows(ref, picked, bands, step):
+    for k in range(CAP):
+        rows = slice(k * bands, (k + 1) * bands)
+        for j in range(2):
+            ref[pl.ds(CAP * j + k, bands, stride=step), :] = picked[rows, 128 * j : 128 * j + 128]
 
 
 def prepare_body(count_ref, flow_ref, part_ref, esc_ref, home_ref, land_ref, dest_ref, meta_ref, w_ref, x_ref, y_ref, sel_ref, rw_ref):
@@ -142,7 +149,7 @@
     k = floor_div(r, bands)
     choose = one_hot((r - k * bands) * CAP + k == jnp.concatenate([slot_row] * 3, axis=1))
     sel_ref[...] = choose
-    rw_ref[...] = mm(choose, stack3(jnp.concatenate([part_ref[2], w], axis=1)))
+    put_rows(rw_ref, mm(choose, stack3(jnp.concatenate([part_ref[2], w], axis=1))), bands, 2 * CAP)
 
 
 def pack_left(f, u, v):
@@ -230,12 +237,12 @@
     return jnp.sum(x, axis=1, keepdims=True)
 
 
-def pack_body(part_ref, w_ref, x_ref, y_ref, meta_ref, mine_ref, left_ref, right_ref, sel_ref, rw_ref, out_ref, across):
+def pack_body(part_ref, w_ref, x_ref, y_ref, meta_ref, mine_ref, left_ref, right_ref, sel_ref, out_ref, across):
     n = w_ref.shape[0]
-    bands = out_ref.shape[0] // (4 * CAP + 1)
+    bands = out_ref.shape[0] // (2 * CAP + 1)
     depth = right_ref.shape[0] - 16
     meta = meta_ref[...]
-    step = 4 * CAP + 1
+    step = 2 * CAP + 1
     w = w_ref[...]
     left_meta = left_ref[0:n]
     both = right_corners(meta, right_ref[0:depth], across)
@@ -281,11 +288,7 @@
     theirs = jnp.transpose(theirs)
     choose = sel_ref[...]
     picked = mm(choose, stack3(jnp.concatenate([new_x, new_y, mine], axis=1)))
-    for k in range(CAP):
-        rows = slice(k * bands, (k + 1) * bands)
-        for j, source in ((0, picked), (1, picked), (2, rw_ref), (3, rw_ref)):
-            sl = slice(128 * (j % 2), 128 * (j % 2) + 128)
-            out_ref[pl.ds(4 * k + j, bands, stride=step), :] = source[rows, sl]
+    put_rows(out_ref, picked, bands, step)
     slot = jnp.concatenate([facts[12:13]] * 3, axis=1)
     d4 = iota((bands, 3 * n), 0) * float(CAP)
     theirs_choose = jnp.concatenate([one_hot(d4 + float(k) == slot) for k in range(CAP)], axis=0)
@@ -296,7 +299,7 @@
     for k in range(CAP):
         table = jnp.where(group == float(k), chosen[k * bands : (k + 1) * bands], table)
     table = table + pltpu.roll(pltpu.roll(table, 1, 0), 64, 1)
-    out_ref[pl.ds(4 * CAP, bands, stride=step), :] = table
+    out_ref[pl.ds(2 * CAP, bands, stride=step), :] = table
 
 
 def side_term(speed, e0, e1, e2, e3, e4, d2, d3):
@@ -394,14 +397,17 @@
         next_ref[16 * j : 16 * j + 16] = out_ref[span * j + height : span * j + height + 16]
 
 
-def deposit_body(rows_ref, recv_ref, base_ref, first_ref, out_ref, moved_ref, sem):
+def deposit_body(fixed_ref, rows_ref, recv_ref, base_ref, first_ref, out_ref, moved_ref, sems):
     height, across = out_ref.shape
-    step = 4 * CAP + 1
+    step = 2 * CAP + 1
     bands = recv_ref.shape[0] // step
-    block = 4 * CAP
-    copy = pltpu.make_async_copy(rows_ref.at[:, pl.ds(0, block)], moved_ref, sem)
-    copy.start()
-    table = recv_ref[pl.ds(block, bands, stride=step), :]
+    copies = []
+    for j, source in enumerate((rows_ref, rows_ref, fixed_ref, fixed_ref)):
+        part = source.at[:, pl.ds(CAP * (j % 2), CAP)]
+        copies.append(pltpu.make_async_copy(part, moved_ref.at[:, :, j], sems.at[j]))
+    for copy in copies:
+        copy.start()
+    table = recv_ref[pl.ds(2 * CAP, bands, stride=step), :]
     turned = jnp.transpose(table)
     count = CAP * bands
 
@@ -442,7 +448,8 @@
         level = jnp.where(early, first_ref[16 * j : 16 * j + 16], base_ref[at : at + 16])
         out_ref[0:16, sl] = level + added[0:16, sl]
         out_ref[16:, sl] = base_ref[at + 16 : at + height] + added[16:, sl]
-    copy.wait()
+    for copy in copies:
+        copy.wait()
 
 
 def ring(axis, distance):
@@ -454,7 +461,7 @@
     height, across = level_set.shape
     n = particles.shape[0]
     bands = lax.axis_size("gy")
-    step = 4 * CAP + 1
+    step = 2 * CAP + 1
     sds = jax.ShapeDtypeStruct
     (head,) = call(
         heads_body,
@@ -471,10 +478,13 @@
         (
             *[sds((n, 128), F32)] * 4,
             sds((bands * CAP, 3 * n), BF16),
-            sds((bands * CAP, 256), F32),
+            sds((bands * 2 * CAP, 128), F32),
         ),
         velocity, parts, escaped, home_cell.reshape(1, n), land_cell.reshape(1, n), dest_rank.reshape(1, n),
         scalars=(block_count,),
+    )
+    settled = lax.all_to_all(
+        fixed.reshape(bands, 2 * CAP, 128), "gy", split_axis=0, concat_axis=0, tiled=True
     )
     to_left, to_right, near_x, near_y = call(
         edges_body,
@@ -486,7 +496,7 @@
     (packed,) = call(
         functools.partial(pack_body, across=across),
         (sds((bands * step, 128), F32),),
-        parts, weight, near_x, near_y, meta, to_left, from_left, from_right, select, fixed,
+        parts, weight, near_x, near_y, meta, to_left, from_left, from_right, select,
     )
     arrived = lax.all_to_all(
         packed.reshape(bands * step, 1, 128), "gy", split_axis=0, concat_axis=0, tiled=True
@@ -502,10 +512,10 @@
     first_rows = lax.ppermute(ahead, "gy", ring("gy", 1))
     level, moved = call(
         deposit_body,
-        (sds((height, across), F32), sds((bands, 4 * CAP, 1, 128), F32)),
-        arrived.reshape(bands, step, 1, 128), arrived.reshape(bands * step, 128), section, first_rows,
+        (sds((height, across), F32), sds((bands, CAP, 4, 1, 128), F32)),
+        settled.reshape(bands, 2 * CAP, 1, 128), arrived.reshape(bands, step, 1, 128), arrived.reshape(bands * step, 128), section, first_rows,
         out_spaces=[pltpu.VMEM, pltpu.HBM],
-        scratch=[pltpu.SemaphoreType.DMA],
+        scratch=[pltpu.SemaphoreType.DMA((4,))],
     )
     return level, moved.reshape(bands * CAP, 4, 128)
 

time: 57.3 us -> 65.7 us (1.15)
  the two profiles are of different devices: /device:TPU:24 before, /device:TPU:31 now
where the time goes in v8:
time: 65.7 us; the launch traced here: 65.2 us
  starting transfers between devices  35.5 us (54%)
  waiting for transfers between devices  16.2 us (25%)
  Pallas kernels  8.73 us (13%)
  local copies, waits for them, and re-layouts  3.28 us (5%)
  between operations  1.41 us (2%)
    all_to_all x1, starting transfers between devices, shards(): lax.all_to_all(fixed.reshape(bands, 2 * CAP, 128), 'gy', split_axis=0, co...  14.3 us
    all_to_all x1, starting transfers between devices, shards(): lax.all_to_all(packed.reshape(bands * step, 1, 128), 'gy', split_axis=0,...  9.2 us
    pallas_call x6, Pallas kernels, call(): pl.pallas_call(body, out_shape=tuple(outs), in_specs=[spec(sm)] * len(sca...  8.73 us
    ppermute x1, waiting for transfers between devices, shards(): below = lax.ppermute(head, 'gy', ring('gy', -1))  5.66 us
    all_to_all x1, waiting for transfers between devices, shards(): lax.all_to_all(packed.reshape(bands * step, 1, 128), 'gy', split_axis=0,...  4.79 us
    ppermute x1, waiting for transfers between devices, shards(): from_right = lax.ppermute(to_left, 'gx', ring('gx', -1))  4.78 us
    ppermute x1, starting transfers between devices, shards(): from_left = lax.ppermute(to_right, 'gx', ring('gx', 1))  4.42 us
    ppermute x1, starting transfers between devices, shards(): first_rows = lax.ppermute(ahead, 'gy', ring('gy', 1))  3.38 us
  transfers between devices with their start and end apart: 6, of which 4 were waited for; matrix products, arithmetic and copies ran while one was open for 0% of the time, Pallas kernels for 9%

profile of v8, /device:TPU:31, one launch (start us, length us, event | category | flops | bytes accessed | tf_op | source)
XLA Modules:
  0.0 65.2 jit_solution(15781320754928887382)
XLA Ops:
  1.3 0.6 copy-done.6
  1.9 0.0 copy-done.7
  1.9 0.0 copy-done.8
  2.0 0.9 %copy-done = f32[2,64,512]{2,1,0:T(8,128)S(1)} copy-done((f32[2,64,512]{2,1,0:T(8,128)S(1)}, f32[2,64,512]{2,1,0:T(8,128)}, u32[]{:S(2)}) %copy-start) | copy-done | bytes 262168
  2.9 0.9 %copy-done.3 = f32[64,3,128]{2,0,1:T(8,128)S(1)} copy-done((f32[64,3,128]{2,0,1:T(8,128)S(1)}, f32[64,3,128]{2,0,1:T(8,128)}, u32[]{:S(2)}) %copy-start.3) | copy-done | bytes 98328
  3.8 0.8 %copy-done.5 = s32[64,128]{1,0:T(8,128)S(1)} copy-done((s32[64,128]{1,0:T(8,128)S(1)}, s32[64,128]{1,0:T(8,128)}, u32[]{:S(2)}) %copy-start.5) | copy-done | bytes 32792
  4.6 1.1 %shard_map.95 = (f32[64,128]{1,0:T(8,128)S(1)}, f32[64,128]{1,0:T(8,128)S(1)}, f32[64,128]{1,0:T(8,128)S(1)}, f32[64,128]{1,0:T(8,128)S(1)}, bf16[256,192]{1,0:T(8,128)(2,1)S(1)}, /*index=5*/f32[512,128]{1,0:T(8,128)}) custom-call(s32[1]{0:T(128)S(6)} %copy.12.count_ref, f32[2,64,512]{2,1,0:T(8,128)S(1)} %copy-done, f32[3,64,128]{2,1,0:T(8,128)S(1)} %bitcast.15, ...), custom_call_target="tpu_custom_call" | custom-call | tf_op jit(solution)/shard_map/pallas_call | solution.py:62
  5.7 14.3 %all-to-all-start = ((f32[64,8,128]{2,1,0:T(8,128)}), f32[64,8,128]{2,1,0:T(8,128)S(1)}, u32[]{:S(2)}, u32[]{:S(2)}) async-start(f32[64,8,128]{2,1,0:T(8,128)} %bitcast.4), calls=%async_computation | async-start | bytes 524288 | tf_op jit(solution)/shard_map/all_to_all | solution.py:486
  20.0 0.0 copy-start.1
  20.0 0.0 copy-start.4
  20.0 0.9 %shard_map.96 = f32[48,512]{1,0:T(8,128)S(1)} custom-call(f32[64,512]{1,0:T(8,128)} %f_ref.5, f32[2,64,512]{2,1,0:T(8,128)} %flow_ref.7), custom_call_target="tpu_custom_call" | custom-call | tf_op jit(solution)/shard_map/pallas_call | solution.py:62
  21.0 2.3 %collective-permute-start = (f32[48,512]{1,0:T(8,128)S(1)}, f32[48,512]{1,0:T(8,128)S(1)}, u32[]{:S(2)}, u32[]{:S(2)}) collective-permute-start(f32[48,512]{1,0:T(8,128)S(1)} %shard_map.96), channel_id=1, source_target_pairs={{0,504},{8,0},{16,8},{24,16},{32,24},{40,32},{48,40},{56,48},{64,5... | collective-permute-start | bytes 294920 | tf_op jit(solution)/shard_map/ppermute | solution.py:474
  23.3 5.7 %collective-permute-done.below_ref = f32[48,512]{1,0:T(8,128)S(1)} collective-permute-done((f32[48,512]{1,0:T(8,128)S(1)}, f32[48,512]{1,0:T(8,128)S(1)}, u32[]{:S(2)}, u32[]{:S(2)}) %collective-permute-start) | collective-permute-done | bytes 98336 | tf_op jit(solution)/shard_map/ppermute | solution.py:474
  28.9 0.4 shard_map.97
  29.3 4.4 %collective-permute-start.1 = (f32[88,128]{1,0:T(8,128)S(1)}, f32[88,128]{1,0:T(8,128)S(1)}, u32[]{:S(2)}, u32[]{:S(2)}) collective-permute-start(f32[88,128]{1,0:T(8,128)S(1)} %get-tuple-element.24), channel_id=1, source_target_pairs={{0,1},{1,2},{2,3},{3,4},{4,5},{5,6},{6,7},{7,0},{8,9},{9,10},{10,1... | collective-permute-start | bytes 135176 | tf_op jit(solution)/shard_map/ppermute | solution.py:494
  33.8 1.9 %collective-permute-start.2 = (f32[88,128]{1,0:T(8,128)S(1)}, f32[88,128]{1,0:T(8,128)S(1)}, u32[]{:S(2)}, u32[]{:S(2)}) collective-permute-start(f32[88,128]{1,0:T(8,128)S(1)} %get-tuple-element.23.mine_ref), channel_id=1, source_target_pairs={{0,7},{1,0},{2,1},{3,2},{4,3},{5,4},{6,5},{7,6},{8,15},{9,8},{10,9... | collective-permute-start | bytes 135176 | tf_op jit(solution)/shard_map/ppermute | solution.py:495
  35.7 4.8 %collective-permute-done.2.right_ref = f32[88,128]{1,0:T(8,128)S(1)} collective-permute-done((f32[88,128]{1,0:T(8,128)S(1)}, f32[88,128]{1,0:T(8,128)S(1)}, u32[]{:S(2)}, u32[]{:S(2)}) %collective-permute-start.2) | collective-permute-done | bytes 45088 | tf_op jit(solution)/shard_map/ppermute | solution.py:495
  40.5 1.6 %shard_map.98 = f32[576,128]{1,0:T(8,128)} custom-call(f32[3,64,128]{2,1,0:T(8,128)S(1)} %bitcast.17, f32[64,128]{1,0:T(8,128)S(1)} %get-tuple-element.17.w_ref, f32[64,128]{1,0:T(8,128)S(1)} %get-tuple-element.21.x_ref, f32[64,128]{1,0:T(8,128)S(1)} %get-tuple-element.22.y_ref, f32[64,128]{1,0:T(8,128)S(1)} %get-tuple-element.18.meta_ref, ...), custom_call_target="tpu_custom_call" | custom-call | tf_op jit(solution)/shard_map/pallas_call | solution.py:62
  42.1 9.2 %all-to-all-start.1 = ((f32[576,1,128]{2,1,0:T(1,128)}), f32[576,1,128]{2,1,0:T(1,128)S(1)}, u32[]{:S(2)}, u32[]{:S(2)}) async-start(f32[576,1,128]{2,1,0:T(1,128)} %bitcast.7), calls=%async_computation.1 | async-start | bytes 589824 | tf_op jit(solution)/shard_map/all_to_all | solution.py:501
  51.3 3.3 %shard_map.99 = (f32[352,128]{1,0:T(8,128)S(1)}, f32[64,128]{1,0:T(8,128)S(1)}) custom-call(f32[64,512]{1,0:T(8,128)S(1)} %copy-done.2, f32[2,64,512]{2,1,0:T(8,128)S(1)} %copy-done.1, f32[48,512]{1,0:T(8,128)S(1)} %collective-permute-done.below_ref, f32[88,128]{1,0:T(8,128)S(1)} %collective-permute-done.2.right_ref, ...), custom_call_target="tpu_custom_call" | custom-call | tf_op jit(solution)/shard_map/pallas_call | solution.py:62
  54.5 3.4 %collective-permute-start.3 = (f32[64,128]{1,0:T(8,128)S(1)}, f32[64,128]{1,0:T(8,128)S(1)}, u32[]{:S(2)}, u32[]{:S(2)}) collective-permute-start(f32[64,128]{1,0:T(8,128)S(1)} %get-tuple-element.27), channel_id=1, source_target_pairs={{0,8},{8,16},{16,24},{24,32},{32,40},{40,48},{48,56},{56,64},{64,7... | collective-permute-start | bytes 98312 | tf_op jit(solution)/shard_map/ppermute | solution.py:512
  57.9 1.0 %collective-permute-done.3.first_ref = f32[64,128]{1,0:T(8,128)S(1)} collective-permute-done((f32[64,128]{1,0:T(8,128)S(1)}, f32[64,128]{1,0:T(8,128)S(1)}, u32[]{:S(2)}, u32[]{:S(2)}) %collective-permute-start.3) | collective-permute-done | bytes 32800 | tf_op jit(solution)/shard_map/ppermute | solution.py:512
  58.9 4.8 %all-to-all-done.1 = f32[576,1,128]{2,1,0:T(1,128)S(1)} async-done(((f32[576,1,128]{2,1,0:T(1,128)}), f32[576,1,128]{2,1,0:T(1,128)S(1)}, u32[]{:S(2)}, u32[]{:S(2)}) %all-to-all-start.1) | async-done | bytes 294944 | tf_op jit(solution)/shard_map/all_to_all | solution.py:501
  63.7 1.5 %shard_map.100 = (f32[64,512]{1,0:T(8,128)}, f32[64,4,4,1,128]{4,3,2,1,0:T(1,128)}) custom-call(f32[64,8,1,128]{3,2,1,0:T(1,128)S(1)} %bitcast.14, f32[64,9,1,128]{3,2,1,0:T(1,128)S(1)} %bitcast.12, f32[576,128]{1,0:T(8,128)S(1)} %bitcast.13, f32[352,128]{1,0:T(8,128)S(1)} %get-tuple-element.26.base_ref, f32[64,128]{1,0:T(8,128)S(1)} %collective-permute-done.3.first_ref), custom_call_target="tpu_custom_call" | custom-call | tf_op jit(solution)/shard_map/pallas_call | solution.py:62
  (12 shorter events, 0.0 us)
Async XLA Ops:
  1.3 0.7 %copy-start.6 = (s32[64]{0:T(128)S(1)}, s32[64]{0:T(128)}, u32[]{:S(2)}) copy-start(s32[64]{0:T(128)} %param.12) | copy-start | bytes 772
  1.3 0.7 %copy-start.7 = (s32[64]{0:T(128)S(1)}, s32[64]{0:T(128)}, u32[]{:S(2)}) copy-start(s32[64]{0:T(128)} %param.13) | copy-start | bytes 772
  1.3 0.7 %copy-start.8 = (s32[64]{0:T(128)S(1)}, s32[64]{0:T(128)}, u32[]{:S(2)}) copy-start(s32[64]{0:T(128)} %param.14) | copy-start | bytes 772
  2.0 0.9 %copy-start = (f32[2,64,512]{2,1,0:T(8,128)S(1)}, f32[2,64,512]{2,1,0:T(8,128)}, u32[]{:S(2)}) copy-start(f32[2,64,512]{2,1,0:T(8,128)} %flow_ref.7) | copy-start | bytes 786436
  2.9 0.9 %copy-start.3 = (f32[64,3,128]{2,0,1:T(8,128)S(1)}, f32[64,3,128]{2,0,1:T(8,128)}, u32[]{:S(2)}) copy-start(f32[64,3,128]{2,0,1:T(8,128)} %param.10) | copy-start | bytes 294916
  3.8 0.8 %copy-start.5 = (s32[64,128]{1,0:T(8,128)S(1)}, s32[64,128]{1,0:T(8,128)}, u32[]{:S(2)}) copy-start(s32[64,128]{1,0:T(8,128)} %esc_ref.1) | copy-start | bytes 98308
  5.7 36.4 %all-to-all-start = ((f32[64,8,128]{2,1,0:T(8,128)}), f32[64,8,128]{2,1,0:T(8,128)S(1)}, u32[]{:S(2)}, u32[]{:S(2)}) async-start(f32[64,8,128]{2,1,0:T(8,128)} %bitcast.4), calls=%async_computation | async-start | bytes 524288 | tf_op jit(solution)/shard_map/all_to_all | solution.py:486
  20.0 9.0 %copy-start.1 = (f32[2,64,512]{2,1,0:T(8,128)S(1)}, f32[2,64,512]{2,1,0:T(8,128)}, u32[]{:S(2)}) copy-start(f32[2,64,512]{2,1,0:T(8,128)} %flow_ref.7) | copy-start | bytes 786436
  20.0 8.9 %copy-start.2 = (f32[64,512]{1,0:T(8,128)S(1)}, f32[64,512]{1,0:T(8,128)}, u32[]{:S(2)}) copy-start(f32[64,512]{1,0:T(8,128)} %f_ref.5) | copy-start | bytes 393220
  20.0 8.9 %copy-start.4 = (f32[64,3,128]{2,0,1:T(8,128)S(1)}, f32[64,3,128]{2,0,1:T(8,128)}, u32[]{:S(2)}) copy-start(f32[64,3,128]{2,0,1:T(8,128)} %param.10) | copy-start | bytes 294916
  21.0 8.0 %collective-permute-start = (f32[48,512]{1,0:T(8,128)S(1)}, f32[48,512]{1,0:T(8,128)S(1)}, u32[]{:S(2)}, u32[]{:S(2)}) collective-permute-start(f32[48,512]{1,0:T(8,128)S(1)} %shard_map.96), channel_id=1, source_target_pairs={{0,504},{8,0},{16,8},{24,16},{32,24},{40,32},{48,40},{56,48},{64,5... | collective-permute-start | bytes 294920 | tf_op jit(solution)/shard_map/ppermute | solution.py:474
  29.3 6.4 %collective-permute-start.1 = (f32[88,128]{1,0:T(8,128)S(1)}, f32[88,128]{1,0:T(8,128)S(1)}, u32[]{:S(2)}, u32[]{:S(2)}) collective-permute-start(f32[88,128]{1,0:T(8,128)S(1)} %get-tuple-element.24), channel_id=1, source_target_pairs={{0,1},{1,2},{2,3},{3,4},{4,5},{5,6},{6,7},{7,0},{8,9},{9,10},{10,1... | collective-permute-start | bytes 135176 | tf_op jit(solution)/shard_map/ppermute | solution.py:494
  33.8 6.7 %collective-permute-start.2 = (f32[88,128]{1,0:T(8,128)S(1)}, f32[88,128]{1,0:T(8,128)S(1)}, u32[]{:S(2)}, u32[]{:S(2)}) collective-permute-start(f32[88,128]{1,0:T(8,128)S(1)} %get-tuple-element.23.mine_ref), channel_id=1, source_target_pairs={{0,7},{1,0},{2,1},{3,2},{4,3},{5,4},{6,5},{7,6},{8,15},{9,8},{10,9... | collective-permute-start | bytes 135176 | tf_op jit(solution)/shard_map/ppermute | solution.py:495
  42.1 21.6 %all-to-all-start.1 = ((f32[576,1,128]{2,1,0:T(1,128)}), f32[576,1,128]{2,1,0:T(1,128)S(1)}, u32[]{:S(2)}, u32[]{:S(2)}) async-start(f32[576,1,128]{2,1,0:T(1,128)} %bitcast.7), calls=%async_computation.1 | async-start | bytes 589824 | tf_op jit(solution)/shard_map/all_to_all | solution.py:501
  54.5 4.4 %collective-permute-start.3 = (f32[64,128]{1,0:T(8,128)S(1)}, f32[64,128]{1,0:T(8,128)S(1)}, u32[]{:S(2)}, u32[]{:S(2)}) collective-permute-start(f32[64,128]{1,0:T(8,128)S(1)} %get-tuple-element.27), channel_id=1, source_target_pairs={{0,8},{8,16},{16,24},{24,32},{32,40},{40,48},{48,56},{56,64},{64,7... | collective-permute-start | bytes 98312 | tf_op jit(solution)/shard_map/ppermute | solution.py:512

commit v9 on v7

--- a/solution.py
+++ b/solution.py
@@ -54,7 +54,7 @@
     return jnp.floor((x + 0.5) * (1.0 / k))
 
 
-def call(body, outs, *args, scratch=(), spaces=None, out_spaces=None, scalars=()):
+def call(body, outs, *args, scratch=(), spaces=None, out_spaces=None, scalars=(), aliases={}):
     vm, sm = pltpu.VMEM, pltpu.SMEM
     spaces = spaces or [vm] * len(args)
     out_spaces = out_spaces or [vm] * len(outs)
@@ -65,6 +65,7 @@
         in_specs=[spec(sm)] * len(scalars) + [spec(x) for x in spaces],
         out_specs=tuple(spec(x) for x in out_spaces),
         scratch_shapes=list(scratch),
+        input_output_aliases=aliases,
         compiler_params=pltpu.CompilerParams(vmem_limit_bytes=16 * 1024 * 1024),
         interpret=INTERPRET,
     )(*scalars, *args)
@@ -230,16 +231,13 @@
     return jnp.sum(x, axis=1, keepdims=True)
 
 
-def pack_body(part_ref, w_ref, x_ref, y_ref, meta_ref, mine_ref, left_ref, right_ref, sel_ref, rw_ref, out_ref, across):
+def pack_body(part_ref, w_ref, x_ref, y_ref, meta_ref, right_ref, sel_ref, rw_ref, out_ref, own_ref, across):
     n = w_ref.shape[0]
     bands = out_ref.shape[0] // (4 * CAP + 1)
-    depth = right_ref.shape[0] - 16
     meta = meta_ref[...]
     step = 4 * CAP + 1
     w = w_ref[...]
-    left_meta = left_ref[0:n]
-    both = right_corners(meta, right_ref[0:depth], across)
-    left_both = right_corners(left_meta, mine_ref[0:depth], across)
+    both = right_corners(meta, right_ref[0 : right_ref.shape[0] - 16], across)
     fy = part_ref[1] + 0.5
     fx = part_ref[0] + 0.5
     e1 = DT * ((1.0 - fy) * fx)
@@ -263,6 +261,20 @@
     mine = jnp.zeros((n, 128), F32)
     for i, value in enumerate(sums):
         mine = jnp.where(lane16 == float(i), value, mine)
+    picked = mm(sel_ref[...], stack3(jnp.concatenate([new_x, new_y, mine], axis=1)))
+    for k in range(CAP):
+        rows = slice(k * bands, (k + 1) * bands)
+        for j, source in ((0, picked), (1, picked), (2, rw_ref), (3, rw_ref)):
+            sl = slice(128 * (j % 2), 128 * (j % 2) + 128)
+            out_ref[pl.ds(4 * k + j, bands, stride=step), :] = source[rows, sl]
+    own_ref[...] = picked[:, 256:]
+
+
+def table_body(left_ref, mine_ref, own_ref, held_ref, out_ref, line_ref, sem, n, across):
+    del held_ref
+    bands = out_ref.shape[0]
+    left_meta = left_ref[0:n]
+    left_both = right_corners(left_meta, mine_ref[0 : mine_ref.shape[0] - 16], across)
     facts = jnp.transpose(left_meta)
     flows = jnp.transpose(left_both)
     u1, u2 = flows[16:17, 0:n], flows[16:17, n:]
@@ -279,24 +291,21 @@
     theirs = jnp.where(line16 == 9.0, jnp.where(over, lh, 0.0), theirs)
     theirs = jnp.where(line16 == 10.0, jnp.where(over, hh, 0.0), theirs)
     theirs = jnp.transpose(theirs)
-    choose = sel_ref[...]
-    picked = mm(choose, stack3(jnp.concatenate([new_x, new_y, mine], axis=1)))
-    for k in range(CAP):
-        rows = slice(k * bands, (k + 1) * bands)
-        for j, source in ((0, picked), (1, picked), (2, rw_ref), (3, rw_ref)):
-            sl = slice(128 * (j % 2), 128 * (j % 2) + 128)
-            out_ref[pl.ds(4 * k + j, bands, stride=step), :] = source[rows, sl]
     slot = jnp.concatenate([facts[12:13]] * 3, axis=1)
     d4 = iota((bands, 3 * n), 0) * float(CAP)
     theirs_choose = jnp.concatenate([one_hot(d4 + float(k) == slot) for k in range(CAP)], axis=0)
-    chosen = picked[:, 256:] + mm(theirs_choose, stack3(theirs))
+    chosen = own_ref[...] + mm(theirs_choose, stack3(theirs))
     lane = iota((bands, 128), 1)
     group = jnp.floor(lane * 0.0625)
+    group = jnp.where(group >= float(CAP), group - float(CAP), group)
     table = jnp.zeros((bands, 128), F32)
     for k in range(CAP):
         table = jnp.where(group == float(k), chosen[k * bands : (k + 1) * bands], table)
-    table = table + pltpu.roll(pltpu.roll(table, 1, 0), 64, 1)
-    out_ref[pl.ds(4 * CAP, bands, stride=step), :] = table
+    table = jnp.where(lane < 64.0, table, pltpu.roll(table, 1, 0))
+    line_ref[...] = table.reshape(bands, 1, 1, 128)
+    copy = pltpu.make_async_copy(line_ref, out_ref.at[:, pl.ds(4 * CAP, 1)], sem)
+    copy.start()
+    copy.wait()
 
 
 def side_term(speed, e0, e1, e2, e3, e4, d2, d3):
@@ -481,12 +490,22 @@
         (*[sds((height + 24, 128), F32)] * 2, *[sds((n, 128), F32)] * 2),
         level_set, velocity, below, meta, parts, weight, near_x, near_y,
     )
+    from_right = lax.ppermute(to_left, "gx", ring("gx", -1))
     from_left = lax.ppermute(to_right, "gx", ring("gx", 1))
-    from_right = lax.ppermute(to_left, "gx", ring("gx", -1))
+    packed, own = call(
+        functools.partial(pack_body, across=across),
+        (sds((bands * step, 128), F32), sds((bands * CAP, 128), F32)),
+        parts, weight, near_x, near_y, meta, from_right, select, fixed,
+    )
     (packed,) = call(
-        functools.partial(pack_body, across=across),
-        (sds((bands * step, 128), F32),),
-        parts, weight, near_x, near_y, meta, to_left, from_left, from_right, select, fixed,
+        functools.partial(table_body, n=n, across=across),
+        (pltpu.HBM((bands, step, 1, 128), F32),),
+        from_left, to_left, own,
+        pltpu.with_memory_space_constraint(packed.reshape(bands, step, 1, 128), pltpu.HBM),
+        spaces=[pltpu.VMEM] * 3 + [pltpu.HBM],
+        out_spaces=[pltpu.HBM],
+        scratch=[pltpu.VMEM((bands, 1, 1, 128), F32), pltpu.SemaphoreType.DMA],
+        aliases={3: 0},
     )
     arrived = lax.all_to_all(
         packed.reshape(bands * step, 1, 128), "gy", split_axis=0, concat_axis=0, tiled=True

time: 57.3 us -> 57.8 us (level)
  the two profiles are of different devices: /device:TPU:24 before, /device:TPU:1 now
where the time goes in v9:
time: 57.8 us; the launch traced here: 57.5 us
  starting transfers between devices  33 us (57%)
  waiting for transfers between devices  12.7 us (22%)
  Pallas kernels  8.37 us (14%)
  local copies, waits for them, and re-layouts  1.93 us (3%)
  between operations  1.46 us (3%)
    all_to_all x1, starting transfers between devices, shards(): lax.all_to_all(packed.reshape(bands * step, 1, 128), 'gy', split_axis=0,...  15.4 us
    ppermute x1, starting transfers between devices, shards(): below = lax.ppermute(head, 'gy', ring('gy', -1))  8.75 us
    pallas_call x7, Pallas kernels, call(): pl.pallas_call(body, out_shape=tuple(outs), in_specs=[spec(sm)] * len(sca...  8.37 us
    all_to_all x1, waiting for transfers between devices, shards(): lax.all_to_all(packed.reshape(bands * step, 1, 128), 'gy', split_axis=0,...  7.82 us
    ppermute x1, waiting for transfers between devices, shards(): first_rows = lax.ppermute(ahead, 'gy', ring('gy', 1))  3.66 us
    ppermute x1, starting transfers between devices, shards(): first_rows = lax.ppermute(ahead, 'gy', ring('gy', 1))  3.54 us
    ppermute x1, starting transfers between devices, shards(): from_left = lax.ppermute(to_right, 'gx', ring('gx', 1))  3.36 us
    unnamed x16, local copies, waits for them, and re-layouts  1.93 us
  transfers between devices with their start and end apart: 5, of which 3 were waited for; matrix products, arithmetic and copies ran while one was open for 0% of the time, Pallas kernels for 7%

profile of v9, /device:TPU:1, one launch (start us, length us, event | category | flops | bytes accessed | tf_op | source)
XLA Modules:
  0.0 57.5 jit_solution(14751021766264281350)
XLA Ops:
  0.7 0.9 %shard_map.95 = f32[48,512]{1,0:T(8,128)S(1)} custom-call(f32[64,512]{1,0:T(8,128)} %f_ref.5, f32[2,64,512]{2,1,0:T(8,128)} %flow_ref.7), custom_call_target="tpu_custom_call" | custom-call | tf_op jit(solution)/shard_map/pallas_call | solution.py:62
  1.6 8.7 %collective-permute-start = (f32[48,512]{1,0:T(8,128)S(1)}, f32[48,512]{1,0:T(8,128)S(1)}, u32[]{:S(2)}, u32[]{:S(2)}) collective-permute-start(f32[48,512]{1,0:T(8,128)S(1)} %shard_map.95), channel_id=1, source_target_pairs={{0,504},{8,0},{16,8},{24,16},{32,24},{40,32},{48,40},{56,48},{64,5... | collective-permute-start | bytes 294920 | tf_op jit(solution)/shard_map/ppermute | solution.py:476
  11.0 0.0 copy-start.5
  11.0 0.0 copy-start.6
  11.0 0.0 copy-start.7
  11.1 0.6 %copy-done.5 = s32[64]{0:T(128)S(1)} copy-done((s32[64]{0:T(128)S(1)}, s32[64]{0:T(128)}, u32[]{:S(2)}) %copy-start.5) | copy-done | bytes 280
  11.7 0.0 copy-done.6
  11.7 0.0 copy-done.7
  11.7 0.4 shard_map.96
  12.1 0.0 collective-permute-done.below_ref
  12.1 0.5 copy-done.2
  12.6 0.4 shard_map.97
  13.0 1.9 %collective-permute-start.2 = (f32[88,128]{1,0:T(8,128)S(1)}, f32[88,128]{1,0:T(8,128)S(1)}, u32[]{:S(2)}, u32[]{:S(2)}) collective-permute-start(f32[88,128]{1,0:T(8,128)S(1)} %get-tuple-element.23.mine_ref), channel_id=1, source_target_pairs={{0,7},{1,0},{2,1},{3,2},{4,3},{5,4},{6,5},{7,6},{8,15},{9,8},{10,9... | collective-permute-start | bytes 135176 | tf_op jit(solution)/shard_map/ppermute | solution.py:493
  14.9 3.4 %collective-permute-start.1 = (f32[88,128]{1,0:T(8,128)S(1)}, f32[88,128]{1,0:T(8,128)S(1)}, u32[]{:S(2)}, u32[]{:S(2)}) collective-permute-start(f32[88,128]{1,0:T(8,128)S(1)} %get-tuple-element.22), channel_id=1, source_target_pairs={{0,1},{1,2},{2,3},{3,4},{4,5},{5,6},{6,7},{7,0},{8,9},{9,10},{10,1... | collective-permute-start | bytes 135176 | tf_op jit(solution)/shard_map/ppermute | solution.py:494
  18.3 0.6 %shard_map.98 = (f32[1088,128]{1,0:T(8,128)S(1)}, f32[256,128]{1,0:T(8,128)S(1)}) custom-call(f32[3,64,128]{2,1,0:T(8,128)S(1)} %bitcast.17, f32[64,128]{1,0:T(8,128)S(1)} %get-tuple-element.19.w_ref, f32[64,128]{1,0:T(8,128)S(1)} %get-tuple-element.24.x_ref, f32[64,128]{1,0:T(8,128)S(1)} %get-tuple-element.25.y_ref, ...), custom_call_target="tpu_custom_call" | custom-call | tf_op jit(solution)/shard_map/pallas_call | solution.py:62
  18.9 0.8 %copy-done.1 = f32[1088,128]{1,0:T(8,128)} copy-done((f32[1088,128]{1,0:T(8,128)}, f32[1088,128]{1,0:T(8,128)S(1)}, u32[]{:S(2)}) %copy-start.1) | copy-done | bytes 557080
  19.7 1.2 %collective-permute-done.1.left_ref = f32[88,128]{1,0:T(8,128)S(1)} collective-permute-done((f32[88,128]{1,0:T(8,128)S(1)}, f32[88,128]{1,0:T(8,128)S(1)}, u32[]{:S(2)}, u32[]{:S(2)}) %collective-permute-start.1) | collective-permute-done | bytes 45088 | tf_op jit(solution)/shard_map/ppermute | solution.py:494
  20.9 1.3 %shard_map.99 = f32[64,17,1,128]{3,2,1,0:T(1,128)} custom-call(f32[88,128]{1,0:T(8,128)S(1)} %collective-permute-done.1.left_ref, f32[88,128]{1,0:T(8,128)S(1)} %get-tuple-element.23.mine_ref, f32[256,128]{1,0:T(8,128)S(1)} %get-tuple-element.28.own_ref, f32[64,17,1,128]{3,2,1,0:T(1,128)} %bitcast.13), custom_call_target="tpu_custom_call", output_to_operand_aliasing={{}: (3, {})} | custom-call | tf_op jit(solution)/shard_map/pallas_call | solution.py:62
  22.3 15.4 %all-to-all-start = ((f32[1088,1,128]{2,1,0:T(1,128)}), f32[1088,1,128]{2,1,0:T(1,128)S(1)}, u32[]{:S(2)}, u32[]{:S(2)}) async-start(f32[1088,1,128]{2,1,0:T(1,128)} %bitcast.14), calls=%async_computation | async-start | bytes 1114112 | tf_op jit(solution)/shard_map/all_to_all | solution.py:510
  37.7 3.3 %shard_map.100 = (f32[352,128]{1,0:T(8,128)S(1)}, f32[64,128]{1,0:T(8,128)S(1)}) custom-call(f32[64,512]{1,0:T(8,128)S(1)} %copy-done.2, f32[2,64,512]{2,1,0:T(8,128)S(1)} %copy-done, f32[48,512]{1,0:T(8,128)S(1)} %collective-permute-done.below_ref, f32[88,128]{1,0:T(8,128)S(1)} %collective-permute-done.2.right_ref, ...), custom_call_target="tpu_custom_call" | custom-call | tf_op jit(solution)/shard_map/pallas_call | solution.py:62
  41.0 3.5 %collective-permute-start.3 = (f32[64,128]{1,0:T(8,128)S(1)}, f32[64,128]{1,0:T(8,128)S(1)}, u32[]{:S(2)}, u32[]{:S(2)}) collective-permute-start(f32[64,128]{1,0:T(8,128)S(1)} %get-tuple-element.31), channel_id=1, source_target_pairs={{0,8},{8,16},{16,24},{24,32},{32,40},{40,48},{48,56},{56,64},{64,7... | collective-permute-start | bytes 98312 | tf_op jit(solution)/shard_map/ppermute | solution.py:521
  44.5 3.7 %collective-permute-done.3.first_ref = f32[64,128]{1,0:T(8,128)S(1)} collective-permute-done((f32[64,128]{1,0:T(8,128)S(1)}, f32[64,128]{1,0:T(8,128)S(1)}, u32[]{:S(2)}, u32[]{:S(2)}) %collective-permute-start.3) | collective-permute-done | bytes 32800 | tf_op jit(solution)/shard_map/ppermute | solution.py:521
  48.2 7.8 %all-to-all-done = f32[1088,1,128]{2,1,0:T(1,128)S(1)} async-done(((f32[1088,1,128]{2,1,0:T(1,128)}), f32[1088,1,128]{2,1,0:T(1,128)S(1)}, u32[]{:S(2)}, u32[]{:S(2)}) %all-to-all-start) | async-done | bytes 557088 | tf_op jit(solution)/shard_map/all_to_all | solution.py:510
  56.0 1.5 %shard_map.101 = (f32[64,512]{1,0:T(8,128)}, f32[64,16,1,128]{3,2,1,0:T(1,128)}) custom-call(f32[64,17,1,128]{3,2,1,0:T(1,128)S(1)} %bitcast.11, f32[1088,128]{1,0:T(8,128)S(1)} %bitcast.12, f32[352,128]{1,0:T(8,128)S(1)} %get-tuple-element.30.base_ref, f32[64,128]{1,0:T(8,128)S(1)} %collective-permute-done.3.first_ref), custom_call_target="tpu_custom_call" | custom-call | tf_op jit(solution)/shard_map/pallas_call | solution.py:62
  (9 shorter events, 0.0 us)
Async XLA Ops:
  0.6 10.4 %copy-start = (f32[2,64,512]{2,1,0:T(8,128)S(1)}, f32[2,64,512]{2,1,0:T(8,128)}, u32[]{:S(2)}) copy-start(f32[2,64,512]{2,1,0:T(8,128)} %flow_ref.7) | copy-start | bytes 786436
  0.6 10.4 %copy-start.3 = (f32[64,3,128]{2,0,1:T(8,128)S(1)}, f32[64,3,128]{2,0,1:T(8,128)}, u32[]{:S(2)}) copy-start(f32[64,3,128]{2,0,1:T(8,128)} %param.10) | copy-start | bytes 294916
  0.7 10.4 %copy-start.4 = (s32[64,128]{1,0:T(8,128)S(1)}, s32[64,128]{1,0:T(8,128)}, u32[]{:S(2)}) copy-start(s32[64,128]{1,0:T(8,128)} %esc_ref.1) | copy-start | bytes 98308
  1.6 10.5 %collective-permute-start = (f32[48,512]{1,0:T(8,128)S(1)}, f32[48,512]{1,0:T(8,128)S(1)}, u32[]{:S(2)}, u32[]{:S(2)}) collective-permute-start(f32[48,512]{1,0:T(8,128)S(1)} %shard_map.95), channel_id=1, source_target_pairs={{0,504},{8,0},{16,8},{24,16},{32,24},{40,32},{48,40},{56,48},{64,5... | collective-permute-start | bytes 294920 | tf_op jit(solution)/shard_map/ppermute | solution.py:476
  11.0 0.7 %copy-start.5 = (s32[64]{0:T(128)S(1)}, s32[64]{0:T(128)}, u32[]{:S(2)}) copy-start(s32[64]{0:T(128)} %param.12) | copy-start | bytes 772
  11.0 0.7 %copy-start.6 = (s32[64]{0:T(128)S(1)}, s32[64]{0:T(128)}, u32[]{:S(2)}) copy-start(s32[64]{0:T(128)} %param.13) | copy-start | bytes 772
  11.0 0.7 %copy-start.7 = (s32[64]{0:T(128)S(1)}, s32[64]{0:T(128)}, u32[]{:S(2)}) copy-start(s32[64]{0:T(128)} %param.14) | copy-start | bytes 772
  11.7 0.9 %copy-start.2 = (f32[64,512]{1,0:T(8,128)S(1)}, f32[64,512]{1,0:T(8,128)}, u32[]{:S(2)}) copy-start(f32[64,512]{1,0:T(8,128)} %f_ref.5) | copy-start | bytes 393220
  13.0 5.3 %collective-permute-start.2 = (f32[88,128]{1,0:T(8,128)S(1)}, f32[88,128]{1,0:T(8,128)S(1)}, u32[]{:S(2)}, u32[]{:S(2)}) collective-permute-start(f32[88,128]{1,0:T(8,128)S(1)} %get-tuple-element.23.mine_ref), channel_id=1, source_target_pairs={{0,7},{1,0},{2,1},{3,2},{4,3},{5,4},{6,5},{7,6},{8,15},{9,8},{10,9... | collective-permute-start | bytes 135176 | tf_op jit(solution)/shard_map/ppermute | solution.py:493
  14.9 6.0 %collective-permute-start.1 = (f32[88,128]{1,0:T(8,128)S(1)}, f32[88,128]{1,0:T(8,128)S(1)}, u32[]{:S(2)}, u32[]{:S(2)}) collective-permute-start(f32[88,128]{1,0:T(8,128)S(1)} %get-tuple-element.22), channel_id=1, source_target_pairs={{0,1},{1,2},{2,3},{3,4},{4,5},{5,6},{6,7},{7,0},{8,9},{9,10},{10,1... | collective-permute-start | bytes 135176 | tf_op jit(solution)/shard_map/ppermute | solution.py:494
  18.9 0.8 %copy-start.1 = (f32[1088,128]{1,0:T(8,128)}, f32[1088,128]{1,0:T(8,128)S(1)}, u32[]{:S(2)}) copy-start(f32[1088,128]{1,0:T(8,128)S(1)} %get-tuple-element.29) | copy-start | bytes 1671172
  22.3 33.7 %all-to-all-start = ((f32[1088,1,128]{2,1,0:T(1,128)}), f32[1088,1,128]{2,1,0:T(1,128)S(1)}, u32[]{:S(2)}, u32[]{:S(2)}) async-start(f32[1088,1,128]{2,1,0:T(1,128)} %bitcast.14), calls=%async_computation | async-start | bytes 1114112 | tf_op jit(solution)/shard_map/all_to_all | solution.py:510
  41.0 7.2 %collective-permute-start.3 = (f32[64,128]{1,0:T(8,128)S(1)}, f32[64,128]{1,0:T(8,128)S(1)}, u32[]{:S(2)}, u32[]{:S(2)}) collective-permute-start(f32[64,128]{1,0:T(8,128)S(1)} %get-tuple-element.31), channel_id=1, source_target_pairs={{0,8},{8,16},{16,24},{24,32},{32,40},{40,48},{48,56},{56,64},{64,7... | collective-permute-start | bytes 98312 | tf_op jit(solution)/shard_map/ppermute | solution.py:521

commit v10 on v7

--- a/solution.py
+++ b/solution.py
@@ -230,16 +230,40 @@
     return jnp.sum(x, axis=1, keepdims=True)
 
 
-def pack_body(part_ref, w_ref, x_ref, y_ref, meta_ref, mine_ref, left_ref, right_ref, sel_ref, rw_ref, out_ref, across):
+def side_body(left_ref, mine_ref, side_ref, n, across):
+    bands = side_ref.shape[0] // CAP
+    left_meta = left_ref[0:n]
+    left_both = right_corners(left_meta, mine_ref[0 : mine_ref.shape[0] - 16], across)
+    facts = jnp.transpose(left_meta)
+    flows = jnp.transpose(left_both)
+    u1, u2 = flows[16:17, 0:n], flows[16:17, n:]
+    v1, v2 = flows[32:33, 0:n], flows[32:33, n:]
+    m = [facts[16 + i : 17 + i] for i in range(11)]
+    hh = (m[3] + u1 * m[4] + u2 * m[5] + v1 * m[6] + v2 * m[7]) + (
+        u1 * v1 * m[8] + (u1 * v2 + u2 * v1) * m[9] + u2 * v2 * m[10]
+    )
+    lh = (m[0] + u1 * m[1] + u2 * m[2]) - hh
+    over = facts[11:12] == float(across - 1)
+    line = iota((128, n), 0)
+    line16 = line - 16.0 * jnp.floor(line * 0.0625)
+    theirs = jnp.where(line16 == 8.0, facts[10:11], 0.0)
+    theirs = jnp.where(line16 == 9.0, jnp.where(over, lh, 0.0), theirs)
+    theirs = jnp.where(line16 == 10.0, jnp.where(over, hh, 0.0), theirs)
+    theirs = jnp.transpose(theirs)
+    slot = jnp.concatenate([facts[12:13]] * 3, axis=1)
+    d4 = iota((bands, 3 * n), 0) * float(CAP)
+    choose = jnp.concatenate([one_hot(d4 + float(k) == slot) for k in range(CAP)], axis=0)
+    side_ref[...] = mm(choose, stack3(theirs))
+
+
+def pack_body(part_ref, w_ref, x_ref, y_ref, meta_ref, right_ref, sel_ref, rw_ref, side_ref, out_ref, across):
     n = w_ref.shape[0]
     bands = out_ref.shape[0] // (4 * CAP + 1)
     depth = right_ref.shape[0] - 16
     meta = meta_ref[...]
     step = 4 * CAP + 1
     w = w_ref[...]
-    left_meta = left_ref[0:n]
     both = right_corners(meta, right_ref[0:depth], across)
-    left_both = right_corners(left_meta, mine_ref[0:depth], across)
     fy = part_ref[1] + 0.5
     fx = part_ref[0] + 0.5
     e1 = DT * ((1.0 - fy) * fx)
@@ -263,22 +287,6 @@
     mine = jnp.zeros((n, 128), F32)
     for i, value in enumerate(sums):
         mine = jnp.where(lane16 == float(i), value, mine)
-    facts = jnp.transpose(left_meta)
-    flows = jnp.transpose(left_both)
-    u1, u2 = flows[16:17, 0:n], flows[16:17, n:]
-    v1, v2 = flows[32:33, 0:n], flows[32:33, n:]
-    m = [facts[16 + i : 17 + i] for i in range(11)]
-    hh = (m[3] + u1 * m[4] + u2 * m[5] + v1 * m[6] + v2 * m[7]) + (
-        u1 * v1 * m[8] + (u1 * v2 + u2 * v1) * m[9] + u2 * v2 * m[10]
-    )
-    lh = (m[0] + u1 * m[1] + u2 * m[2]) - hh
-    over = facts[11:12] == float(across - 1)
-    line = iota((128, n), 0)
-    line16 = line - 16.0 * jnp.floor(line * 0.0625)
-    theirs = jnp.where(line16 == 8.0, facts[10:11], 0.0)
-    theirs = jnp.where(line16 == 9.0, jnp.where(over, lh, 0.0), theirs)
-    theirs = jnp.where(line16 == 10.0, jnp.where(over, hh, 0.0), theirs)
-    theirs = jnp.transpose(theirs)
     choose = sel_ref[...]
     picked = mm(choose, stack3(jnp.concatenate([new_x, new_y, mine], axis=1)))
     for k in range(CAP):
@@ -286,16 +294,14 @@
         for j, source in ((0, picked), (1, picked), (2, rw_ref), (3, rw_ref)):
             sl = slice(128 * (j % 2), 128 * (j % 2) + 128)
             out_ref[pl.ds(4 * k + j, bands, stride=step), :] = source[rows, sl]
-    slot = jnp.concatenate([facts[12:13]] * 3, axis=1)
-    d4 = iota((bands, 3 * n), 0) * float(CAP)
-    theirs_choose = jnp.concatenate([one_hot(d4 + float(k) == slot) for k in range(CAP)], axis=0)
-    chosen = picked[:, 256:] + mm(theirs_choose, stack3(theirs))
+    chosen = picked[:, 256:] + side_ref[...]
     lane = iota((bands, 128), 1)
     group = jnp.floor(lane * 0.0625)
+    group = jnp.where(group >= float(CAP), group - float(CAP), group)
     table = jnp.zeros((bands, 128), F32)
     for k in range(CAP):
         table = jnp.where(group == float(k), chosen[k * bands : (k + 1) * bands], table)
-    table = table + pltpu.roll(pltpu.roll(table, 1, 0), 64, 1)
+    table = jnp.where(lane < 64.0, table, pltpu.roll(table, 1, 0))
     out_ref[pl.ds(4 * CAP, bands, stride=step), :] = table
 
 
@@ -483,10 +489,15 @@
     )
     from_left = lax.ppermute(to_right, "gx", ring("gx", 1))
     from_right = lax.ppermute(to_left, "gx", ring("gx", -1))
+    (side,) = call(
+        functools.partial(side_body, n=n, across=across),
+        (sds((bands * CAP, 128), F32),),
+        from_left, to_left,
+    )
     (packed,) = call(
         functools.partial(pack_body, across=across),
         (sds((bands * step, 128), F32),),
-        parts, weight, near_x, near_y, meta, to_left, from_left, from_right, select, fixed,
+        parts, weight, near_x, near_y, meta, from_right, select, fixed, side,
     )
     arrived = lax.all_to_all(
         packed.reshape(bands * step, 1, 128), "gy", split_axis=0, concat_axis=0, tiled=True

time: 57.3 us -> 57.1 us (level)
  waiting for transfers between devices: 19.6 us -> 18.9 us
    ppermute x1, waiting for transfers between devices: 5.21 us -> 4.52 us  [shards(): from_right = lax.ppermute(to_left, 'gx', ring('gx', -1))]
    pallas_call x6 -> x7, Pallas kernels: 8.13 us -> 8.54 us  [call(): pl.pallas_call(body, out_shape=tuple(outs), in_specs=[spec(sm)] * len(sca...]
  transfers between devices with their start and end apart: 5 -> 5, of which waited for: 4 -> 4; matrix products, arithmetic and copies ran while one was open for 0% -> 0% of each run, Pallas kernels for 6% -> 8%
where the time goes in v10:
time: 57.1 us; the launch traced here: 56.7 us
  starting transfers between devices  27.1 us (47%)
  waiting for transfers between devices  18.9 us (33%)
  Pallas kernels  8.54 us (15%)
  between operations  1.44 us (3%)
  local copies, waits for them, and re-layouts  0.7 us (1%)
    ppermute x1, starting transfers between devices, shards(): below = lax.ppermute(head, 'gy', ring('gy', -1))  12.6 us
    ppermute x1, waiting for transfers between devices, shards(): first_rows = lax.ppermute(ahead, 'gy', ring('gy', 1))  11.8 us
    pallas_call x7, Pallas kernels, call(): pl.pallas_call(body, out_shape=tuple(outs), in_specs=[spec(sm)] * len(sca...  8.54 us
    all_to_all x1, starting transfers between devices, shards(): lax.all_to_all(packed.reshape(bands * step, 1, 128), 'gy', split_axis=0,...  5.96 us
    ppermute x1, starting transfers between devices, shards(): from_left = lax.ppermute(to_right, 'gx', ring('gx', 1))  4.7 us
    ppermute x1, waiting for transfers between devices, shards(): from_right = lax.ppermute(to_left, 'gx', ring('gx', -1))  4.52 us
    all_to_all x1, waiting for transfers between devices, shards(): lax.all_to_all(packed.reshape(bands * step, 1, 128), 'gy', split_axis=0,...  2.12 us
    ppermute x1, starting transfers between devices, shards(): first_rows = lax.ppermute(ahead, 'gy', ring('gy', 1))  1.96 us
  transfers between devices with their start and end apart: 5, of which 4 were waited for; matrix products, arithmetic and copies ran while one was open for 0% of the time, Pallas kernels for 8%

profile of v10, /device:TPU:24, one launch (start us, length us, event | category | flops | bytes accessed | tf_op | source)
XLA Modules:
  0.0 56.7 jit_solution(3623381882187373634)
XLA Ops:
  0.7 0.9 %shard_map.96 = f32[48,512]{1,0:T(8,128)S(1)} custom-call(f32[64,512]{1,0:T(8,128)} %f_ref.5, f32[2,64,512]{2,1,0:T(8,128)} %flow_ref.7), custom_call_target="tpu_custom_call" | custom-call | tf_op jit(solution)/shard_map/pallas_call | solution.py:62
  1.6 12.6 %collective-permute-start = (f32[48,512]{1,0:T(8,128)S(1)}, f32[48,512]{1,0:T(8,128)S(1)}, u32[]{:S(2)}, u32[]{:S(2)}) collective-permute-start(f32[48,512]{1,0:T(8,128)S(1)} %shard_map.96), channel_id=1, source_target_pairs={{0,504},{8,0},{16,8},{24,16},{32,24},{40,32},{48,40},{56,48},{64,5... | collective-permute-start | bytes 294920 | tf_op jit(solution)/shard_map/ppermute | solution.py:473
  14.8 0.0 copy-start.4
  14.9 0.0 copy-start.5
  14.9 0.0 copy-start.6
  14.9 0.6 %copy-done.4 = s32[64]{0:T(128)S(1)} copy-done((s32[64]{0:T(128)S(1)}, s32[64]{0:T(128)}, u32[]{:S(2)}) %copy-start.4) | copy-done | bytes 280
  15.5 0.0 copy-done.5
  15.5 0.0 copy-done.6
  15.5 0.4 shard_map.95
  16.0 0.4 collective-permute-done.below_ref
  16.4 0.0 copy-done.1
  16.4 0.4 shard_map.97
  16.8 4.7 %collective-permute-start.2 = (f32[88,128]{1,0:T(8,128)S(1)}, f32[88,128]{1,0:T(8,128)S(1)}, u32[]{:S(2)}, u32[]{:S(2)}) collective-permute-start(f32[88,128]{1,0:T(8,128)S(1)} %get-tuple-element.25), channel_id=1, source_target_pairs={{0,1},{1,2},{2,3},{3,4},{4,5},{5,6},{6,7},{7,0},{8,9},{9,10},{10,1... | collective-permute-start | bytes 135176 | tf_op jit(solution)/shard_map/ppermute | solution.py:490
  21.5 1.9 %collective-permute-start.1 = (f32[88,128]{1,0:T(8,128)S(1)}, f32[88,128]{1,0:T(8,128)S(1)}, u32[]{:S(2)}, u32[]{:S(2)}) collective-permute-start(f32[88,128]{1,0:T(8,128)S(1)} %get-tuple-element.22.mine_ref), channel_id=1, source_target_pairs={{0,7},{1,0},{2,1},{3,2},{4,3},{5,4},{6,5},{7,6},{8,15},{9,8},{10,9... | collective-permute-start | bytes 135176 | tf_op jit(solution)/shard_map/ppermute | solution.py:491
  23.5 0.0 collective-permute-done.2.left_ref
  23.5 0.7 %shard_map.98.side_ref = f32[256,128]{1,0:T(8,128)S(1)} custom-call(f32[88,128]{1,0:T(8,128)S(1)} %collective-permute-done.2.left_ref, f32[88,128]{1,0:T(8,128)S(1)} %get-tuple-element.22.mine_ref), custom_call_target="tpu_custom_call" | custom-call | tf_op jit(solution)/shard_map/pallas_call | solution.py:62
  24.2 4.5 %collective-permute-done.1.right_ref = f32[88,128]{1,0:T(8,128)S(1)} collective-permute-done((f32[88,128]{1,0:T(8,128)S(1)}, f32[88,128]{1,0:T(8,128)S(1)}, u32[]{:S(2)}, u32[]{:S(2)}) %collective-permute-start.1) | collective-permute-done | bytes 45088 | tf_op jit(solution)/shard_map/ppermute | solution.py:491
  28.7 1.4 %shard_map.99 = f32[1088,128]{1,0:T(8,128)} custom-call(f32[3,64,128]{2,1,0:T(8,128)S(1)} %bitcast.14, f32[64,128]{1,0:T(8,128)S(1)} %get-tuple-element.16.w_ref, f32[64,128]{1,0:T(8,128)S(1)} %get-tuple-element.20.x_ref, f32[64,128]{1,0:T(8,128)S(1)} %get-tuple-element.21.y_ref, f32[64,128]{1,0:T(8,128)S(1)} %get-tuple-element.17.meta_ref, ...), custom_call_target="tpu_custom_call" | custom-call | tf_op jit(solution)/shard_map/pallas_call | solution.py:62
  30.1 6.0 %all-to-all-start = ((f32[1088,1,128]{2,1,0:T(1,128)}), f32[1088,1,128]{2,1,0:T(1,128)S(1)}, u32[]{:S(2)}, u32[]{:S(2)}) async-start(f32[1088,1,128]{2,1,0:T(1,128)} %bitcast.5), calls=%async_computation | async-start | bytes 1114112 | tf_op jit(solution)/shard_map/all_to_all | solution.py:502
  36.1 3.3 %shard_map.100 = (f32[352,128]{1,0:T(8,128)S(1)}, f32[64,128]{1,0:T(8,128)S(1)}) custom-call(f32[64,512]{1,0:T(8,128)S(1)} %copy-done.1, f32[2,64,512]{2,1,0:T(8,128)S(1)} %copy-done, f32[48,512]{1,0:T(8,128)S(1)} %collective-permute-done.below_ref, f32[88,128]{1,0:T(8,128)S(1)} %collective-permute-done.1.right_ref, ...), custom_call_target="tpu_custom_call" | custom-call | tf_op jit(solution)/shard_map/pallas_call | solution.py:62
  39.3 2.0 %collective-permute-start.3 = (f32[64,128]{1,0:T(8,128)S(1)}, f32[64,128]{1,0:T(8,128)S(1)}, u32[]{:S(2)}, u32[]{:S(2)}) collective-permute-start(f32[64,128]{1,0:T(8,128)S(1)} %get-tuple-element.27), channel_id=1, source_target_pairs={{0,8},{8,16},{16,24},{24,32},{32,40},{40,48},{48,56},{56,64},{64,7... | collective-permute-start | bytes 98312 | tf_op jit(solution)/shard_map/ppermute | solution.py:513
  41.3 11.8 %collective-permute-done.3.first_ref = f32[64,128]{1,0:T(8,128)S(1)} collective-permute-done((f32[64,128]{1,0:T(8,128)S(1)}, f32[64,128]{1,0:T(8,128)S(1)}, u32[]{:S(2)}, u32[]{:S(2)}) %collective-permute-start.3) | collective-permute-done | bytes 32800 | tf_op jit(solution)/shard_map/ppermute | solution.py:513
  53.1 2.1 %all-to-all-done = f32[1088,1,128]{2,1,0:T(1,128)S(1)} async-done(((f32[1088,1,128]{2,1,0:T(1,128)}), f32[1088,1,128]{2,1,0:T(1,128)S(1)}, u32[]{:S(2)}, u32[]{:S(2)}) %all-to-all-start) | async-done | bytes 557088 | tf_op jit(solution)/shard_map/all_to_all | solution.py:502
  55.3 1.5 %shard_map.101 = (f32[64,512]{1,0:T(8,128)}, f32[64,16,1,128]{3,2,1,0:T(1,128)}) custom-call(f32[64,17,1,128]{3,2,1,0:T(1,128)S(1)} %bitcast.10, f32[1088,128]{1,0:T(8,128)S(1)} %bitcast.11, f32[352,128]{1,0:T(8,128)S(1)} %get-tuple-element.26.base_ref, f32[64,128]{1,0:T(8,128)S(1)} %collective-permute-done.3.first_ref), custom_call_target="tpu_custom_call" | custom-call | tf_op jit(solution)/shard_map/pallas_call | solution.py:62
  (7 shorter events, 0.0 us)
Async XLA Ops:
  0.6 14.2 %copy-start = (f32[2,64,512]{2,1,0:T(8,128)S(1)}, f32[2,64,512]{2,1,0:T(8,128)}, u32[]{:S(2)}) copy-start(f32[2,64,512]{2,1,0:T(8,128)} %flow_ref.7) | copy-start | bytes 786436
  0.6 14.2 %copy-start.2 = (f32[64,3,128]{2,0,1:T(8,128)S(1)}, f32[64,3,128]{2,0,1:T(8,128)}, u32[]{:S(2)}) copy-start(f32[64,3,128]{2,0,1:T(8,128)} %param.10) | copy-start | bytes 294916
  0.7 14.2 %copy-start.3 = (s32[64,128]{1,0:T(8,128)S(1)}, s32[64,128]{1,0:T(8,128)}, u32[]{:S(2)}) copy-start(s32[64,128]{1,0:T(8,128)} %esc_ref.1) | copy-start | bytes 98308
  1.6 14.8 %collective-permute-start = (f32[48,512]{1,0:T(8,128)S(1)}, f32[48,512]{1,0:T(8,128)S(1)}, u32[]{:S(2)}, u32[]{:S(2)}) collective-permute-start(f32[48,512]{1,0:T(8,128)S(1)} %shard_map.96), channel_id=1, source_target_pairs={{0,504},{8,0},{16,8},{24,16},{32,24},{40,32},{48,40},{56,48},{64,5... | collective-permute-start | bytes 294920 | tf_op jit(solution)/shard_map/ppermute | solution.py:473
  14.8 0.7 %copy-start.4 = (s32[64]{0:T(128)S(1)}, s32[64]{0:T(128)}, u32[]{:S(2)}) copy-start(s32[64]{0:T(128)} %param.12) | copy-start | bytes 772
  14.9 0.7 %copy-start.5 = (s32[64]{0:T(128)S(1)}, s32[64]{0:T(128)}, u32[]{:S(2)}) copy-start(s32[64]{0:T(128)} %param.13) | copy-start | bytes 772
  14.9 0.7 %copy-start.6 = (s32[64]{0:T(128)S(1)}, s32[64]{0:T(128)}, u32[]{:S(2)}) copy-start(s32[64]{0:T(128)} %param.14) | copy-start | bytes 772
  15.5 0.9 %copy-start.1 = (f32[64,512]{1,0:T(8,128)S(1)}, f32[64,512]{1,0:T(8,128)}, u32[]{:S(2)}) copy-start(f32[64,512]{1,0:T(8,128)} %f_ref.5) | copy-start | bytes 393220
  16.8 6.6 %collective-permute-start.2 = (f32[88,128]{1,0:T(8,128)S(1)}, f32[88,128]{1,0:T(8,128)S(1)}, u32[]{:S(2)}, u32[]{:S(2)}) collective-permute-start(f32[88,128]{1,0:T(8,128)S(1)} %get-tuple-element.25), channel_id=1, source_target_pairs={{0,1},{1,2},{2,3},{3,4},{4,5},{5,6},{6,7},{7,0},{8,9},{9,10},{10,1... | collective-permute-start | bytes 135176 | tf_op jit(solution)/shard_map/ppermute | solution.py:490
  21.5 7.2 %collective-permute-start.1 = (f32[88,128]{1,0:T(8,128)S(1)}, f32[88,128]{1,0:T(8,128)S(1)}, u32[]{:S(2)}, u32[]{:S(2)}) collective-permute-start(f32[88,128]{1,0:T(8,128)S(1)} %get-tuple-element.22.mine_ref), channel_id=1, source_target_pairs={{0,7},{1,0},{2,1},{3,2},{4,3},{5,4},{6,5},{7,6},{8,15},{9,8},{10,9... | collective-permute-start | bytes 135176 | tf_op jit(solution)/shard_map/ppermute | solution.py:491
  30.1 25.2 %all-to-all-start = ((f32[1088,1,128]{2,1,0:T(1,128)}), f32[1088,1,128]{2,1,0:T(1,128)S(1)}, u32[]{:S(2)}, u32[]{:S(2)}) async-start(f32[1088,1,128]{2,1,0:T(1,128)} %bitcast.5), calls=%async_computation | async-start | bytes 1114112 | tf_op jit(solution)/shard_map/all_to_all | solution.py:502
  39.3 13.8 %collective-permute-start.3 = (f32[64,128]{1,0:T(8,128)S(1)}, f32[64,128]{1,0:T(8,128)S(1)}, u32[]{:S(2)}, u32[]{:S(2)}) collective-permute-start(f32[64,128]{1,0:T(8,128)S(1)} %get-tuple-element.27), channel_id=1, source_target_pairs={{0,8},{8,16},{16,24},{24,32},{32,40},{40,48},{48,56},{56,64},{64,7... | collective-permute-start | bytes 98312 | tf_op jit(solution)/shard_map/ppermute | solution.py:513
